TPU v7x, 32 devices: a whole 2x2x4 slice. The times are simulated.
32 devices in a mesh: height: 4 (over x, core), dom: 8 (over z, y).
Axes of the slice: x: 2, y: 2, z: 4, core: 2. Of those that a mesh axis runs over, the one named last changes fastest.
Arguments:
- modes_now: float32 [64, 64, 4096], P('height', 'dom'), may hold values from -6 to 6
- modes_prev: float32 [64, 64, 4096], P('height', 'dom'), may hold values from -6 to 6
- partition_boxes: int32 [64, 2], P('dom'), may hold values from 16 to 64, as said below
- face_table: int32 [256, 8], P('dom'), may hold values from 0 to 64, as said below
Outputs:
- new_modes: float32 [64, 64, 4096], P('height', 'dom')
- pressure: float32 [64, 64, 4096], P('height', 'dom')
Inputs may be any that keep to these rules, and one draw needn't show every extreme that they name: `partition_boxes`: column 0 is a partition's extent along x, column 1 along y. `face_table`: row r belongs to dom index r // 32. Columns: 0 the local number of the source partition on that index, 1 its side (0 low x, 1 high x, 2 low y, 3 high y), 2 the first cell of the face along that side, 3 the face's length in cells (0 marks an unused row), 4 the dom index holding the target partition, 5 the target's local number, 6 its side, 7 the first cell along it. Sides 0 and 1 run along y, sides 2 and 3 along x; start plus length never passes either side's extent. Among the rows of one dom index at most 4 name the same dom index in column 4, and that many is reached in every draw.
All inputs are finite; a program needn't handle non-finite values.
Results may differ from a plain program's by a relative error of at most 0.0002.
Values sent between devices are 32-bit elements; how exact they have to be, the bound alone decides.
A program may use at most 64 MiB of HBM per device.

v0:
```python
import jax
import jax.numpy as jnp
from jax import lax
from jax.experimental import pallas as pl
from jax.experimental.pallas import tpu as pltpu
from jax.sharding import PartitionSpec as P

B = 64


COUPLING = 32.0
STENCIL = (COUPLING * 270.0 / 180.0, COUPLING * -27.0 / 180.0, COUPLING * 2.0 / 180.0)
TIME_STEP = 0.4
SERIES = (1.0, -1.0 / 6, 1.0 / 120, -1.0 / 5040, 1.0 / 362880, -1.0 / 39916800, 1.0 / 6227020800)


def cosine_table(lengths, box_side):
    lengths = lengths.astype(jnp.float32)[..., None, None]
    ordinal = jnp.arange(box_side, dtype=jnp.float32)
    waves = ordinal[:, None]
    places = ordinal[None, :]
    scales = jnp.sqrt(jnp.where(waves == 0, 1.0, 2.0) / lengths)
    values = scales * jnp.cos(jnp.pi * waves * (places + 0.5) / lengths)
    inside = (waves < lengths) & (places < lengths)
    return jnp.where(inside, values, 0.0)


def to_modes(table_rows, table_cols, grid_field, box_side):
    planes, holders, cells = grid_field.shape
    squares = grid_field.reshape(planes, holders, box_side, box_side)
    halfway = jnp.einsum("pka,zpab->zpkb", table_rows, squares, precision=lax.Precision.HIGH)
    complete = jnp.einsum("zpkb,plb->zpkl", halfway, table_cols, precision=lax.Precision.HIGH)
    return complete.reshape(planes, holders, cells)


def mix_kernel(m_ref, x_ref, o_ref):
    for p in range(x_ref.shape[1]):
        x = x_ref[:, p, :]
        xh = x.astype(jnp.bfloat16)
        xl = (x - xh.astype(jnp.float32)).astype(jnp.bfloat16)
        o_ref[:, p, :] = jnp.dot(
            m_ref[...], jnp.concatenate([xh, xl, xh], 0), preferred_element_type=jnp.float32
        )


def depth_mix(grid_field, matrix):
    shares, planes, holders, width = grid_field.shape
    total = shares * planes
    pieces = lax.all_to_all(grid_field, "height", split_axis=0, concat_axis=0, tiled=True)
    mh, ml = split(matrix)
    step = min(width, 512)
    combined = pl.pallas_call(
        mix_kernel,
        grid=(width // step,),
        in_specs=[
            pl.BlockSpec((total, 3 * total), lambda i: (0, 0)),
            pl.BlockSpec((total, holders, step), lambda i: (0, 0, i)),
        ],
        out_specs=pl.BlockSpec((total, holders, step), lambda i: (0, 0, i)),
        out_shape=jax.ShapeDtypeStruct((total, holders, width), jnp.float32),
        name="depth",
        cost_estimate=pl.CostEstimate(
            flops=2 * total * total * holders * width,
            bytes_accessed=8 * total * holders * width,
            transcendentals=0,
        ),
    )(jnp.concatenate([mh, mh, ml], 1), pieces.reshape(total, holders, width))
    received = lax.all_to_all(
        combined.reshape(grid_field.shape), "height", split_axis=0, concat_axis=0, tiled=True
    )
    return received.transpose(1, 2, 0, 3).reshape(planes, holders, shares * width)


def split(values):
    high = lax.reduce_precision(values, 8, 7)
    return high.astype(jnp.bfloat16), (values - high).astype(jnp.bfloat16)


GROUP = 4


def cells_kernel(x_ref, w_ref, c_ref, q_ref, sr_ref, sc_ref):
    group, holders, cells = x_ref.shape
    half = B // 2
    low = lax.broadcasted_iota(jnp.int32, (half, 2 * B), 1) < B
    planes = [x_ref[z].reshape(holders, half, 2 * B) for z in range(group)]
    outs = [[] for _ in range(group)]
    for p in range(holders):
        cols = []
        for k in range(group // 2):
            one, two = planes[2 * k][p], planes[2 * k + 1][p]
            top = jnp.where(low, one, pltpu.roll(two, B, 1))
            bottom = jnp.where(low, pltpu.roll(one, B, 1), two)
            cols.append(jnp.concatenate([top, bottom], 0))
        u = jnp.concatenate(cols, 1)
        uh = u.astype(jnp.bfloat16)
        ul = (u - uh.astype(jnp.float32)).astype(jnp.bfloat16)
        v = jnp.dot(
            w_ref[p], jnp.concatenate([uh, ul, uh], 0), preferred_element_type=jnp.float32
        )
        v = jnp.concatenate([v[:, 2 * B * k : 2 * B * (k + 1)] for k in range(group // 2)], 0)
        vh = v.astype(jnp.bfloat16)
        vl = (v - vh.astype(jnp.float32)).astype(jnp.bfloat16)
        q = jnp.dot(
            jnp.concatenate([vh, vl, vh], 1), c_ref[p], preferred_element_type=jnp.float32
        )
        rows = B + 16
        for k in range(group // 2):
            top = q[rows * k : rows * k + half, : 2 * B]
            bottom = q[rows * k + half : rows * k + B, : 2 * B]
            outs[2 * k].append(jnp.where(low, top, pltpu.roll(bottom, B, 1)))
            outs[2 * k + 1].append(jnp.where(low, pltpu.roll(top, B, 1), bottom))
            sr_ref[k, p] = q[rows * k + B : rows * k + B + 8, : 2 * B]
            sc_ref[k, p] = jnp.transpose(q[rows * k : rows * k + B, 2 * B :])[:16]
    for z in range(group):
        plane = jnp.stack(outs[z], 0).reshape(holders, cells)
        width = q_ref.shape[-1]
        for h in range(q_ref.shape[0]):
            q_ref[h, z] = plane[:, h * width : (h + 1) * width]


def cells_and_sides(modes, table_rows, table_cols, select_rows, select_cols):
    planes, holders, cells = modes.shape
    order = jnp.concatenate([jnp.arange(0, B, 2), jnp.arange(1, B, 2)])
    exact = lax.Precision.HIGHEST
    pick_r = jnp.pad(select_rows.reshape(holders, 6, B), ((0, 0), (0, 10), (0, 0)))
    pick_c = jnp.pad(select_cols.reshape(holders, 6, B), ((0, 0), (0, 2), (0, 0)))
    side_r = jnp.einsum("psx,pkx->psk", pick_r, table_rows, precision=exact)
    side_c = jnp.einsum("psy,pky->pks", pick_c, table_cols, precision=exact)
    weights = jnp.concatenate([table_rows.swapaxes(1, 2)[:, order], side_r], 1)[:, :, order]
    wh, wl = split(weights)
    weights = jnp.concatenate([wh, wh, wl], 2)
    blank = jnp.zeros_like(table_cols)
    none = jnp.zeros_like(side_c)
    tail = jnp.zeros((holders, B, 2 * B - 16), jnp.float32)
    upper = jnp.concatenate([table_cols, blank, side_c, none, tail], 2)
    lower = jnp.concatenate([blank, table_cols, none, side_c, tail], 2)
    ch, cl = split(jnp.concatenate([upper, lower], 1))
    columns = jnp.concatenate([ch, ch, cl], 1)
    pairs = planes // 2
    shares = lax.axis_size("height")
    whole = lambda shape: pl.BlockSpec(shape, lambda i: (0,) * len(shape))
    q, sr, sc = pl.pallas_call(
        cells_kernel,
        grid=(planes // GROUP,),
        in_specs=[
            pl.BlockSpec((GROUP, holders, cells), lambda i: (i, 0, 0)),
            whole(weights.shape),
            whole(columns.shape),
        ],
        out_specs=[
            pl.BlockSpec((shares, GROUP, holders, cells // shares), lambda i: (0, i, 0, 0)),
            pl.BlockSpec((GROUP // 2, holders, 8, 2 * B), lambda i: (i, 0, 0, 0)),
            pl.BlockSpec((GROUP // 2, holders, 16, B), lambda i: (i, 0, 0, 0)),
        ],
        out_shape=[
            jax.ShapeDtypeStruct((shares, planes, holders, cells // shares), jnp.float32),
            jax.ShapeDtypeStruct((pairs, holders, 8, 2 * B), jnp.float32),
            jax.ShapeDtypeStruct((pairs, holders, 16, B), jnp.float32),
        ],
        name="cells",
        cost_estimate=pl.CostEstimate(
            flops=4 * planes * holders * B**3, bytes_accessed=8 * planes * holders * cells, transcendentals=0
        ),
    )(modes, weights, columns)
    sr = sr.reshape(pairs, holders, 8, 2, B)[:, :, :6].transpose(0, 3, 1, 2, 4)
    sc = sc.reshape(pairs, holders, 2, 8, 2, B // 2)[:, :, :, :6].transpose(0, 2, 1, 3, 5, 4)
    sides = jnp.concatenate(
        [sr.reshape(planes, holders, 2, 3 * B), sc.reshape(planes, holders, 2, 3 * B)], 2
    )
    return q, sides.reshape(planes, holders * 4, 3 * B)


def side_selectors(extent_rows, extent_cols, box_side):
    holders = extent_rows.shape[0]
    layers = jnp.arange(3, dtype=jnp.int32)[None, :, None]
    place = jnp.arange(box_side, dtype=jnp.int32)[None, None, :]
    lowest = jnp.broadcast_to(place == layers, (holders, 3, box_side))
    high_rows = place == extent_rows[:, None, None] - 1 - layers
    high_cols = place == extent_cols[:, None, None] - 1 - layers
    select_rows = jnp.stack([lowest, high_rows], 1).astype(jnp.float32)
    select_cols = jnp.stack([lowest, high_cols], 1).astype(jnp.float32)
    return (select_rows, select_cols)


def shifter(offsets, amounts, box_side):
    spot = jnp.arange(box_side, dtype=jnp.int32)[None, :, None]
    cellpos = jnp.arange(box_side, dtype=jnp.int32)[None, None, :]
    hits = (cellpos == offsets[:, None, None] + spot) & (spot < amounts[:, None, None])
    return hits.astype(jnp.float32)


def pick_rows(row_ids, count):
    return (row_ids[:, None] == jnp.arange(count, dtype=jnp.int32)[None, :]).astype(jnp.float32)


def select_faces(stacked, row_ids, offsets, amounts, box_side):
    planes, count, width = stacked.shape
    picked = jnp.einsum(
        "rk,zkm->zrm", pick_rows(row_ids, count), stacked, precision=lax.Precision.HIGH
    )
    picked = picked.reshape(planes, row_ids.shape[0], 3, box_side)
    return jnp.einsum(
        "rqc,zrjc->zrjq",
        shifter(offsets, amounts, box_side),
        picked,
        precision=lax.Precision.HIGH,
    )


def face_forcing(
    local_sides, aligned, targets, facing, offsets, amounts, select_rows, select_cols, box_side
):
    planes, count, width = local_sides.shape
    holders = count // 4
    number = targets.shape[0]
    target_ids = targets * 4 + facing
    inside_rim = select_faces(local_sides, target_ids, offsets, amounts, box_side)
    jumps = aligned - inside_rim
    nearest = jumps[:, :, 0]
    second = jumps[:, :, 1]
    farthest = jumps[:, :, 2]
    closest = STENCIL[0] * nearest + STENCIL[1] * second + STENCIL[2] * farthest
    middle = STENCIL[1] * nearest + STENCIL[2] * second
    outer = STENCIL[2] * nearest
    pushes = jnp.stack([closest, middle, outer], 2)
    placed = jnp.einsum(
        "rqc,zrjq->zrjc",
        shifter(offsets, amounts, box_side),
        pushes,
        precision=lax.Precision.HIGH,
    )
    placed = placed.reshape(planes, number, 3 * box_side)
    side_force = jnp.einsum(
        "rk,zrm->zkm", pick_rows(target_ids, count), placed, precision=lax.Precision.HIGH
    )
    side_force = side_force.reshape(planes, holders, 4, 3, box_side)
    from_cols = jnp.einsum(
        "psjx,zpsjy->zpxy", select_rows, side_force[:, :, 0:2], precision=lax.Precision.HIGH
    )
    from_rows = jnp.einsum(
        "psjy,zpsjx->zpxy", select_cols, side_force[:, :, 2:4], precision=lax.Precision.HIGH
    )
    return (from_cols + from_rows).reshape(planes, holders, box_side * box_side)


def interfaces(local_sides, face_table, select_rows, select_cols):
    planes = local_sides.shape[0]
    listed = face_table.shape[0]
    dom_count = lax.axis_size("dom")
    pair_most = max(2, listed // dom_count)
    source_ids = face_table[:, 0] * 4 + face_table[:, 1]
    rim_values = select_faces(
        local_sides, source_ids, face_table[:, 2], face_table[:, 3], B
    ).reshape(planes, listed, 3 * B)
    targets = face_table[:, 4]
    matches = (targets[:, None] == jnp.arange(dom_count, dtype=jnp.int32)[None, :]).astype(
        jnp.int32
    )
    position_in = jnp.sum(jnp.cumsum(matches, 0) * matches, 1) - 1
    slot_ids = targets * pair_most + position_in
    slot_hits = (
        jnp.arange(dom_count * pair_most, dtype=jnp.int32)[:, None] == slot_ids[None, :]
    ).astype(jnp.int32)
    outgoing = jnp.einsum(
        "sr,zrm->zsm", slot_hits.astype(jnp.float32), rim_values, precision=lax.Precision.HIGH
    )
    labels = jnp.stack([face_table[:, 5], face_table[:, 6], face_table[:, 7], face_table[:, 3]], 1)
    label_slots = jnp.sum(slot_hits[:, :, None] * labels[None, :, :], 1)[None]
    label_plane = jnp.pad(label_slots.astype(jnp.float32), ((0, 0), (0, 0), (0, 3 * B - 4)))
    received = lax.all_to_all(
        jnp.concatenate([outgoing, label_plane], 0), "dom", split_axis=1, concat_axis=1, tiled=True
    )
    arrived = received[planes, :, :4].astype(jnp.int32)
    aligned = received[:planes].reshape(planes, dom_count * pair_most, 3, B)
    targets_here = arrived[:, 0]
    facing = arrived[:, 1]
    offsets = arrived[:, 2]
    lengths = arrived[:, 3]
    return face_forcing(
        local_sides, aligned, targets_here, facing, offsets, lengths, select_rows, select_cols, B
    )


def advance(
    modes_now,
    modes_prev,
    force_modes,
    extent_rows,
    extent_cols,
    first_plane,
    total_planes,
    box_side,
):
    planes, holders, cells = modes_now.shape
    wave_depth = (first_plane + jnp.arange(planes, dtype=jnp.int32)).astype(
        jnp.float32
    ) / total_planes
    wave_side = jnp.arange(box_side, dtype=jnp.float32)
    float_rows = extent_rows.astype(jnp.float32)
    float_cols = extent_cols.astype(jnp.float32)
    ratio_rows = wave_side[None, :] / float_rows[:, None]
    ratio_cols = wave_side[None, :] / float_cols[:, None]
    quarter = (jnp.pi * TIME_STEP / 2) ** 2 * (
        wave_depth[:, None, None, None] ** 2
        + ratio_rows[None, :, :, None] ** 2
        + ratio_cols[None, :, None, :] ** 2
    )
    ratio = jnp.float32(SERIES[-1])
    for coefficient in SERIES[-2::-1]:
        ratio = ratio * quarter + coefficient
    ratio = ratio * ratio
    growth = TIME_STEP * TIME_STEP * ratio
    inside = (wave_side[None, :, None] < float_rows[:, None, None]) & (
        wave_side[None, None, :] < float_cols[:, None, None]
    )
    grid_shape = (planes, holders, box_side, box_side)
    updated = (
        (2.0 - 4.0 * quarter * ratio) * modes_now.reshape(grid_shape)
        - modes_prev.reshape(grid_shape)
        + growth * force_modes.reshape(grid_shape)
    )
    return jnp.where(inside[None], updated, 0.0).reshape(planes, holders, cells)


def on_device(modes_now, modes_prev, partition_boxes, face_table):
    planes = modes_now.shape[0]
    total_planes = planes * lax.axis_size("height")
    extent_rows = partition_boxes[:, 0]
    extent_cols = partition_boxes[:, 1]
    table_rows = cosine_table(extent_rows, B)
    table_cols = cosine_table(extent_cols, B)
    table_depth = cosine_table(jnp.full((), total_planes, jnp.int32), total_planes)
    select_rows, select_cols = side_selectors(extent_rows, extent_cols, B)
    layers, local_sides = cells_and_sides(
        modes_now, table_rows, table_cols, select_rows, select_cols
    )
    pressure = depth_mix(layers, table_depth.T)
    forcing = interfaces(local_sides, face_table, select_rows, select_cols)
    force_modes = to_modes(table_rows, table_cols, forcing, B)
    first_plane = lax.axis_index("height") * planes
    new_modes = advance(
        modes_now, modes_prev, force_modes, extent_rows, extent_cols, first_plane, total_planes, B
    )
    return (new_modes, pressure)


def solution(mesh):
    placed = (P("height", "dom", None), P("height", "dom", None), P("dom", None), P("dom", None))
    return jax.shard_map(
        on_device,
        mesh=mesh,
        in_specs=placed,
        out_specs=(P("height", "dom", None), P("height", "dom", None)),
        check_vma=False,
    )
```

profile of v0, /device:TPU:0, one launch (start us, length us, event | category | flops | bytes accessed | tf_op | source)
XLA Modules:
  0.0 141.7 jit_solution(17698982495802780989)
XLA Ops:
  6.8 1.8 %and_select_fusion.1 = (f32[8,64,64]{2,1,0:T(8,128)S(1)}, f32[8,64,64]{2,1,0:T(8,128)S(1)}) fusion(f32[8]{0:T(128)S(1)} %get-tuple-element.34, f32[64,64]{1,0:T(8,128)S(1)} %get-tuple-element.29, f32[8,64]{1,0:T(8,128)S(1)} %get-tuple-element.36, pred[8,64]{1,0:T(8,128)(4,1)S(1)} %iota_compare_fusion.12, f32[8]{0:T(128)S(1)} %get-tuple-element.33, ...), kind=kLoop, calls=%fused_computation.72 | loop fusion | flops 262144 | bytes 300096 | tf_op jit(solution)/shard_map/jit(_where)/select_n | solution.py:25
  16.5 8.2 %cells.1 = (f32[4,16,8,1024]{3,2,1,0:T(8,128)}, f32[8,8,8,128]{3,2,1,0:T(8,128)}, f32[8,8,16,64]{3,2,1,0:T(8,128)}) custom-call(f32[16,8,4096]{2,1,0:T(8,128)} %x_ref.1, bf16[8,80,192]{2,1,0:T(8,128)(2,1)} %pad_maximum_fusion.4.w_ref, bf16[8,384,256]{2,1,0:T(8,128)(2,1)} %pad_maximum_fusion.c_ref), custom_call_target="tpu_custom_call" | custom-call | flops 134217728 | bytes 4194304 | tf_op jit(solution)/shard_map/cells/pallas_call | solution.py:143
  26.4 1.7 %reshape.636 = f32[8,8,2,8,2,32]{5,4,3,2,1,0:T(2,128)S(1)} reshape(f32[8,8,16,64]{3,2,1,0:T(8,128)} %get-tuple-element.6) | data formatting | bytes 524288 | tf_op jit(solution)/shard_map/reshape | solution.py:167
  29.1 3.9 %copy.155 = f32[8,8,2,6,2,32]{1,4,5,3,2,0:T(2,128)S(1)} copy(f32[8,8,2,6,2,32]{5,4,3,2,1,0:T(2,128)} %slice.105) | data formatting | bytes 393216
  32.9 2.0 %copy.122 = f32[16,8,2,192]{3,2,1,0:T(2,128)} copy(f32[16,8,2,192]{1,3,2,0:T(8,128)S(1)} %bitcast.142) | data formatting | bytes 393216 | tf_op jit(solution)/shard_map/reshape | solution.py:169
  40.1 1.7 %reshape.640 = f32[16,32,192]{2,1,0:T(8,128)S(1)} reshape(f32[16,32,3,64]{3,2,1,0:T(4,128)} %copy.124) | data formatting | bytes 786432 | tf_op jit(solution)/shard_map/reshape | solution.py:255
  43.5 7.4 %all-to-all-start = ((f32[17,32,192]{2,0,1:T(8,128)}), f32[17,32,192]{2,0,1:T(8,128)S(1)}, u32[]{:S(2)}, u32[]{:S(2)}) async-start(f32[17,32,192]{2,0,1:T(8,128)} %copy.126), calls=%async_computation | async-start | bytes 1572864 | tf_op jit(solution)/shard_map/all_to_all | solution.py:271
  50.9 3.1 %reshape.632 = f32[16,8,64,64]{3,2,1,0:T(8,128)} reshape(f32[16,8,4096]{2,1,0:T(8,128)S(1)} %copy-done) | data formatting | bytes 4194304 | tf_op jit(solution)/shard_map/reshape | solution.py:319
  54.3 4.7 %reshape.633 = f32[16,8,64,64]{3,2,1,0:T(8,128)} reshape(f32[16,8,4096]{2,1,0:T(8,128)} %param.5) | data formatting | bytes 4194304 | tf_op jit(solution)/shard_map/reshape | solution.py:320
  59.0 5.3 %copy.109 = f32[16,8,64,64]{2,3,0,1:T(8,128)} copy(f32[16,8,64,64]{3,2,1,0:T(8,128)} %reshape.633) | data formatting | bytes 4194304 | tf_op jit(solution)/shard_map/reshape | solution.py:320
  64.3 5.5 %copy.108 = f32[16,8,64,64]{2,3,0,1:T(8,128)} copy(f32[16,8,64,64]{3,2,1,0:T(8,128)} %reshape.632) | data formatting | bytes 4194304 | tf_op jit(solution)/shard_map/reshape | solution.py:319
  71.2 3.8 %all-to-all-start.1 = ((f32[4,16,8,1024]{3,2,1,0:T(8,128)}), f32[4,16,8,1024]{3,2,1,0:T(8,128)S(1)}, u32[]{:S(2)}, u32[]{:S(2)}) async-start(f32[4,16,8,1024]{3,2,1,0:T(8,128)} %get-tuple-element.7), calls=%async_computation.1 | async-start | bytes 4194304 | tf_op jit(solution)/shard_map/all_to_all | solution.py:49
  78.1 2.0 %slice.106 = f32[16,32,192]{2,0,1:T(8,128)} slice(f32[17,32,192]{2,0,1:T(8,128)} %copy-done.4), slice={[0:16], [0:32], [0:192]} | slice | bytes 786432 | tf_op jit(solution)/shard_map/slice | solution.py:275
  80.0 2.3 %reshape.677 = f32[16,32,3,64]{3,2,0,1:T(4,128)} reshape(f32[16,32,192]{2,0,1:T(8,128)} %slice.106) | data formatting | bytes 786432 | tf_op jit(solution)/shard_map/reshape | solution.py:275
  82.3 2.3 %fusion.24 = f32[16,32,3,64]{3,0,2,1:T(8,128)S(1)} fusion(f32[16,32,3,64]{3,2,0,1:T(4,128)} %reshape.677, f32[16,32,3,64]{3,2,1,0:T(4,128)S(1)} %reshape.642, s32[32,64]{1,0:T(8,128)S(1)} %iota_add_fusion, pred[32,64]{1,0:T(8,128)(4,1)S(1)} %iota_compare_fusion.3), kind=kOutput, calls=%fused_computation.35 | convolution fusion | flops 38109184 | bytes 1189888 | tf_op jit(solution)/shard_map/rqc,zrjc->zrjq/dot_general | solution.py:203
  88.0 2.2 %convolution_bitcast_fusion.3 = f32[16,32,192]{2,1,0:T(8,128)} fusion(f32[16,32,192]{2,1,0:T(8,128)} %reshape.643, s32[32]{0:T(128)S(1)} %get-tuple-element.28), kind=kOutput, calls=%fused_computation.36 | convolution fusion | flops 18875392 | bytes 786560 | tf_op jit(solution)/shard_map/rk,zrm->zkm/dot_general | solution.py:234
  92.0 4.3 %fusion.42 = f32[8,16,64,64,1]{3,2,4,1,0:T(8,128)} fusion(f32[16,8,2,3,64]{4,3,2,1,0:T(4,128)S(1)} %get-tuple-element.8, pred[8,1,3,64]{3,2,1,0:T(4,128)(4,1)S(1)} %stack_broadcast_in_dim.4, pred[8,1,3,64]{3,2,1,0:T(4,128)(4,1)S(1)} %iota_compare_fusion.10), kind=kOutput, calls=%fused_computation.60 | convolution fusion | flops 18877440 | bytes 2296832 | tf_op jit(solution)/shard_map/psjx,zpsjy->zpxy/dot_general | solution.py:238
  96.3 3.3 %fusion.40 = f32[8,16,64,64,1]{2,3,4,1,0:T(8,128)} fusion(f32[16,8,2,3,64]{4,3,2,1,0:T(4,128)S(1)} %get-tuple-element.9, pred[8,1,3,64]{3,2,1,0:T(4,128)(4,1)S(1)} %stack_broadcast_in_dim.4, pred[8,1,3,64]{3,2,1,0:T(4,128)(4,1)S(1)} %iota_compare_fusion.9), kind=kOutput, calls=%fused_computation.58 | convolution fusion | flops 18877440 | bytes 2296832 | tf_op jit(solution)/shard_map/psjy,zpsjx->zpxy/dot_general | solution.py:241
  101.8 9.2 %depth.1 = f32[64,8,1024]{2,1,0:T(8,128)} custom-call(bf16[64,192]{1,0:T(8,128)(2,1)} %pad_maximum_fusion.5.m_ref, f32[64,8,1024]{2,1,0:T(8,128)} %bitcast.143), custom_call_target="tpu_custom_call" | custom-call | flops 67108864 | bytes 4194304 | tf_op jit(solution)/shard_map/depth/pallas_call | solution.py:52
  111.0 3.9 %all-to-all-start.2 = ((f32[4,16,8,1024]{3,2,1,0:T(8,128)}), f32[4,16,8,1024]{3,2,1,0:T(8,128)S(1)}, u32[]{:S(2)}, u32[]{:S(2)}) async-start(f32[4,16,8,1024]{3,2,1,0:T(8,128)} %bitcast.145), calls=%async_computation.2 | async-start | bytes 4194304 | tf_op jit(solution)/shard_map/all_to_all | solution.py:68
  114.9 5.5 %fusion.18 = f32[8,16,64,64]{3,2,1,0:T(8,128)S(1)} fusion(f32[8,16,64,64,1]{2,3,4,1,0:T(8,128)} %fusion.40, f32[8,16,64,64,1]{3,2,4,1,0:T(8,128)} %fusion.42, f32[8,64]{1,0:T(8,128)S(1)} %get-tuple-element.36, f32[8]{0:T(128)S(1)} %copy-done.16, f32[64,64]{1,0:T(8,128)S(1)} %get-tuple-element.30, pred[8,64]{1,0:T(8,128)(4,1)S(1)} %copy-done.8), kind=kOutput, calls=%fused_computation.24 | convolution fusion | flops 201981952 | bytes 6310432 | tf_op jit(solution)/shard_map/pka,zpab->zpkb/dot_general | solution.py:31
  120.8 7.7 %fusion.16 = f32[16,8,64,64]{2,3,0,1:T(8,128)} fusion(f32[16,8,64,64]{2,3,0,1:T(8,128)S(1)} %copy-done.2, f32[16,8,64,64]{2,3,0,1:T(8,128)S(1)} %copy-done.3, f32[8,16,64,64]{3,2,1,0:T(8,128)S(1)} %fusion.18, f32[8,64]{1,0:T(8,128)S(1)} %copy-done.19, f32[16,8,64]{2,0,1:T(8,128)S(1)} %copy-done.5, pred[8,64,64]{1,2,0:T(8,128)(4,1)S(1)} %copy.107, ...), kind=kOutput, calls=%fused_computation.21 | convolution fusion | flops 214040576 | bytes 8475168 | tf_op jit(solution)/shard_map/zpkb,plb->zpkl/dot_general | solution.py:32
  128.5 5.4 %copy.137 = f32[16,8,64,64]{3,2,1,0:T(8,128)} copy(f32[16,8,64,64]{2,3,0,1:T(8,128)} %fusion.16) | data formatting | bytes 4194304 | tf_op jit(solution)/shard_map/jit(_where)/select_n | solution.py:323
  133.9 4.8 %reshape.645 = f32[16,8,4096]{2,1,0:T(8,128)} reshape(f32[16,8,64,64]{3,2,1,0:T(8,128)} %copy.137) | data formatting | bytes 4194304 | tf_op jit(solution)/shard_map/reshape | solution.py:323
  (133 shorter events, 38.5 us)
Async XLA Ops:
  3.6 5.9 %copy-start.17 = (f32[8]{0:T(128)}, f32[8]{0:T(128)S(1)}, u32[]{:S(2)}) copy-start(f32[8]{0:T(128)S(1)} %get-tuple-element.33) | copy-start | bytes 100
  3.6 8.8 %copy-start.15 = (f32[8]{0:T(128)}, f32[8]{0:T(128)S(1)}, u32[]{:S(2)}) copy-start(f32[8]{0:T(128)S(1)} %get-tuple-element.34) | copy-start | bytes 100
  3.7 5.9 %copy-start.12 = (pred[8,64]{1,0:T(8,128)(4,1)}, pred[8,64]{1,0:T(8,128)(4,1)S(1)}, u32[]{:S(2)}) copy-start(pred[8,64]{1,0:T(8,128)(4,1)S(1)} %iota_compare_fusion.11) | copy-start | bytes 1540
  3.8 50.2 %copy-start.7 = (pred[8,64]{1,0:T(8,128)(4,1)}, pred[8,64]{1,0:T(8,128)(4,1)S(1)}, u32[]{:S(2)}) copy-start(pred[8,64]{1,0:T(8,128)(4,1)S(1)} %iota_compare_fusion.12) | copy-start | bytes 1540
  4.7 7.8 %copy-start.9 = (f32[8,64]{1,0:T(8,128)}, f32[8,64]{1,0:T(8,128)S(1)}, u32[]{:S(2)}) copy-start(f32[8,64]{1,0:T(8,128)S(1)} %get-tuple-element.37) | copy-start | bytes 6148
  29.1 7.3 %copy-start.20 = (s32[32]{0:T(128)S(1)}, s32[32]{0:T(128)}, u32[]{:S(2)}) copy-start(s32[32]{0:T(128)} %get-tuple-element.19) | copy-start | bytes 388
  38.7 12.2 %copy-start = (f32[16,8,4096]{2,1,0:T(8,128)S(1)}, f32[16,8,4096]{2,1,0:T(8,128)}, u32[]{:S(2)}) copy-start(f32[16,8,4096]{2,1,0:T(8,128)} %x_ref.1) | copy-start | bytes 6291460
  43.4 10.5 %copy-start.13 = (pred[8,64]{1,0:T(8,128)(4,1)S(1)}, pred[8,64]{1,0:T(8,128)(4,1)}, u32[]{:S(2)}) copy-start(pred[8,64]{1,0:T(8,128)(4,1)} %copy-done.12) | copy-start | bytes 1540
  43.5 27.8 %all-to-all-start = ((f32[17,32,192]{2,0,1:T(8,128)}), f32[17,32,192]{2,0,1:T(8,128)S(1)}, u32[]{:S(2)}, u32[]{:S(2)}) async-start(f32[17,32,192]{2,0,1:T(8,128)} %copy.126), calls=%async_computation | async-start | bytes 1572864 | tf_op jit(solution)/shard_map/all_to_all | solution.py:271
  64.3 5.5 %copy-start.6 = (bf16[64,64]{1,0:T(8,128)(2,1)S(1)}, bf16[64,64]{1,0:T(8,128)(2,1)}, u32[]{:S(2)}) copy-start(bf16[64,64]{1,0:T(8,128)(2,1)} %get-tuple-element.25) | copy-start | bytes 24580
  64.3 6.2 %copy-start.11 = (f32[8,64]{1,0:T(8,128)S(1)}, f32[8,64]{1,0:T(8,128)}, u32[]{:S(2)}) copy-start(f32[8,64]{1,0:T(8,128)} %get-tuple-element.35) | copy-start | bytes 6148
  71.2 5.3 %copy-start.4 = (f32[17,32,192]{2,0,1:T(8,128)}, f32[17,32,192]{2,0,1:T(8,128)S(1)}, u32[]{:S(2)}) copy-start(f32[17,32,192]{2,0,1:T(8,128)S(1)} %all-to-all-done) | copy-start | bytes 1253380
  71.2 29.3 %all-to-all-start.1 = ((f32[4,16,8,1024]{3,2,1,0:T(8,128)}), f32[4,16,8,1024]{3,2,1,0:T(8,128)S(1)}, u32[]{:S(2)}, u32[]{:S(2)}) async-start(f32[4,16,8,1024]{3,2,1,0:T(8,128)} %get-tuple-element.7), calls=%async_computation.1 | async-start | bytes 4194304 | tf_op jit(solution)/shard_map/all_to_all | solution.py:49
  100.5 1.3 copy-start.1
  101.8 13.1 %copy-start.8 = (pred[8,64]{1,0:T(8,128)(4,1)S(1)}, pred[8,64]{1,0:T(8,128)(4,1)}, u32[]{:S(2)}) copy-start(pred[8,64]{1,0:T(8,128)(4,1)} %copy-done.7) | copy-start | bytes 1540
  101.8 13.1 %copy-start.16 = (f32[8]{0:T(128)S(1)}, f32[8]{0:T(128)}, u32[]{:S(2)}) copy-start(f32[8]{0:T(128)} %copy-done.15) | copy-start | bytes 100
  111.0 29.2 %all-to-all-start.2 = ((f32[4,16,8,1024]{3,2,1,0:T(8,128)}), f32[4,16,8,1024]{3,2,1,0:T(8,128)S(1)}, u32[]{:S(2)}, u32[]{:S(2)}) async-start(f32[4,16,8,1024]{3,2,1,0:T(8,128)} %bitcast.145), calls=%async_computation.2 | async-start | bytes 4194304 | tf_op jit(solution)/shard_map/all_to_all | solution.py:68
  114.9 5.6 %copy-start.2 = (f32[16,8,64,64]{2,3,0,1:T(8,128)S(1)}, f32[16,8,64,64]{2,3,0,1:T(8,128)}, u32[]{:S(2)}) copy-start(f32[16,8,64,64]{2,3,0,1:T(8,128)} %copy.109) | copy-start | bytes 6291460
  114.9 5.9 %copy-start.3 = (f32[16,8,64,64]{2,3,0,1:T(8,128)S(1)}, f32[16,8,64,64]{2,3,0,1:T(8,128)}, u32[]{:S(2)}) copy-start(f32[16,8,64,64]{2,3,0,1:T(8,128)} %copy.108) | copy-start | bytes 6291460
  114.9 5.9 %copy-start.5 = (f32[16,8,64]{2,0,1:T(8,128)S(1)}, f32[16,8,64]{2,0,1:T(8,128)}, u32[]{:S(2)}) copy-start(f32[16,8,64]{2,0,1:T(8,128)} %broadcast_add_fusion) | copy-start | bytes 98308
  114.9 5.9 %copy-start.10 = (f32[8,64]{1,0:T(8,128)S(1)}, f32[8,64]{1,0:T(8,128)}, u32[]{:S(2)}) copy-start(f32[8,64]{1,0:T(8,128)} %copy-done.9) | copy-start | bytes 6148
  114.9 5.9 %copy-start.14 = (pred[8,64]{1,0:T(8,128)(4,1)S(1)}, pred[8,64]{1,0:T(8,128)(4,1)}, u32[]{:S(2)}) copy-start(pred[8,64]{1,0:T(8,128)(4,1)} %copy-done.12) | copy-start | bytes 1540
  114.9 5.9 %copy-start.18 = (f32[8]{0:T(128)S(1)}, f32[8]{0:T(128)}, u32[]{:S(2)}) copy-start(f32[8]{0:T(128)} %copy-done.17) | copy-start | bytes 100
  114.9 5.9 %copy-start.19 = (f32[8,64]{1,0:T(8,128)S(1)}, f32[8,64]{1,0:T(8,128)}, u32[]{:S(2)}) copy-start(f32[8,64]{1,0:T(8,128)} %get-tuple-element.38) | copy-start | bytes 6148
where the time goes:
time: 143 us; the launch traced here: 142 us
  local copies, waits for them, and re-layouts  59.9 us (42%)
  matrix products  32.9 us (23%)
  Pallas kernels  17.4 us (12%)
  starting transfers between devices  15.1 us (11%)
  other arithmetic  12.9 us (9%)
  waiting for transfers between devices  2.37 us (2%)
    reshape x2, local copies, waits for them, and re-layouts, advance(): modes_prev.reshape(grid_shape)  10.1 us
    pallas_call x1, Pallas kernels, depth_mix(): pl.pallas_call(mix_kernel, grid=(width // step,), in_specs=[pl.BlockSpec(...  9.18 us
    reshape x2, local copies, waits for them, and re-layouts, advance(): modes_now.reshape(grid_shape)  8.53 us
    pallas_call x1, Pallas kernels, cells_and_sides(): pl.pallas_call(cells_kernel, grid=(planes // GROUP,), in_specs=[pl.BlockS...  8.19 us
    dot_general x1, matrix products, to_modes(): jnp.einsum('zpkb,plb->zpkl', halfway, table_cols, precision=lax.Precision...  7.66 us
    all_to_all x1, starting transfers between devices, interfaces(): lax.all_to_all(jnp.concatenate([outgoing, label_plane], 0), 'dom', split_...  7.44 us
    unnamed x45, local copies, waits for them, and re-layouts  5.78 us
    dot_general x1, matrix products, to_modes(): jnp.einsum('pka,zpab->zpkb', table_rows, squares, precision=lax.Precision...  5.48 us
  transfers between devices with their start and end apart: 3, of which 2 were waited for; matrix products, arithmetic and copies ran while one was open for 48% of the time, Pallas kernels for 0%

commit v1 on v0

v1 whole, which is shorter than its diff:
```python
import functools
import math

import jax
import jax.numpy as jnp
from jax import lax
from jax.experimental import pallas as pl
from jax.experimental.pallas import tpu as pltpu
from jax.sharding import PartitionSpec as P

COUPLING = 32.0
STENCIL = (COUPLING * 270.0 / 180.0, COUPLING * -27.0 / 180.0, COUPLING * 2.0 / 180.0)
TIME_STEP = 0.4
SERIES = (1.0, -1.0 / 6, 1.0 / 120, -1.0 / 5040, 1.0 / 362880, -1.0 / 39916800, 1.0 / 6227020800)
GROUP = 4
SIDES = 12


def iota(shape, axis):
    return lax.broadcasted_iota(jnp.int32, shape, axis)


def whole(shape):
    return pl.BlockSpec(shape, lambda *_: (0,) * len(shape))


def split(values):
    high = values.astype(jnp.bfloat16)
    return high, (values - high.astype(jnp.float32)).astype(jnp.bfloat16)


def halves(values):
    return jnp.concatenate(split(values), 0)


def dot(left, right):
    return jnp.dot(left, right, preferred_element_type=jnp.float32)


def thrice(values):
    high, low = split(values)
    return jnp.concatenate([high, low, high], 1)


def stacked(pair):
    size = pair.shape[0] // 2
    return jnp.concatenate([pair[:size], pair[:size], pair[size:]], 0)


def cosines(wave, place, length):
    span = jnp.full((1, wave.shape[1]), length, jnp.int32).astype(jnp.float32)
    inverse = 0.25 / span
    wave = wave.astype(jnp.float32)
    place = place.astype(jnp.float32)
    turns = wave * (2.0 * place + 1.0)
    rest = (turns - jnp.floor(turns * inverse + 0.5) * (4.0 * span)) * (inverse * math.pi)
    square = rest * rest
    sine = jnp.float32(1.0 / math.factorial(13))
    for order in (11, 9, 7, 5, 3, 1):
        sine = sine * square + (-1.0) ** (order // 2) / math.factorial(order)
    sine = sine * rest
    scale = jnp.where(wave == 0.0, jnp.sqrt(1.0 / span), jnp.sqrt(2.0 / span))
    return jnp.where((wave < span) & (place < span), (1.0 - 2.0 * sine * sine) * scale, 0.0)


def shuffle(index, side):
    half = side // 2
    return jnp.where(index < half, 2 * index, 2 * (index - half) + 1)


def layer_place(row, extent):
    return jnp.where(row < 3, row, jnp.where(row < 6, extent + 2 - row, extent))


def tables_kernel(boxes, w_ref, c_ref, ws_ref, cs_ref, ct_ref, rt_ref, sr_ref, sc_ref):
    side = w_ref.shape[1]
    spare = sr_ref.shape[1] // 6

    def paired(wave_of, place_of, length):
        shape = (2 * side, 2 * side)
        row, col = iota(shape, 0), iota(shape, 1)
        values = cosines(wave_of(row % side, col % side), place_of(row % side, col % side), length)
        return jnp.where(row // side == col // side, values, 0.0)

    def body(p, carry):
        rows, cols = boxes[p, 0], boxes[p, 1]
        shape = (side, side)
        row, col = iota(shape, 0), shuffle(iota(shape, 1), side)
        high, low = split(cosines(col, shuffle(row, side), rows))
        w_ref[p] = jnp.concatenate([high, high, low], 1)
        high, low = split(cosines(col, row, rows))
        ws_ref[p, :side] = jnp.concatenate([high, high, low], 1)
        shape = (16, side)
        row, col = iota(shape, 0), shuffle(iota(shape, 1), side)
        high, low = split(cosines(col, layer_place(row, rows), rows))
        ws_ref[p, side:] = jnp.concatenate([high, high, low], 1)
        straight = paired(lambda r, c: r, lambda r, c: c, cols)
        high, low = split(straight)
        c_ref[p] = jnp.concatenate([high, high, low], 0)
        cs_ref[p, :, : 2 * side] = jnp.concatenate([high, high, low], 0)
        shape = (2 * side, 2 * side)
        row, col = iota(shape, 0), iota(shape, 1)
        values = cosines(row % side, layer_place(col % 8, cols), cols)
        values = jnp.where((row // side == col // 8) & (col % 8 < 6), values, 0.0)
        high, low = split(values)
        cs_ref[p, :, 2 * side :] = jnp.concatenate([high, high, low], 0)
        ct_ref[p] = stacked(halves(paired(lambda r, c: c, lambda r, c: r, cols)))
        rt_ref[p] = stacked(halves(paired(lambda r, c: shuffle(c, side), lambda r, c: r, rows)))
        shape = (6 * spare, side)
        row, col = iota(shape, 0) // spare, iota(shape, 1)
        sr_ref[p] = cosines(shuffle(col, side), layer_place(row, rows), rows)
        shape = (6 * spare, 2 * side)
        row, col = iota(shape, 0) // spare, iota(shape, 1)
        sc_ref[p] = cosines(col % side, layer_place(row, cols), cols)
        return carry

    lax.fori_loop(0, w_ref.shape[0], body, 0)


def make_tables(boxes, side, spare):
    holders = boxes.shape[0]
    shapes = [
        ((holders, side, 3 * side), jnp.bfloat16),
        ((holders, 6 * side, 2 * side), jnp.bfloat16),
        ((holders, side + 16, 3 * side), jnp.bfloat16),
        ((holders, 6 * side, 4 * side), jnp.bfloat16),
        ((holders, 6 * side, 2 * side), jnp.bfloat16),
        ((holders, 6 * side, 2 * side), jnp.bfloat16),
        ((holders, 6 * spare, side), jnp.float32),
        ((holders, 6 * spare, 2 * side), jnp.float32),
    ]
    return pl.pallas_call(
        tables_kernel,
        grid_spec=pltpu.PrefetchScalarGridSpec(
            num_scalar_prefetch=1,
            grid=(1,),
            in_specs=[],
            out_specs=[whole(shape) for shape, _ in shapes],
        ),
        out_shape=[jax.ShapeDtypeStruct(*shape) for shape in shapes],
        name="tables",
        cost_estimate=pl.CostEstimate(flops=10**9, bytes_accessed=5 * 10**6, transcendentals=0),
    )(boxes)


def mix_kernel(total, chunks, spot, own_ref, other_ref, *refs):
    *out_refs, t_ref = refs
    planes, holders, step = own_ref.shape
    rows, cols = planes * holders * (len(out_refs) // chunks), 2 * planes * holders
    me = spot[0]
    masks = [m for m in range(total // planes) if m & 1 == m // (total // planes // 2)]

    @pl.when(pl.program_id(0) == 0)
    def _():
        for k, mask in enumerate(masks):
            shape = (planes * holders, cols)
            row, col = iota(shape, 0), iota(shape, 1)
            near = col < planes * holders
            mode = jnp.where(near, me * planes, (me ^ 1) * planes - planes) + col // holders
            place = (me ^ mask) * planes + row // holders
            values = jnp.where(row % holders == col % holders, cosines(mode, place, total), 0.0)
            t_ref[k * planes * holders : (k + 1) * planes * holders] = thrice(values)

    x = jnp.concatenate(
        [r[...].reshape(planes * holders, step) for r in (own_ref, other_ref)], 0
    )
    high, low = split(x)
    mixed = dot(t_ref[...], jnp.concatenate([high, high, low], 0))
    size = planes // chunks
    for k, out_ref in enumerate(out_refs):
        part = mixed[k * size * holders : (k + 1) * size * holders]
        out_ref[...] = part.reshape(size, holders, step)


def mix(spot, own, other, shares):
    planes, holders, cells = own.shape
    chunks = planes // GROUP
    count = max(1, shares // 2)
    step = min(512, cells)
    part = jax.ShapeDtypeStruct((GROUP, holders, cells), jnp.float32)
    block = lambda i, s: (0, 0, i)
    outs = pl.pallas_call(
        functools.partial(mix_kernel, shares * planes, chunks),
        grid_spec=pltpu.PrefetchScalarGridSpec(
            num_scalar_prefetch=1,
            grid=(cells // step,),
            in_specs=[pl.BlockSpec((planes, holders, step), block)] * 2,
            out_specs=[pl.BlockSpec((GROUP, holders, step), block)] * (count * chunks),
            scratch_shapes=[
                pltpu.VMEM((count * planes * holders, 6 * planes * holders), jnp.bfloat16)
            ],
        ),
        out_shape=[part] * (count * chunks),
        name="mix",
        cost_estimate=pl.CostEstimate(
            flops=3 * 10**9, bytes_accessed=16 * planes * holders * cells, transcendentals=0
        ),
    )(spot, own, other)
    return [list(outs[k * chunks : (k + 1) * chunks]) for k in range(count)]


def columns_of(planes, p, low, side):
    cols = []
    for k in range(len(planes) // 2):
        one, two = planes[2 * k][p], planes[2 * k + 1][p]
        top = jnp.where(low, one, pltpu.roll(two, side, 1))
        bottom = jnp.where(low, pltpu.roll(one, side, 1), two)
        cols.append(jnp.concatenate([top, bottom], 0))
    high, rest = split(jnp.concatenate(cols, 1))
    return jnp.concatenate([high, rest, high], 0)


def unpaired(top, bottom, low, side):
    one = jnp.where(low, top, pltpu.roll(bottom, side, 1))
    two = jnp.where(low, pltpu.roll(top, side, 1), bottom)
    return one, two


def sides_kernel(x_ref, w_ref, c_ref, s_ref):
    group, holders, cells = x_ref.shape
    side = math.isqrt(cells)
    half = side // 2
    wide = 2 * side
    low = iota((half, wide), 1) < side
    first = iota((side, wide), 1) < 8
    planes = [x_ref[z].reshape(holders, half, wide) for z in range(group)]
    pairs = group // 2
    base = pl.program_id(0) * pairs
    rows = side + 16
    for p in range(holders):
        v = dot(w_ref[p], columns_of(planes, p, low, side))
        v = jnp.concatenate([v[:, wide * k : wide * (k + 1)] for k in range(pairs)], 0)
        q = dot(thrice(v), c_ref[p])
        ends = [q[rows * k : rows * k + side, wide:] for k in range(pairs)]
        upper = jnp.where(first, ends[0], pltpu.roll(ends[1], 8, 1))
        lower = jnp.where(first, pltpu.roll(ends[0], wide - 8, 1), ends[1])
        turned = jnp.transpose(jnp.concatenate([upper, lower], 0))
        for k in range(pairs):
            for s in range(6):
                at = rows * k + side + s
                s_ref[p, s, pl.ds(base + k, 1), :] = q[at : at + 1, :wide]
                s_ref[p, 6 + s, pl.ds(base + k, 1), :] = turned[8 * k + s : 8 * k + s + 1]


def find_sides(modes, weights, columns, spare):
    planes, holders, cells = modes.shape
    wide = 2 * math.isqrt(cells)
    shape = (holders, SIDES, spare, wide)
    return pl.pallas_call(
        sides_kernel,
        grid=(planes // GROUP,),
        in_specs=[
            pl.BlockSpec((GROUP, holders, cells), lambda i: (i, 0, 0)),
            whole(weights.shape),
            whole(columns.shape),
        ],
        out_specs=whole(shape),
        out_shape=jax.ShapeDtypeStruct(shape, jnp.float32),
        name="sides",
        cost_estimate=pl.CostEstimate(
            flops=6 * 10**9, bytes_accessed=4 * planes * holders * cells, transcendentals=0
        ),
    )(modes, weights, columns)


def faces_kernel(table, s_ref, o_ref, count):
    doms, tiles, spare, wide = o_ref.shape
    slots = (tiles - 1) // 3
    place = iota((spare, wide), 1) % (wide // 2)
    lane = iota((1, wide), 1)
    o_ref[...] = jnp.zeros_like(o_ref)
    for d in range(doms):
        count[d] = 0

    def body(r, carry):
        length = table[r, 3]
        part = jnp.minimum(table[r, 0], s_ref.shape[0] - 1)
        facing = jnp.minimum(table[r, 1], 3)
        to = jnp.minimum(table[r, 4], doms - 1)
        seen = count[to]
        count[to] = seen + jnp.minimum(length, 1)
        slot = jnp.minimum(seen, slots - 1)
        for j in range(3):
            moved = pltpu.roll(s_ref[part, facing * 3 + j], wide - table[r, 2], 1)
            o_ref[to, slot * 3 + j] += jnp.where(place < length, moved, 0.0)
        label = jnp.where(lane == 0, table[r, 5], jnp.where(lane == 1, table[r, 6], table[r, 7]))
        label = jnp.where(lane == 3, length, label) * jnp.minimum(length, 1)
        o_ref[to, tiles - 1, pl.ds(slot, 1), :] += label.astype(jnp.float32)
        return carry

    lax.fori_loop(0, table.shape[0], body, 0, unroll=4)


def find_faces(sides, table, doms):
    holders, _, spare, wide = sides.shape
    slots = max(2, table.shape[0] // doms)
    shape = (doms, 3 * slots + 1, spare, wide)
    return pl.pallas_call(
        faces_kernel,
        grid_spec=pltpu.PrefetchScalarGridSpec(
            num_scalar_prefetch=1,
            grid=(1,),
            in_specs=[whole(sides.shape)],
            out_specs=whole(shape),
            scratch_shapes=[pltpu.SMEM((doms,), jnp.int32)],
        ),
        out_shape=jax.ShapeDtypeStruct(shape, jnp.float32),
        name="faces",
        cost_estimate=pl.CostEstimate(flops=10**8, bytes_accessed=10**6, transcendentals=0),
    )(table, sides)


def force_kernel(
    total, pairs, labels, spot, box_ref, r_ref, s_ref, ct_ref, rt_ref, sr_ref, sc_ref, now_ref,
    prev_ref, o_ref, f_ref, m_ref, b_ref,
):
    group, holders, cells = now_ref.shape
    doms, tiles, spare, wide = r_ref.shape
    side = wide // 2
    half = side // 2
    slots = (tiles - 1) // 3
    scale = (math.pi * TIME_STEP / 2) ** 2

    @pl.when(pl.program_id(0) == 0)
    def _():
        f_ref[...] = jnp.zeros_like(f_ref)
        place = iota((spare, wide), 1) % side

        def gather(n, carry):
            d, i = n // slots, n % slots
            part = labels[n, 0]
            facing = labels[n, 1]
            start = labels[n, 2]
            mask = (place >= start) & (place < start + labels[n, 3])
            jumps = [
                jnp.where(
                    mask,
                    pltpu.roll(r_ref[d, i * 3 + j], start, 1) - s_ref[part, facing * 3 + j],
                    0.0,
                )
                for j in range(3)
            ]
            for i in range(3):
                f_ref[part, facing * 3 + i] += sum(STENCIL[i + j] * jumps[j] for j in range(3 - i))
            return carry

        lax.fori_loop(0, doms * slots, gather, 0, unroll=4)
        shape = (6 * spare, wide)
        pair = iota(shape, 0) % spare
        left = iota(shape, 1) < side

        def spread(p, carry):
            f = f_ref[p, :6].reshape(6 * spare, wide)
            g = f_ref[p, 6:].reshape(6 * spare, wide)
            fc = dot(thrice(f), ct_ref[p])
            gr = dot(thrice(g), rt_ref[p])
            near = jnp.concatenate([sr_ref[p], gr[:, :side], gr[:, side:]], 0)
            sc = sc_ref[p]
            sc_left = jnp.where(left, sc, 0.0)
            sc_right = jnp.where(left, 0.0, sc)
            far = jnp.concatenate(
                [
                    jnp.concatenate([jnp.where(pair == k, t, 0.0) for t in (fc, sc_left, sc_right)], 0)
                    for k in range(pairs)
                ],
                1,
            )
            near_high, near_low = split(near)
            far_high, far_low = split(far)
            out = lax.dot_general(
                jnp.concatenate([near_high, near_low, near_high], 0),
                jnp.concatenate([far_high, far_high, far_low], 0),
                (((0,), (0,)), ((), ())),
                preferred_element_type=jnp.float32,
            )
            for k in range(pairs):
                m_ref[k, p] = out[:, k * wide : (k + 1) * wide]
            return carry

        lax.fori_loop(0, holders, spread, 0)
        cell = iota((holders, cells), 1)
        wave_row, wave_col = cell // side, cell % side
        extent_row, extent_col = box_ref[:, 0:1], box_ref[:, 1:2]
        ratio_row = wave_row.astype(jnp.float32) / extent_row.astype(jnp.float32)
        ratio_col = wave_col.astype(jnp.float32) / extent_col.astype(jnp.float32)
        inside = (wave_row < extent_row) & (wave_col < extent_col)
        b_ref[...] = jnp.where(inside, scale * (ratio_row * ratio_row + ratio_col * ratio_col), -1.0)

    low = iota((half, wide), 1) < side
    for k in range(group // 2):
        at = pl.program_id(0) * (group // 2) + k
        outs = [
            unpaired(m_ref[at, p, :half], m_ref[at, p, half:], low, side) for p in range(holders)
        ]
        for c in range(2):
            z = 2 * k + c
            force = jnp.stack([out[c] for out in outs], 0).reshape(holders, cells)
            depth = (spot[0] * 2 * pairs + pl.program_id(0) * group + z).astype(jnp.float32)
            depth = depth / total
            base = b_ref[...]
            quarter = base + scale * (depth * depth)
            ratio = jnp.float32(SERIES[-1])
            for coefficient in SERIES[-2::-1]:
                ratio = ratio * quarter + coefficient
            ratio = ratio * ratio
            updated = (
                (2.0 - 4.0 * quarter * ratio) * now_ref[z]
                - prev_ref[z]
                + (TIME_STEP * TIME_STEP) * ratio * force
            )
            o_ref[z] = jnp.where(base >= 0.0, updated, 0.0)


def advance(spot, boxes, received, sides, tables, modes_now, modes_prev, shares):
    planes, holders, cells = modes_now.shape
    doms, tiles, spare, wide = received.shape
    slots = (tiles - 1) // 3
    labels = received[:, tiles - 1, :slots, :4].astype(jnp.int32).reshape(doms * slots, 4)
    pairs = planes // 2
    operands = (boxes, received, sides, *tables)
    block = pl.BlockSpec((GROUP, holders, cells), lambda i, *_: (i, 0, 0))
    return pl.pallas_call(
        functools.partial(force_kernel, float(shares * planes), pairs),
        grid_spec=pltpu.PrefetchScalarGridSpec(
            num_scalar_prefetch=2,
            grid=(planes // GROUP,),
            in_specs=[whole(o.shape) for o in operands] + [block, block],
            out_specs=block,
            scratch_shapes=[
                pltpu.VMEM((holders, SIDES, spare, wide), jnp.float32),
                pltpu.VMEM((pairs, holders, wide // 2, wide), jnp.float32),
                pltpu.VMEM((holders, cells), jnp.float32),
            ],
        ),
        out_shape=jax.ShapeDtypeStruct(modes_now.shape, jnp.float32),
        name="force",
        cost_estimate=pl.CostEstimate(
            flops=8 * 10**9, bytes_accessed=12 * planes * holders * cells, transcendentals=0
        ),
    )(labels, spot, *operands, modes_now, modes_prev)


def cells_kernel(w_ref, c_ref, *refs):
    *part_refs, q_ref = [ref for ref in refs if ref is not None]
    group, holders, cells = q_ref.shape
    side = math.isqrt(cells)
    half = side // 2
    wide = 2 * side
    low = iota((half, wide), 1) < side
    planes = [sum(ref[z] for ref in part_refs).reshape(holders, half, wide) for z in range(group)]
    outs = [[] for _ in range(group)]
    for p in range(holders):
        v = dot(w_ref[p], columns_of(planes, p, low, side))
        v = jnp.concatenate([v[:, wide * k : wide * (k + 1)] for k in range(group // 2)], 0)
        q = dot(thrice(v), c_ref[p])
        for k in range(group // 2):
            pair = q[side * k : side * (k + 1)]
            outs[2 * k], outs[2 * k + 1] = (
                out + [new]
                for out, new in zip(outs[2 * k : 2 * k + 2], unpaired(pair[:half], pair[half:], low, side))
            )
    for z in range(group):
        q_ref[z] = jnp.stack(outs[z], 0).reshape(holders, cells)


def resumed_kernel(buffer_ref, *refs):
    cells_kernel(*refs)


def to_cells(parts, weights, columns, chunk, planes, buffer):
    group, holders, cells = parts[0].shape
    operands = [weights, columns, *parts]
    specs = [whole(o.shape) for o in operands]
    kernel, aliases = cells_kernel, {}
    if buffer is not None:
        operands = [buffer] + operands
        specs = [pl.BlockSpec(memory_space=pl.ANY)] + specs
        kernel, aliases = resumed_kernel, {0: 0}
    return pl.pallas_call(
        kernel,
        grid=(1,),
        in_specs=specs,
        out_specs=pl.BlockSpec((group, holders, cells), lambda i: (chunk, 0, 0)),
        out_shape=jax.ShapeDtypeStruct((planes, holders, cells), jnp.float32),
        input_output_aliases=aliases,
        name="cells",
        cost_estimate=pl.CostEstimate(
            flops=2 * 10**9, bytes_accessed=12 * group * holders * cells, transcendentals=0
        ),
    )(*operands)


def on_device(modes_now, modes_prev, partition_boxes, face_table):
    planes, holders, cells = modes_now.shape
    side = math.isqrt(cells)
    shares = lax.axis_size("height")
    doms = lax.axis_size("dom")
    spare = -(-planes // 16) * 8
    spot = lax.axis_index("height").astype(jnp.int32).reshape(1)
    masks = [m for m in range(shares) if m & 1 == m // (shares // 2)]
    swap = lambda mask: [(h, h ^ mask) for h in range(shares)]
    other = lax.ppermute(modes_now, "height", swap(1))
    w, c, ws, cs, *tables = make_tables(partition_boxes, side, spare)
    parts = mix(spot, modes_now, other, shares)
    sent = [[lax.ppermute(x, "height", swap(m)) for x in part] for m, part in zip(masks[1:], parts[1:])]
    later, _ = lax.optimization_barrier((modes_now, parts[0][0]))
    sides = find_sides(later, ws, cs, spare)
    outgoing = find_faces(sides, face_table, doms)
    received = lax.all_to_all(outgoing, "dom", split_axis=0, concat_axis=0, tiled=True)
    new_modes = advance(
        spot, partition_boxes, received, sides, tables, modes_now, modes_prev, shares
    )
    pressure = None
    parts[0][0], new_modes = lax.optimization_barrier((parts[0][0], new_modes))
    for k in range(planes // GROUP):
        pieces = [parts[0][k]] + [group[k] for group in sent]
        pressure = to_cells(pieces, w, c, k, planes, pressure)
    return (new_modes, pressure)


def solution(mesh):
    placed = (P("height", "dom", None), P("height", "dom", None), P("dom", None), P("dom", None))
    return jax.shard_map(
        on_device,
        mesh=mesh,
        in_specs=placed,
        out_specs=(P("height", "dom", None), P("height", "dom", None)),
        check_vma=False,
    )
```

time: 143 us -> 91.7 us (0.64)
  local copies, waits for them, and re-layouts: 59.9 us -> 4.97 us
  Pallas kernels: 17.4 us -> 54.5 us
  matrix products: 32.9 us -> 0 us
  waiting for transfers between devices: 2.37 us -> 19.1 us
  other arithmetic: 12.9 us -> 0.64 us
  starting transfers between devices: 15.1 us -> 10.9 us
    reshape x16 -> x0, local copies, waits for them, and re-layouts: 37.4 us -> none  [the longest x2 10.1 us: advance(): modes_prev.reshape(grid_shape)]
    pallas_call x2 -> x9, Pallas kernels: 17.4 us -> 54.5 us  [the longest x4 15.8 us: to_cells(): pl.pallas_call(kernel, grid=(1,), in_specs=specs, out_specs=pl.BlockSpec(...]
    dot_general x13 -> x0, matrix products: 32.9 us -> none  [the longest x1 7.66 us: to_modes(): jnp.einsum('zpkb,plb->zpkl', halfway, table_cols, precision=lax.Precision...]
    ppermute x0 -> x5, waiting for transfers between devices: none -> 9.63 us  [the longest x4 9.63 us: on_device(): lax.ppermute(x, 'height', swap(m))]
    all_to_all x3 -> x1, starting transfers between devices: 15.1 us -> 6.83 us  [on_device(): lax.all_to_all(outgoing, 'dom', split_axis=0, concat_axis=0, tiled=True)]
    all_to_all x3 -> x1, waiting for transfers between devices: 2.37 us -> 9.45 us  [on_device(): lax.all_to_all(outgoing, 'dom', split_axis=0, concat_axis=0, tiled=True)]
    select_n x2 -> x0, local copies, waits for them, and re-layouts: 5.6 us -> none  [the longest x1 5.44 us: advance(): return jnp.where(inside[None], updated, 0.0).reshape(planes, holders, cells)]
    concatenate x7 -> x0, other arithmetic: 4.17 us -> none  [the longest x1 1.28 us: cells_and_sides(): columns = jnp.concatenate([ch, ch, cl], 1)]
  transfers between devices with their start and end apart: 3 -> 6, of which waited for: 2 -> 3; matrix products, arithmetic and copies ran while one was open for 48% -> 4% of each run, Pallas kernels for 0% -> 34%
where the time goes in v1:
time: 91.7 us; the launch traced here: 90.9 us
  Pallas kernels  54.5 us (59%)
  waiting for transfers between devices  19.1 us (21%)
  starting transfers between devices  10.9 us (12%)
  local copies, waits for them, and re-layouts  4.97 us (5%)
    pallas_call x4, Pallas kernels, to_cells(): pl.pallas_call(kernel, grid=(1,), in_specs=specs, out_specs=pl.BlockSpec(...  15.8 us
    pallas_call x1, Pallas kernels, advance(): pl.pallas_call(functools.partial(force_kernel, float(shares * planes), pa...  12.3 us
    ppermute x4, waiting for transfers between devices, on_device(): lax.ppermute(x, 'height', swap(m))  9.63 us
    all_to_all x1, waiting for transfers between devices, on_device(): lax.all_to_all(outgoing, 'dom', split_axis=0, concat_axis=0, tiled=True)  9.45 us
    pallas_call x1, Pallas kernels, find_sides(): pl.pallas_call(sides_kernel, grid=(planes // GROUP,), in_specs=[pl.BlockS...  8.26 us
    pallas_call x1, Pallas kernels, mix(): pl.pallas_call(functools.partial(mix_kernel, shares * planes, chunks), gr...  7.9 us
    all_to_all x1, starting transfers between devices, on_device(): lax.all_to_all(outgoing, 'dom', split_axis=0, concat_axis=0, tiled=True)  6.83 us
    pallas_call x1, Pallas kernels, make_tables(): pl.pallas_call(tables_kernel, grid_spec=pltpu.PrefetchScalarGridSpec(num_...  6.73 us
  transfers between devices with their start and end apart: 6, of which 3 were waited for; matrix products, arithmetic and copies ran while one was open for 4% of the time, Pallas kernels for 34%

profile of v1, /device:TPU:0, one launch (start us, length us, event | category | flops | bytes accessed | tf_op | source)
XLA Modules:
  0.0 90.9 jit_solution(10000621752501802715)
XLA Ops:
  0.6 0.6 collective-permute-start
  1.2 1.3 %copy.19.boxes.box_ref = s32[8,2]{1,0:T(8,128)} copy(s32[8,2]{0,1:T(2,128)} %param.6) | data formatting | bytes 128 | tf_op args[2]
  2.5 1.4 %copy.20.table = s32[32,8]{1,0:T(8,128)} copy(s32[32,8]{0,1:T(8,128)} %param.7) | data formatting | bytes 2048 | tf_op args[3]
  3.9 6.7 %tables.1 = (bf16[8,64,192]{2,1,0:T(8,128)(2,1)}, bf16[8,384,128]{2,1,0:T(8,128)(2,1)}, bf16[8,80,192]{2,1,0:T(8,128)(2,1)}, bf16[8,384,256]{2,1,0:T(8,128)(2,1)...) custom-call(s32[8,2]{1,0:T(8,128)} %copy.19.boxes.box_ref), custom_call_target="tpu_custom_call" | custom-call | flops 1000000000 | bytes 5000000 | tf_op jit(solution)/shard_map/tables/pallas_call | solution.py:132
  10.6 1.3 %copy-done.1 = f32[16,8,4096]{2,1,0:T(8,128)} copy-done((f32[16,8,4096]{2,1,0:T(8,128)}, f32[16,8,4096]{2,1,0:T(8,128)S(1)}, u32[]{:S(2)}) %copy-start.1) | copy-done | bytes 2097176
  11.9 7.9 %mix.1 = (f32[4,8,4096]{2,1,0:T(8,128)}, f32[4,8,4096]{2,1,0:T(8,128)}, f32[4,8,4096]{2,1,0:T(8,128)}, f32[4,8,4096]{2,1,0:T(8,128)}, f32[4,8,4096]{2,1,0:T(8,12...) custom-call(s32[1]{0:T(128)} %bitcast.spot, f32[16,8,4096]{2,1,0:T(8,128)} %now_ref.1, ...), custom_call_target="tpu_custom_call" | custom-call | flops 3000000000 | bytes 8388608 | tf_op jit(solution)/shard_map/mix/pallas_call | solution.py:182
  19.9 8.3 %sides.1.s_ref = f32[8,12,8,128]{3,2,1,0:T(8,128)} custom-call(f32[16,8,4096]{2,1,0:T(8,128)} %now_ref.1, bf16[8,80,192]{2,1,0:T(8,128)(2,1)} %get-tuple-element.23.w_ref, bf16[8,384,256]{2,1,0:T(8,128)(2,1)} %get-tuple-element.24.c_ref), custom_call_target="tpu_custom_call" | custom-call | flops 6000000000 | bytes 2097152 | tf_op jit(solution)/shard_map/sides/pallas_call | solution.py:249
  28.1 3.5 %faces.1 = f32[8,13,8,128]{3,2,1,0:T(8,128)} custom-call(s32[32,8]{1,0:T(8,128)} %copy.20.table, f32[8,12,8,128]{3,2,1,0:T(8,128)} %sides.1.s_ref), custom_call_target="tpu_custom_call" | custom-call | flops 100000000 | bytes 1000000 | tf_op jit(solution)/shard_map/faces/pallas_call | solution.py:298
  31.6 6.8 %all-to-all-start = ((f32[8,13,8,128]{3,2,1,0:T(8,128)}), f32[8,13,8,128]{3,2,1,0:T(8,128)S(1)}, u32[]{:S(2)}, u32[]{:S(2)}) async-start(f32[8,13,8,128]{3,2,1,0:T(8,128)} %faces.1), calls=%async_computation | async-start | bytes 851968 | tf_op jit(solution)/shard_map/all_to_all | solution.py:509
  38.5 1.4 %collective-permute-start.1 = (f32[4,8,4096]{2,1,0:T(8,128)S(1)}, f32[4,8,4096]{2,1,0:T(8,128)}, u32[]{:S(2)}, u32[]{:S(2)}) collective-permute-start(f32[4,8,4096]{2,1,0:T(8,128)S(1)} %copy-done.5), channel_id=1, source_target_pairs={{0,24},{8,16},{16,8},{24,0},{1,25},{9,17},{17,9},{25,1},{2,26},{10... | collective-permute-start | bytes 1572872 | tf_op jit(solution)/shard_map/ppermute | solution.py:505
  39.8 0.4 collective-permute-start.2
  40.3 1.3 %collective-permute-start.3 = (f32[4,8,4096]{2,1,0:T(8,128)S(1)}, f32[4,8,4096]{2,1,0:T(8,128)}, u32[]{:S(2)}, u32[]{:S(2)}) collective-permute-start(f32[4,8,4096]{2,1,0:T(8,128)S(1)} %copy-done.3), channel_id=1, source_target_pairs={{0,24},{8,16},{16,8},{24,0},{1,25},{9,17},{17,9},{25,1},{2,26},{10... | collective-permute-start | bytes 1572872 | tf_op jit(solution)/shard_map/ppermute | solution.py:505
  41.6 0.4 collective-permute-start.4
  42.0 9.5 %all-to-all-done.r_ref = f32[8,13,8,128]{3,2,1,0:T(8,128)S(1)} async-done(((f32[8,13,8,128]{3,2,1,0:T(8,128)}), f32[8,13,8,128]{3,2,1,0:T(8,128)S(1)}, u32[]{:S(2)}, u32[]{:S(2)}) %all-to-all-start) | async-done | bytes 426016 | tf_op jit(solution)/shard_map/all_to_all | solution.py:509
  51.5 0.6 slice_convert_fusion
  52.1 0.1 copy-done
  52.3 12.3 %force.1 = f32[16,8,4096]{2,1,0:T(8,128)} custom-call(s32[32,4]{1,0:T(8,128)} %bitcast.2, s32[1]{0:T(128)} %bitcast.spot, s32[8,2]{1,0:T(8,128)} %copy.19.boxes.box_ref, f32[8,13,8,128]{3,2,1,0:T(8,128)} %copy-done, f32[8,12,8,128]{3,2,1,0:T(8,128)} %sides.1.s_ref, bf16[8,384,128]{2,1,0:T(8,128)(2,1)} %get-tuple-element.25.ct_ref, ...), custom_call_target="tpu_custom_call" | custom-call | flops 8000000000 | bytes 6291456 | tf_op jit(solution)/shard_map/force/pallas_call | solution.py:422
  64.6 4.0 %cells.4.buffer_ref = f32[16,8,4096]{2,1,0:T(8,128)} custom-call(bf16[8,64,192]{2,1,0:T(8,128)(2,1)} %get-tuple-element.30.w_ref.refs_0_, bf16[8,384,128]{2,1,0:T(8,128)(2,1)} %get-tuple-element.31.c_ref.refs_1_, f32[4,8,4096]{2,1,0:T(8,128)} %get-tuple-element.32.refs_0_, f32[4,8,4096]{2,1,0:T(8,128)} %collective-permute-done.1.refs_1_), custom_call_target="tpu_custom_call" | custom-call | flops 2000000000 | bytes 1572864 | tf_op jit(solution)/shard_map/cells/pallas_call | solution.py:479
  68.5 4.0 %cells.5.buffer_ref = f32[16,8,4096]{2,1,0:T(8,128)} custom-call(f32[16,8,4096]{2,1,0:T(8,128)} %cells.4.buffer_ref, bf16[8,64,192]{2,1,0:T(8,128)(2,1)} %get-tuple-element.30.w_ref.refs_0_, bf16[8,384,128]{2,1,0:T(8,128)(2,1)} %get-tuple-element.31.c_ref.refs_1_, f32[4,8,4096]{2,1,0:T(8,128)} %get-tuple-element.34.refs_2_, ...), custom_call_target="tpu_custom_call", output_to_operand_aliasing={{}: (0, {})} | custom-call | flops 2000000000 | bytes 1572864 | tf_op jit(solution)/shard_map/cells/pallas_call | solution.py:479
  72.5 2.4 %collective-permute-done.3.refs_3_ = f32[4,8,4096]{2,1,0:T(8,128)} collective-permute-done((f32[4,8,4096]{2,1,0:T(8,128)S(1)}, f32[4,8,4096]{2,1,0:T(8,128)}, u32[]{:S(2)}, u32[]{:S(2)}) %collective-permute-start.3) | collective-permute-done | bytes 524320 | tf_op jit(solution)/shard_map/ppermute | solution.py:505
  75.0 4.0 %cells.6.buffer_ref = f32[16,8,4096]{2,1,0:T(8,128)} custom-call(f32[16,8,4096]{2,1,0:T(8,128)} %cells.5.buffer_ref, bf16[8,64,192]{2,1,0:T(8,128)(2,1)} %get-tuple-element.30.w_ref.refs_0_, bf16[8,384,128]{2,1,0:T(8,128)(2,1)} %get-tuple-element.31.c_ref.refs_1_, f32[4,8,4096]{2,1,0:T(8,128)} %get-tuple-element.36.refs_2_, ...), custom_call_target="tpu_custom_call", output_to_operand_aliasing={{}: (0, {})} | custom-call | flops 2000000000 | bytes 1572864 | tf_op jit(solution)/shard_map/cells/pallas_call | solution.py:479
  78.9 7.2 %collective-permute-done.4.refs_3_ = f32[4,8,4096]{2,1,0:T(8,128)S(1)} collective-permute-done((f32[4,8,4096]{2,1,0:T(8,128)S(1)}, f32[4,8,4096]{2,1,0:T(8,128)S(1)}, u32[]{:S(2)}, u32[]{:S(2)}) %collective-permute-start.4) | collective-permute-done | bytes 524320 | tf_op jit(solution)/shard_map/ppermute | solution.py:505
  86.1 0.8 copy-done.6
  86.9 4.0 %cells.7 = f32[16,8,4096]{2,1,0:T(8,128)} custom-call(f32[16,8,4096]{2,1,0:T(8,128)} %cells.6.buffer_ref, bf16[8,64,192]{2,1,0:T(8,128)(2,1)} %get-tuple-element.30.w_ref.refs_0_, bf16[8,384,128]{2,1,0:T(8,128)(2,1)} %get-tuple-element.31.c_ref.refs_1_, f32[4,8,4096]{2,1,0:T(8,128)} %get-tuple-element.38.refs_2_, ...), custom_call_target="tpu_custom_call", output_to_operand_aliasing={{}: (0, {})} | custom-call | flops 2000000000 | bytes 1572864 | tf_op jit(solution)/shard_map/cells/pallas_call | solution.py:479
  (14 shorter events, 0.0 us)
Async XLA Ops:
  0.6 10.0 %collective-permute-start = (f32[16,8,4096]{2,1,0:T(8,128)}, f32[16,8,4096]{2,1,0:T(8,128)S(1)}, u32[]{:S(2)}, u32[]{:S(2)}) collective-permute-start(f32[16,8,4096]{2,1,0:T(8,128)} %now_ref.1), channel_id=1, source_target_pairs={{0,8},{8,0},{16,24},{24,16},{1,9},{9,1},{17,25},{25,17},{2,10},{10... | collective-permute-start | bytes 6291464 | tf_op jit(solution)/shard_map/ppermute | solution.py:502
  10.6 1.3 %copy-start.1 = (f32[16,8,4096]{2,1,0:T(8,128)}, f32[16,8,4096]{2,1,0:T(8,128)S(1)}, u32[]{:S(2)}) copy-start(f32[16,8,4096]{2,1,0:T(8,128)S(1)} %collective-permute-done.other_ref) | copy-start | bytes 6291460
  19.8 18.6 %copy-start.5 = (f32[4,8,4096]{2,1,0:T(8,128)S(1)}, f32[4,8,4096]{2,1,0:T(8,128)}, u32[]{:S(2)}) copy-start(f32[4,8,4096]{2,1,0:T(8,128)} %get-tuple-element.33) | copy-start | bytes 1572868
  19.8 20.0 %copy-start.4 = (f32[4,8,4096]{2,1,0:T(8,128)S(1)}, f32[4,8,4096]{2,1,0:T(8,128)}, u32[]{:S(2)}) copy-start(f32[4,8,4096]{2,1,0:T(8,128)} %get-tuple-element.35) | copy-start | bytes 1572868
  19.8 20.4 %copy-start.3 = (f32[4,8,4096]{2,1,0:T(8,128)S(1)}, f32[4,8,4096]{2,1,0:T(8,128)}, u32[]{:S(2)}) copy-start(f32[4,8,4096]{2,1,0:T(8,128)} %get-tuple-element.37) | copy-start | bytes 1572868
  19.9 21.7 %copy-start.2 = (f32[4,8,4096]{2,1,0:T(8,128)S(1)}, f32[4,8,4096]{2,1,0:T(8,128)}, u32[]{:S(2)}) copy-start(f32[4,8,4096]{2,1,0:T(8,128)} %get-tuple-element.39) | copy-start | bytes 1572868
  31.6 19.9 %all-to-all-start = ((f32[8,13,8,128]{3,2,1,0:T(8,128)}), f32[8,13,8,128]{3,2,1,0:T(8,128)S(1)}, u32[]{:S(2)}, u32[]{:S(2)}) async-start(f32[8,13,8,128]{3,2,1,0:T(8,128)} %faces.1), calls=%async_computation | async-start | bytes 851968 | tf_op jit(solution)/shard_map/all_to_all | solution.py:509
  38.5 26.1 %collective-permute-start.1 = (f32[4,8,4096]{2,1,0:T(8,128)S(1)}, f32[4,8,4096]{2,1,0:T(8,128)}, u32[]{:S(2)}, u32[]{:S(2)}) collective-permute-start(f32[4,8,4096]{2,1,0:T(8,128)S(1)} %copy-done.5), channel_id=1, source_target_pairs={{0,24},{8,16},{16,8},{24,0},{1,25},{9,17},{17,9},{25,1},{2,26},{10... | collective-permute-start | bytes 1572872 | tf_op jit(solution)/shard_map/ppermute | solution.py:505
  39.8 28.7 %collective-permute-start.2 = (f32[4,8,4096]{2,1,0:T(8,128)S(1)}, f32[4,8,4096]{2,1,0:T(8,128)}, u32[]{:S(2)}, u32[]{:S(2)}) collective-permute-start(f32[4,8,4096]{2,1,0:T(8,128)S(1)} %copy-done.4), channel_id=1, source_target_pairs={{0,24},{8,16},{16,8},{24,0},{1,25},{9,17},{17,9},{25,1},{2,26},{10... | collective-permute-start | bytes 1572872 | tf_op jit(solution)/shard_map/ppermute | solution.py:505
  40.3 34.7 %collective-permute-start.3 = (f32[4,8,4096]{2,1,0:T(8,128)S(1)}, f32[4,8,4096]{2,1,0:T(8,128)}, u32[]{:S(2)}, u32[]{:S(2)}) collective-permute-start(f32[4,8,4096]{2,1,0:T(8,128)S(1)} %copy-done.3), channel_id=1, source_target_pairs={{0,24},{8,16},{16,8},{24,0},{1,25},{9,17},{17,9},{25,1},{2,26},{10... | collective-permute-start | bytes 1572872 | tf_op jit(solution)/shard_map/ppermute | solution.py:505
  41.6 44.5 %collective-permute-start.4 = (f32[4,8,4096]{2,1,0:T(8,128)S(1)}, f32[4,8,4096]{2,1,0:T(8,128)S(1)}, u32[]{:S(2)}, u32[]{:S(2)}) collective-permute-start(f32[4,8,4096]{2,1,0:T(8,128)S(1)} %copy-done.2), channel_id=1, source_target_pairs={{0,24},{8,16},{16,8},{24,0},{1,25},{9,17},{17,9},{25,1},{2,26},{10... | collective-permute-start | bytes 1572872 | tf_op jit(solution)/shard_map/ppermute | solution.py:505
  51.5 0.8 copy-start
  86.1 0.8 copy-start.6

commit v2 on v1

--- a/solution.py
+++ b/solution.py
@@ -8,12 +8,14 @@
 from jax.experimental.pallas import tpu as pltpu
 from jax.sharding import PartitionSpec as P
 
+
 COUPLING = 32.0
 STENCIL = (COUPLING * 270.0 / 180.0, COUPLING * -27.0 / 180.0, COUPLING * 2.0 / 180.0)
 TIME_STEP = 0.4
 SERIES = (1.0, -1.0 / 6, 1.0 / 120, -1.0 / 5040, 1.0 / 362880, -1.0 / 39916800, 1.0 / 6227020800)
 GROUP = 4
 SIDES = 12
+ROOM = pltpu.CompilerParams(vmem_limit_bytes=24 * 2**20)
 
 
 def iota(shape, axis):
@@ -139,6 +141,7 @@
         ),
         out_shape=[jax.ShapeDtypeStruct(*shape) for shape in shapes],
         name="tables",
+        compiler_params=ROOM,
         cost_estimate=pl.CostEstimate(flops=10**9, bytes_accessed=5 * 10**6, transcendentals=0),
     )(boxes)
 
@@ -146,7 +149,7 @@
 def mix_kernel(total, chunks, spot, own_ref, other_ref, *refs):
     *out_refs, t_ref = refs
     planes, holders, step = own_ref.shape
-    rows, cols = planes * holders * (len(out_refs) // chunks), 2 * planes * holders
+    cols = 2 * planes * holders
     me = spot[0]
     masks = [m for m in range(total // planes) if m & 1 == m // (total // planes // 2)]
 
@@ -192,6 +195,7 @@
         ),
         out_shape=[part] * (count * chunks),
         name="mix",
+        compiler_params=ROOM,
         cost_estimate=pl.CostEstimate(
             flops=3 * 10**9, bytes_accessed=16 * planes * holders * cells, transcendentals=0
         ),
@@ -257,6 +261,7 @@
         out_specs=whole(shape),
         out_shape=jax.ShapeDtypeStruct(shape, jnp.float32),
         name="sides",
+        compiler_params=ROOM,
         cost_estimate=pl.CostEstimate(
             flops=6 * 10**9, bytes_accessed=4 * planes * holders * cells, transcendentals=0
         ),
@@ -292,7 +297,7 @@
 
 
 def find_faces(sides, table, doms):
-    holders, _, spare, wide = sides.shape
+    _, _, spare, wide = sides.shape
     slots = max(2, table.shape[0] // doms)
     shape = (doms, 3 * slots + 1, spare, wide)
     return pl.pallas_call(
@@ -306,6 +311,7 @@
         ),
         out_shape=jax.ShapeDtypeStruct(shape, jnp.float32),
         name="faces",
+        compiler_params=ROOM,
         cost_estimate=pl.CostEstimate(flops=10**8, bytes_accessed=10**6, transcendentals=0),
     )(table, sides)
 
@@ -434,6 +440,7 @@
         ),
         out_shape=jax.ShapeDtypeStruct(modes_now.shape, jnp.float32),
         name="force",
+        compiler_params=ROOM,
         cost_estimate=pl.CostEstimate(
             flops=8 * 10**9, bytes_accessed=12 * planes * holders * cells, transcendentals=0
         ),
@@ -484,6 +491,7 @@
         out_shape=jax.ShapeDtypeStruct((planes, holders, cells), jnp.float32),
         input_output_aliases=aliases,
         name="cells",
+        compiler_params=ROOM,
         cost_estimate=pl.CostEstimate(
             flops=2 * 10**9, bytes_accessed=12 * group * holders * cells, transcendentals=0
         ),
@@ -491,7 +499,7 @@
 
 
 def on_device(modes_now, modes_prev, partition_boxes, face_table):
-    planes, holders, cells = modes_now.shape
+    planes, _, cells = modes_now.shape
     side = math.isqrt(cells)
     shares = lax.axis_size("height")
     doms = lax.axis_size("dom")
@@ -502,7 +510,9 @@
     other = lax.ppermute(modes_now, "height", swap(1))
     w, c, ws, cs, *tables = make_tables(partition_boxes, side, spare)
     parts = mix(spot, modes_now, other, shares)
-    sent = [[lax.ppermute(x, "height", swap(m)) for x in part] for m, part in zip(masks[1:], parts[1:])]
+    sent = []
+    for m, part in zip(masks[1:], parts[1:]):
+        sent.append([lax.ppermute(x, "height", swap(m)) for x in part])
     later, _ = lax.optimization_barrier((modes_now, parts[0][0]))
     sides = find_sides(later, ws, cs, spare)
     outgoing = find_faces(sides, face_table, doms)
@@ -520,6 +530,7 @@
 
 def solution(mesh):
     placed = (P("height", "dom", None), P("height", "dom", None), P("dom", None), P("dom", None))
+
     return jax.shard_map(
         on_device,
         mesh=mesh,

time: 91.7 us -> 85.8 us (0.936)
  Pallas kernels: 54.5 us -> 42.9 us
  local copies, waits for them, and re-layouts: 4.97 us -> 12 us
    unnamed x16 -> x52, local copies, waits for them, and re-layouts: 4.97 us -> 12 us
    pallas_call x1, Pallas kernels: 12.3 us -> 9.52 us  [advance(): pl.pallas_call(functools.partial(force_kernel, float(shares * planes), pa...]
    pallas_call x1, Pallas kernels: 8.26 us -> 5.72 us  [find_sides(): pl.pallas_call(sides_kernel, grid=(planes // GROUP,), in_specs=[pl.BlockS...]
    pallas_call x1, Pallas kernels: 6.73 us -> 4.67 us  [make_tables(): pl.pallas_call(tables_kernel, grid_spec=pltpu.PrefetchScalarGridSpec(num_...]
    pallas_call x4, Pallas kernels: 15.8 us -> 14.1 us  [to_cells(): pl.pallas_call(kernel, grid=(1,), in_specs=specs, out_specs=pl.BlockSpec(...]
    pallas_call x1, Pallas kernels: 7.9 us -> 6.43 us  [mix(): pl.pallas_call(functools.partial(mix_kernel, shares * planes, chunks), gr...]
    pallas_call x1, Pallas kernels: 3.51 us -> 2.4 us  [find_faces(): pl.pallas_call(faces_kernel, grid_spec=pltpu.PrefetchScalarGridSpec(num_s...]
  transfers between devices with their start and end apart: 6 -> 6, of which waited for: 3 -> 3; matrix products, arithmetic and copies ran while one was open for 4% -> 2% of each run, Pallas kernels for 34% -> 29%
where the time goes in v2:
time: 85.8 us; the launch traced here: 85.2 us
  Pallas kernels  42.9 us (50%)
  waiting for transfers between devices  18.6 us (22%)
  local copies, waits for them, and re-layouts  12 us (14%)
  starting transfers between devices  11 us (13%)
    pallas_call x4, Pallas kernels, to_cells(): pl.pallas_call(kernel, grid=(1,), in_specs=specs, out_specs=pl.BlockSpec(...  14.1 us
    unnamed x52, local copies, waits for them, and re-layouts  12 us
    pallas_call x1, Pallas kernels, advance(): pl.pallas_call(functools.partial(force_kernel, float(shares * planes), pa...  9.52 us
    all_to_all x1, waiting for transfers between devices, on_device(): lax.all_to_all(outgoing, 'dom', split_axis=0, concat_axis=0, tiled=True)  9.41 us
    ppermute x4, waiting for transfers between devices, on_device(): sent.append([lax.ppermute(x, 'height', swap(m)) for x in part])  9.15 us
    all_to_all x1, starting transfers between devices, on_device(): lax.all_to_all(outgoing, 'dom', split_axis=0, concat_axis=0, tiled=True)  6.9 us
    pallas_call x1, Pallas kernels, mix(): pl.pallas_call(functools.partial(mix_kernel, shares * planes, chunks), gr...  6.43 us
    pallas_call x1, Pallas kernels, find_sides(): pl.pallas_call(sides_kernel, grid=(planes // GROUP,), in_specs=[pl.BlockS...  5.72 us
  transfers between devices with their start and end apart: 6, of which 3 were waited for; matrix products, arithmetic and copies ran while one was open for 2% of the time, Pallas kernels for 29%

profile of v2, /device:TPU:0, one launch (start us, length us, event | category | flops | bytes accessed | tf_op | source)
XLA Modules:
  0.0 85.2 jit_solution(7425551691238584882)
XLA Ops:
  1.2 0.8 copy.19.boxes.box_ref
  2.8 4.7 %tables.1 = (bf16[8,64,192]{2,1,0:T(8,128)(2,1)S(1)}, bf16[8,384,128]{2,1,0:T(8,128)(2,1)S(1)}, bf16[8,80,192]{2,1,0:T(8,128)(2,1)S(1)}, bf16[8,384,256]{2,1,0:T...) custom-call(s32[8,2]{1,0:T(8,128)S(1)} %copy.19.boxes.box_ref), custom_call_target="tpu_custom_call" | custom-call | flops 1000000000 | bytes 5000000 | tf_op jit(solution)/shard_map/tables/pallas_call | solution.py:134
  7.5 0.9 %copy-done.5 = bf16[8,384,128]{2,1,0:T(8,128)(2,1)} copy-done((bf16[8,384,128]{2,1,0:T(8,128)(2,1)}, bf16[8,384,128]{2,1,0:T(8,128)(2,1)S(1)}, u32[]{:S(2)}) %copy-start.5) | copy-done | bytes 786456
  9.0 0.9 %copy-done.15 = bf16[8,384,128]{2,1,0:T(8,128)(2,1)} copy-done((bf16[8,384,128]{2,1,0:T(8,128)(2,1)}, bf16[8,384,128]{2,1,0:T(8,128)(2,1)S(1)}, u32[]{:S(2)}) %copy-start.15) | copy-done | bytes 786456
  9.9 0.9 %copy-done.17 = bf16[8,384,128]{2,1,0:T(8,128)(2,1)} copy-done((bf16[8,384,128]{2,1,0:T(8,128)(2,1)}, bf16[8,384,128]{2,1,0:T(8,128)(2,1)S(1)}, u32[]{:S(2)}) %copy-start.17) | copy-done | bytes 786456
  12.1 6.4 %mix.1 = (f32[4,8,4096]{2,1,0:T(8,128)S(1)}, f32[4,8,4096]{2,1,0:T(8,128)S(1)}, f32[4,8,4096]{2,1,0:T(8,128)S(1)}, f32[4,8,4096]{2,1,0:T(8,128)S(1)}, f32[4,8,40...) custom-call(s32[1]{0:T(128)} %bitcast.spot, ...), custom_call_target="tpu_custom_call" | custom-call | flops 3000000000 | bytes 8388608 | tf_op jit(solution)/shard_map/mix/pallas_call | solution.py:185
  18.6 5.7 %sides.1.s_ref = f32[8,12,8,128]{3,2,1,0:T(8,128)S(1)} custom-call(f32[16,8,4096]{2,1,0:T(8,128)S(1)} %copy-done, bf16[8,80,192]{2,1,0:T(8,128)(2,1)S(1)} %get-tuple-element.23.w_ref, bf16[8,384,256]{2,1,0:T(8,128)(2,1)S(1)} %get-tuple-element.24.c_ref), custom_call_target="tpu_custom_call" | custom-call | flops 6000000000 | bytes 2097152 | tf_op jit(solution)/shard_map/sides/pallas_call | solution.py:253
  24.4 2.4 %faces.1 = f32[8,13,8,128]{3,2,1,0:T(8,128)} custom-call(s32[32,8]{1,0:T(8,128)S(1)} %copy.20.table, f32[8,12,8,128]{3,2,1,0:T(8,128)S(1)} %sides.1.s_ref), custom_call_target="tpu_custom_call" | custom-call | flops 100000000 | bytes 1000000 | tf_op jit(solution)/shard_map/faces/pallas_call | solution.py:303
  26.8 6.9 %all-to-all-start = ((f32[8,13,8,128]{3,2,1,0:T(8,128)}), f32[8,13,8,128]{3,2,1,0:T(8,128)S(1)}, u32[]{:S(2)}, u32[]{:S(2)}) async-start(f32[8,13,8,128]{3,2,1,0:T(8,128)} %faces.1), calls=%async_computation | async-start | bytes 851968 | tf_op jit(solution)/shard_map/all_to_all | solution.py:519
  33.7 1.2 %collective-permute-start.1 = (f32[4,8,4096]{2,1,0:T(8,128)}, f32[4,8,4096]{2,1,0:T(8,128)}, u32[]{:S(2)}, u32[]{:S(2)}) collective-permute-start(f32[4,8,4096]{2,1,0:T(8,128)} %copy-done.4), channel_id=1, source_target_pairs={{0,24},{8,16},{16,8},{24,0},{1,25},{9,17},{17,9},{25,1},{2,26},{10... | collective-permute-start | bytes 1572872 | tf_op jit(solution)/shard_map/ppermute | solution.py:515
  35.5 1.2 %collective-permute-start.3 = (f32[4,8,4096]{2,1,0:T(8,128)}, f32[4,8,4096]{2,1,0:T(8,128)}, u32[]{:S(2)}, u32[]{:S(2)}) collective-permute-start(f32[4,8,4096]{2,1,0:T(8,128)} %copy-done.2), channel_id=1, source_target_pairs={{0,24},{8,16},{16,8},{24,0},{1,25},{9,17},{17,9},{25,1},{2,26},{10... | collective-permute-start | bytes 1572872 | tf_op jit(solution)/shard_map/ppermute | solution.py:515
  37.2 9.4 %all-to-all-done.r_ref = f32[8,13,8,128]{3,2,1,0:T(8,128)S(1)} async-done(((f32[8,13,8,128]{3,2,1,0:T(8,128)}), f32[8,13,8,128]{3,2,1,0:T(8,128)S(1)}, u32[]{:S(2)}, u32[]{:S(2)}) %all-to-all-start) | async-done | bytes 426016 | tf_op jit(solution)/shard_map/all_to_all | solution.py:519
  46.6 1.6 %copy-done.1 = f32[16,8,4096]{2,1,0:T(8,128)S(1)} copy-done((f32[16,8,4096]{2,1,0:T(8,128)S(1)}, f32[16,8,4096]{2,1,0:T(8,128)}, u32[]{:S(2)}) %copy-start.1) | copy-done | bytes 2097176
  48.2 1.1 %copy-done.16 = bf16[8,384,128]{2,1,0:T(8,128)(2,1)S(1)} copy-done((bf16[8,384,128]{2,1,0:T(8,128)(2,1)S(1)}, bf16[8,384,128]{2,1,0:T(8,128)(2,1)}, u32[]{:S(2)}) %copy-start.16) | copy-done | bytes 786456
  49.4 1.1 %copy-done.18 = bf16[8,384,128]{2,1,0:T(8,128)(2,1)S(1)} copy-done((bf16[8,384,128]{2,1,0:T(8,128)(2,1)S(1)}, bf16[8,384,128]{2,1,0:T(8,128)(2,1)}, u32[]{:S(2)}) %copy-start.18) | copy-done | bytes 786456
  50.5 0.9 %copy-done.22 = f32[8,48,64]{2,1,0:T(8,128)S(1)} copy-done((f32[8,48,64]{2,1,0:T(8,128)S(1)}, f32[8,48,64]{2,1,0:T(8,128)}, u32[]{:S(2)}) %copy-start.22) | copy-done | bytes 98328
  51.4 0.9 %copy-done.24 = f32[8,48,128]{2,1,0:T(8,128)S(1)} copy-done((f32[8,48,128]{2,1,0:T(8,128)S(1)}, f32[8,48,128]{2,1,0:T(8,128)}, u32[]{:S(2)}) %copy-start.24) | copy-done | bytes 196632
  52.4 9.5 %force.1 = f32[16,8,4096]{2,1,0:T(8,128)} custom-call(s32[32,4]{1,0:T(8,128)S(1)} %bitcast.2, s32[1]{0:T(128)} %bitcast.spot, s32[8,2]{1,0:T(8,128)S(1)} %copy.19.boxes.box_ref, f32[8,13,8,128]{3,2,1,0:T(8,128)S(1)} %all-to-all-done.r_ref, f32[8,12,8,128]{3,2,1,0:T(8,128)S(1)} %sides.1.s_ref, bf16[8,384,128]{2,1,0:T(8,128)(2,1)S(1)} %copy-done.16, ...), custom_call_target="tpu_custom_call" | custom-call | flops 8000000000 | bytes 6291456 | tf_op jit(solution)/shard_map/force/pallas_call | solution.py:428
  61.9 3.5 %cells.4.buffer_ref = f32[16,8,4096]{2,1,0:T(8,128)} custom-call(bf16[8,64,192]{2,1,0:T(8,128)(2,1)S(1)} %copy-done.14, bf16[8,384,128]{2,1,0:T(8,128)(2,1)S(1)} %copy-done.6, f32[4,8,4096]{2,1,0:T(8,128)S(1)} %copy-done.20, f32[4,8,4096]{2,1,0:T(8,128)} %collective-permute-done.1.refs_1_), custom_call_target="tpu_custom_call" | custom-call | flops 2000000000 | bytes 1572864 | tf_op jit(solution)/shard_map/cells/pallas_call | solution.py:486
  65.5 3.5 %cells.5.buffer_ref = f32[16,8,4096]{2,1,0:T(8,128)} custom-call(f32[16,8,4096]{2,1,0:T(8,128)} %cells.4.buffer_ref, bf16[8,64,192]{2,1,0:T(8,128)(2,1)S(1)} %copy-done.14, bf16[8,384,128]{2,1,0:T(8,128)(2,1)S(1)} %copy-done.6, f32[4,8,4096]{2,1,0:T(8,128)S(1)} %copy-done.12, ...), custom_call_target="tpu_custom_call", output_to_operand_aliasing={{}: (0, {})} | custom-call | flops 2000000000 | bytes 1572864 | tf_op jit(solution)/shard_map/cells/pallas_call | solution.py:486
  69.0 1.5 %collective-permute-done.3.refs_3_ = f32[4,8,4096]{2,1,0:T(8,128)} collective-permute-done((f32[4,8,4096]{2,1,0:T(8,128)}, f32[4,8,4096]{2,1,0:T(8,128)}, u32[]{:S(2)}, u32[]{:S(2)}) %collective-permute-start.3) | collective-permute-done | bytes 524320 | tf_op jit(solution)/shard_map/ppermute | solution.py:515
  70.5 3.5 %cells.6.buffer_ref = f32[16,8,4096]{2,1,0:T(8,128)} custom-call(f32[16,8,4096]{2,1,0:T(8,128)} %cells.5.buffer_ref, bf16[8,64,192]{2,1,0:T(8,128)(2,1)S(1)} %copy-done.14, bf16[8,384,128]{2,1,0:T(8,128)(2,1)S(1)} %copy-done.6, f32[4,8,4096]{2,1,0:T(8,128)S(1)} %copy-done.10, ...), custom_call_target="tpu_custom_call", output_to_operand_aliasing={{}: (0, {})} | custom-call | flops 2000000000 | bytes 1572864 | tf_op jit(solution)/shard_map/cells/pallas_call | solution.py:486
  74.0 7.7 %collective-permute-done.4.refs_3_ = f32[4,8,4096]{2,1,0:T(8,128)} collective-permute-done((f32[4,8,4096]{2,1,0:T(8,128)S(1)}, f32[4,8,4096]{2,1,0:T(8,128)}, u32[]{:S(2)}, u32[]{:S(2)}) %collective-permute-start.4) | collective-permute-done | bytes 524320 | tf_op jit(solution)/shard_map/ppermute | solution.py:515
  81.7 3.5 %cells.7 = f32[16,8,4096]{2,1,0:T(8,128)} custom-call(f32[16,8,4096]{2,1,0:T(8,128)} %cells.6.buffer_ref, bf16[8,64,192]{2,1,0:T(8,128)(2,1)S(1)} %copy-done.14, bf16[8,384,128]{2,1,0:T(8,128)(2,1)S(1)} %copy-done.6, f32[4,8,4096]{2,1,0:T(8,128)S(1)} %copy-done.8, f32[4,8,4096]{2,1,0:T(8,128)} %collective-permute-done.4.refs_3_), custom_call_target="tpu_custom_call", output_to_operand_aliasing={{}: (0, {})} | custom-call | flops 2000000000 | bytes 1572864 | tf_op jit(solution)/shard_map/cells/pallas_call | solution.py:486
  (50 shorter events, 4.6 us)
Async XLA Ops:
  0.6 11.5 %copy-start = (f32[16,8,4096]{2,1,0:T(8,128)S(1)}, f32[16,8,4096]{2,1,0:T(8,128)}, u32[]{:S(2)}) copy-start(f32[16,8,4096]{2,1,0:T(8,128)} %now_ref.1) | copy-start | bytes 6291460
  0.6 11.5 %collective-permute-start = (f32[16,8,4096]{2,1,0:T(8,128)}, f32[16,8,4096]{2,1,0:T(8,128)}, u32[]{:S(2)}, u32[]{:S(2)}) collective-permute-start(f32[16,8,4096]{2,1,0:T(8,128)} %now_ref.1), channel_id=1, source_target_pairs={{0,8},{8,0},{16,24},{24,16},{1,9},{9,1},{17,25},{25,17},{2,10},{10... | collective-permute-start | bytes 6291464 | tf_op jit(solution)/shard_map/ppermute | solution.py:510
  18.6 5.8 %copy-start.2 = (f32[4,8,4096]{2,1,0:T(8,128)}, f32[4,8,4096]{2,1,0:T(8,128)S(1)}, u32[]{:S(2)}) copy-start(f32[4,8,4096]{2,1,0:T(8,128)S(1)} %get-tuple-element.37) | copy-start | bytes 1572868
  18.6 5.8 %copy-start.3 = (f32[4,8,4096]{2,1,0:T(8,128)}, f32[4,8,4096]{2,1,0:T(8,128)S(1)}, u32[]{:S(2)}) copy-start(f32[4,8,4096]{2,1,0:T(8,128)S(1)} %get-tuple-element.35) | copy-start | bytes 1572868
  18.6 5.8 %copy-start.4 = (f32[4,8,4096]{2,1,0:T(8,128)}, f32[4,8,4096]{2,1,0:T(8,128)S(1)}, u32[]{:S(2)}) copy-start(f32[4,8,4096]{2,1,0:T(8,128)S(1)} %get-tuple-element.33) | copy-start | bytes 1572868
  18.6 5.8 %copy-start.7 = (f32[4,8,4096]{2,1,0:T(8,128)}, f32[4,8,4096]{2,1,0:T(8,128)S(1)}, u32[]{:S(2)}) copy-start(f32[4,8,4096]{2,1,0:T(8,128)S(1)} %get-tuple-element.38.refs_2_) | copy-start | bytes 1572868
  18.6 5.8 %copy-start.9 = (f32[4,8,4096]{2,1,0:T(8,128)}, f32[4,8,4096]{2,1,0:T(8,128)S(1)}, u32[]{:S(2)}) copy-start(f32[4,8,4096]{2,1,0:T(8,128)S(1)} %get-tuple-element.36.refs_2_) | copy-start | bytes 1572868
  18.6 5.8 %copy-start.11 = (f32[4,8,4096]{2,1,0:T(8,128)}, f32[4,8,4096]{2,1,0:T(8,128)S(1)}, u32[]{:S(2)}) copy-start(f32[4,8,4096]{2,1,0:T(8,128)S(1)} %get-tuple-element.34.refs_2_) | copy-start | bytes 1572868
  18.6 5.8 %copy-start.19 = (f32[4,8,4096]{2,1,0:T(8,128)}, f32[4,8,4096]{2,1,0:T(8,128)S(1)}, u32[]{:S(2)}) copy-start(f32[4,8,4096]{2,1,0:T(8,128)S(1)} %get-tuple-element.32.refs_0_) | copy-start | bytes 1572868
  26.8 19.8 %all-to-all-start = ((f32[8,13,8,128]{3,2,1,0:T(8,128)}), f32[8,13,8,128]{3,2,1,0:T(8,128)S(1)}, u32[]{:S(2)}, u32[]{:S(2)}) async-start(f32[8,13,8,128]{3,2,1,0:T(8,128)} %faces.1), calls=%async_computation | async-start | bytes 851968 | tf_op jit(solution)/shard_map/all_to_all | solution.py:519
  33.7 28.2 %collective-permute-start.1 = (f32[4,8,4096]{2,1,0:T(8,128)}, f32[4,8,4096]{2,1,0:T(8,128)}, u32[]{:S(2)}, u32[]{:S(2)}) collective-permute-start(f32[4,8,4096]{2,1,0:T(8,128)} %copy-done.4), channel_id=1, source_target_pairs={{0,24},{8,16},{16,8},{24,0},{1,25},{9,17},{17,9},{25,1},{2,26},{10... | collective-permute-start | bytes 1572872 | tf_op jit(solution)/shard_map/ppermute | solution.py:515
  34.9 30.6 %collective-permute-start.2 = (f32[4,8,4096]{2,1,0:T(8,128)}, f32[4,8,4096]{2,1,0:T(8,128)}, u32[]{:S(2)}, u32[]{:S(2)}) collective-permute-start(f32[4,8,4096]{2,1,0:T(8,128)} %copy-done.3), channel_id=1, source_target_pairs={{0,24},{8,16},{16,8},{24,0},{1,25},{9,17},{17,9},{25,1},{2,26},{10... | collective-permute-start | bytes 1572872 | tf_op jit(solution)/shard_map/ppermute | solution.py:515
  35.5 35.0 %collective-permute-start.3 = (f32[4,8,4096]{2,1,0:T(8,128)}, f32[4,8,4096]{2,1,0:T(8,128)}, u32[]{:S(2)}, u32[]{:S(2)}) collective-permute-start(f32[4,8,4096]{2,1,0:T(8,128)} %copy-done.2), channel_id=1, source_target_pairs={{0,24},{8,16},{16,8},{24,0},{1,25},{9,17},{17,9},{25,1},{2,26},{10... | collective-permute-start | bytes 1572872 | tf_op jit(solution)/shard_map/ppermute | solution.py:515
  36.6 45.1 %collective-permute-start.4 = (f32[4,8,4096]{2,1,0:T(8,128)S(1)}, f32[4,8,4096]{2,1,0:T(8,128)}, u32[]{:S(2)}, u32[]{:S(2)}) collective-permute-start(f32[4,8,4096]{2,1,0:T(8,128)S(1)} %get-tuple-element.39), channel_id=1, source_target_pairs={{0,24},{8,16},{16,8},{24,0},{1,25},{9,17},{17,9},{25,1},{2,26},{10... | collective-permute-start | bytes 1572872 | tf_op jit(solution)/shard_map/ppermute | solution.py:515
  46.6 1.6 %copy-start.1 = (f32[16,8,4096]{2,1,0:T(8,128)S(1)}, f32[16,8,4096]{2,1,0:T(8,128)}, u32[]{:S(2)}) copy-start(f32[16,8,4096]{2,1,0:T(8,128)} %prev_ref.1) | copy-start | bytes 6291460
  48.2 1.1 %copy-start.16 = (bf16[8,384,128]{2,1,0:T(8,128)(2,1)S(1)}, bf16[8,384,128]{2,1,0:T(8,128)(2,1)}, u32[]{:S(2)}) copy-start(bf16[8,384,128]{2,1,0:T(8,128)(2,1)} %copy-done.15) | copy-start | bytes 2359300
  49.4 1.1 %copy-start.18 = (bf16[8,384,128]{2,1,0:T(8,128)(2,1)S(1)}, bf16[8,384,128]{2,1,0:T(8,128)(2,1)}, u32[]{:S(2)}) copy-start(bf16[8,384,128]{2,1,0:T(8,128)(2,1)} %copy-done.17) | copy-start | bytes 2359300
  50.5 0.9 %copy-start.22 = (f32[8,48,64]{2,1,0:T(8,128)S(1)}, f32[8,48,64]{2,1,0:T(8,128)}, u32[]{:S(2)}) copy-start(f32[8,48,64]{2,1,0:T(8,128)} %copy-done.21) | copy-start | bytes 294916
  52.4 9.5 %copy-start.6 = (bf16[8,384,128]{2,1,0:T(8,128)(2,1)S(1)}, bf16[8,384,128]{2,1,0:T(8,128)(2,1)}, u32[]{:S(2)}) copy-start(bf16[8,384,128]{2,1,0:T(8,128)(2,1)} %copy-done.5) | copy-start | bytes 2359300
  52.4 9.5 %copy-start.14 = (bf16[8,64,192]{2,1,0:T(8,128)(2,1)S(1)}, bf16[8,64,192]{2,1,0:T(8,128)(2,1)}, u32[]{:S(2)}) copy-start(bf16[8,64,192]{2,1,0:T(8,128)(2,1)} %copy-done.13) | copy-start | bytes 589828
  52.4 9.5 %copy-start.20 = (f32[4,8,4096]{2,1,0:T(8,128)S(1)}, f32[4,8,4096]{2,1,0:T(8,128)}, u32[]{:S(2)}) copy-start(f32[4,8,4096]{2,1,0:T(8,128)} %copy-done.19) | copy-start | bytes 1572868
  61.9 3.6 %copy-start.12 = (f32[4,8,4096]{2,1,0:T(8,128)S(1)}, f32[4,8,4096]{2,1,0:T(8,128)}, u32[]{:S(2)}) copy-start(f32[4,8,4096]{2,1,0:T(8,128)} %copy-done.11) | copy-start | bytes 1572868
  65.5 5.0 %copy-start.10 = (f32[4,8,4096]{2,1,0:T(8,128)S(1)}, f32[4,8,4096]{2,1,0:T(8,128)}, u32[]{:S(2)}) copy-start(f32[4,8,4096]{2,1,0:T(8,128)} %copy-done.9) | copy-start | bytes 1572868
  70.5 11.2 %copy-start.8 = (f32[4,8,4096]{2,1,0:T(8,128)S(1)}, f32[4,8,4096]{2,1,0:T(8,128)}, u32[]{:S(2)}) copy-start(f32[4,8,4096]{2,1,0:T(8,128)} %copy-done.7) | copy-start | bytes 1572868
  (7 other events, 5.6 us)

commit v3 on v2

--- a/solution.py
+++ b/solution.py
@@ -31,10 +31,6 @@
     return high, (values - high.astype(jnp.float32)).astype(jnp.bfloat16)
 
 
-def halves(values):
-    return jnp.concatenate(split(values), 0)
-
-
 def dot(left, right):
     return jnp.dot(left, right, preferred_element_type=jnp.float32)
 
@@ -42,11 +38,6 @@
 def thrice(values):
     high, low = split(values)
     return jnp.concatenate([high, low, high], 1)
-
-
-def stacked(pair):
-    size = pair.shape[0] // 2
-    return jnp.concatenate([pair[:size], pair[:size], pair[size:]], 0)
 
 
 def cosines(wave, place, length):
@@ -74,15 +65,16 @@
     return jnp.where(row < 3, row, jnp.where(row < 6, extent + 2 - row, extent))
 
 
-def tables_kernel(boxes, w_ref, c_ref, ws_ref, cs_ref, ct_ref, rt_ref, sr_ref, sc_ref):
+def tables_kernel(boxes, faces, here, spot, w_ref, c_ref, ws_ref, cs_ref, ct_ref, rt_ref, sr_ref, sc_ref):
     side = w_ref.shape[1]
     spare = sr_ref.shape[1] // 6
 
-    def paired(wave_of, place_of, length):
-        shape = (2 * side, 2 * side)
-        row, col = iota(shape, 0), iota(shape, 1)
-        values = cosines(wave_of(row % side, col % side), place_of(row % side, col % side), length)
-        return jnp.where(row // side == col // side, values, 0.0)
+    def paired(values, left):
+        high, low = split(values)
+        return [
+            jnp.concatenate([jnp.where(left, part, 0), jnp.where(left, 0, part)], 0)
+            for part in (high, high, low)
+        ]
 
     def body(p, carry):
         rows, cols = boxes[p, 0], boxes[p, 1]
@@ -96,18 +88,17 @@
         row, col = iota(shape, 0), shuffle(iota(shape, 1), side)
         high, low = split(cosines(col, layer_place(row, rows), rows))
         ws_ref[p, side:] = jnp.concatenate([high, high, low], 1)
-        straight = paired(lambda r, c: r, lambda r, c: c, cols)
-        high, low = split(straight)
-        c_ref[p] = jnp.concatenate([high, high, low], 0)
-        cs_ref[p, :, : 2 * side] = jnp.concatenate([high, high, low], 0)
-        shape = (2 * side, 2 * side)
-        row, col = iota(shape, 0), iota(shape, 1)
-        values = cosines(row % side, layer_place(col % 8, cols), cols)
-        values = jnp.where((row // side == col // 8) & (col % 8 < 6), values, 0.0)
-        high, low = split(values)
-        cs_ref[p, :, 2 * side :] = jnp.concatenate([high, high, low], 0)
-        ct_ref[p] = stacked(halves(paired(lambda r, c: c, lambda r, c: r, cols)))
-        rt_ref[p] = stacked(halves(paired(lambda r, c: shuffle(c, side), lambda r, c: r, rows)))
+        shape = (side, 2 * side)
+        row, wide = iota(shape, 0), iota(shape, 1)
+        left, col = wide < side, wide % side
+        straight = jnp.concatenate(paired(cosines(row, col, cols), left), 0)
+        c_ref[p] = straight
+        cs_ref[p, :, : 2 * side] = straight
+        values = cosines(row, layer_place(wide % 8, cols), cols)
+        values = jnp.where((wide < 16) & (wide % 8 < 6), values, 0.0)
+        cs_ref[p, :, 2 * side :] = jnp.concatenate(paired(values, wide < 8), 0)
+        ct_ref[p] = jnp.concatenate(paired(cosines(col, row, cols), left), 0)
+        rt_ref[p] = jnp.concatenate(paired(cosines(shuffle(col, side), row, rows), left), 0)
         shape = (6 * spare, side)
         row, col = iota(shape, 0) // spare, iota(shape, 1)
         sr_ref[p] = cosines(shuffle(col, side), layer_place(row, rows), rows)
@@ -119,7 +110,7 @@
     lax.fori_loop(0, w_ref.shape[0], body, 0)
 
 
-def make_tables(boxes, side, spare):
+def make_tables(boxes, faces, here, spot, side, spare):
     holders = boxes.shape[0]
     shapes = [
         ((holders, side, 3 * side), jnp.bfloat16),
@@ -134,7 +125,7 @@
     return pl.pallas_call(
         tables_kernel,
         grid_spec=pltpu.PrefetchScalarGridSpec(
-            num_scalar_prefetch=1,
+            num_scalar_prefetch=4,
             grid=(1,),
             in_specs=[],
             out_specs=[whole(shape) for shape, _ in shapes],
@@ -143,64 +134,126 @@
         name="tables",
         compiler_params=ROOM,
         cost_estimate=pl.CostEstimate(flops=10**9, bytes_accessed=5 * 10**6, transcendentals=0),
-    )(boxes)
-
-
-def mix_kernel(total, chunks, spot, own_ref, other_ref, *refs):
+    )(boxes, faces, here, spot)
+
+
+def mix_kernel(total, spot, own_ref, other_ref, *refs):
     *out_refs, t_ref = refs
-    planes, holders, step = own_ref.shape
-    cols = 2 * planes * holders
+    planes, holders, _ = own_ref.shape
+    early = out_refs[0].shape[0]
+    shares = total // planes
+    count = planes * holders
     me = spot[0]
-    masks = [m for m in range(total // planes) if m & 1 == m // (total // planes // 2)]
+    masks = near_masks(shares)
 
     @pl.when(pl.program_id(0) == 0)
     def _():
         for k, mask in enumerate(masks):
-            shape = (planes * holders, cols)
-            row, col = iota(shape, 0), iota(shape, 1)
-            near = col < planes * holders
-            mode = jnp.where(near, me * planes, (me ^ 1) * planes - planes) + col // holders
-            place = (me ^ mask) * planes + row // holders
-            values = jnp.where(row % holders == col % holders, cosines(mode, place, total), 0.0)
-            t_ref[k * planes * holders : (k + 1) * planes * holders] = thrice(values)
-
-    x = jnp.concatenate(
-        [r[...].reshape(planes * holders, step) for r in (own_ref, other_ref)], 0
-    )
-    high, low = split(x)
-    mixed = dot(t_ref[...], jnp.concatenate([high, high, low], 0))
-    size = planes // chunks
-    for k, out_ref in enumerate(out_refs):
-        part = mixed[k * size * holders : (k + 1) * size * holders]
-        out_ref[...] = part.reshape(size, holders, step)
-
-
-def mix(spot, own, other, shares):
+            for odd in range(2):
+                shape = (count, count)
+                row, col = iota(shape, 0), iota(shape, 1)
+                slot = col // holders
+                half = planes // 2
+                where_from = jnp.where(slot < half, me * planes, (me ^ 1) * planes - planes)
+                mode = where_from + 2 * slot + odd
+                place = (me ^ mask) * planes + row // holders
+                values = cosines(mode, place, total)
+                values = jnp.where(row % holders == col % holders, values, 0.0)
+                t_ref[odd, k * count : (k + 1) * count] = thrice(values)
+
+    mixed = []
+    for odd in range(2):
+        picked = [r[z] for r in (own_ref, other_ref) for z in range(odd, planes, 2)]
+        high, low = split(jnp.concatenate(picked, 0))
+        mixed.append(dot(t_ref[odd], jnp.concatenate([high, high, low], 0)))
+    for k in range(len(masks)):
+        near, far = out_refs[4 * k : 4 * k + 2], out_refs[4 * k + 2 : 4 * k + 4]
+        for z in range(planes):
+            at = slice((k * planes + z) * holders, (k * planes + z + 1) * holders)
+            even, odd = mixed[0][at], mixed[1][at]
+            for refs, n, value in ((near, z, even + odd), (far, planes - 1 - z, even - odd)):
+                refs[n // early][n % early] = value
+
+
+def near_masks(shares):
+    top = shares // 2
+    return [m for m in range(top) if m & 1 == 0]
+
+
+def mix(spot, own, other, shares, front):
     planes, holders, cells = own.shape
-    chunks = planes // GROUP
-    count = max(1, shares // 2)
-    step = min(512, cells)
-    part = jax.ShapeDtypeStruct((GROUP, holders, cells), jnp.float32)
+    cells = cells - front
+    count = len(near_masks(shares))
+    step = math.gcd(front, cells)
+    sizes = [planes - GROUP, GROUP] * (2 * count)
     block = lambda i, s: (0, 0, i)
+    later = lambda i, s: (0, 0, i + front // step)
     outs = pl.pallas_call(
-        functools.partial(mix_kernel, shares * planes, chunks),
+        functools.partial(mix_kernel, shares * planes),
         grid_spec=pltpu.PrefetchScalarGridSpec(
             num_scalar_prefetch=1,
             grid=(cells // step,),
-            in_specs=[pl.BlockSpec((planes, holders, step), block)] * 2,
-            out_specs=[pl.BlockSpec((GROUP, holders, step), block)] * (count * chunks),
+            in_specs=[pl.BlockSpec((planes, holders, step), later)] * 2,
+            out_specs=[pl.BlockSpec((size, holders, step), block) for size in sizes],
             scratch_shapes=[
-                pltpu.VMEM((count * planes * holders, 6 * planes * holders), jnp.bfloat16)
+                pltpu.VMEM((2, count * planes * holders, 3 * planes * holders), jnp.bfloat16)
             ],
         ),
-        out_shape=[part] * (count * chunks),
+        out_shape=[jax.ShapeDtypeStruct((size, holders, cells), jnp.float32) for size in sizes],
         name="mix",
         compiler_params=ROOM,
         cost_estimate=pl.CostEstimate(
             flops=3 * 10**9, bytes_accessed=16 * planes * holders * cells, transcendentals=0
         ),
     )(spot, own, other)
-    return [list(outs[k * chunks : (k + 1) * chunks]) for k in range(count)]
+    return [list(outs[2 * k : 2 * k + 2]) for k in range(2 * count)]
+
+
+def gather_kernel(places, spot, *refs):
+    *in_refs, o_ref, t_ref = refs
+    planes, holders, step = o_ref.shape
+    count = planes * holders
+    total = planes * len(places)
+    me = spot[0]
+
+    @pl.when(pl.program_id(0) == 0)
+    def _():
+        for k, mask in enumerate(places):
+            shape = (count, count)
+            row, col = iota(shape, 0), iota(shape, 1)
+            values = cosines((me ^ mask) * planes + col // holders, me * planes + row // holders, total)
+            high, low = split(jnp.where(row % holders == col % holders, values, 0.0))
+            for n, part in enumerate((high, low, high)):
+                at = n * len(places) + k
+                t_ref[:, at * count : (at + 1) * count] = part
+
+    x = jnp.concatenate([ref[...].reshape(count, step) for ref in in_refs], 0)
+    high, low = split(x)
+    out = dot(t_ref[...], jnp.concatenate([high, high, low], 0))
+    o_ref[...] = out.reshape(planes, holders, step)
+
+
+def gather_mix(spot, fields, places, front):
+    planes, holders, _ = fields[0].shape
+    step = front // 2
+    spec = pl.BlockSpec((planes, holders, step), lambda i, s: (0, 0, i))
+    count = planes * holders
+    return pl.pallas_call(
+        functools.partial(gather_kernel, places),
+        grid_spec=pltpu.PrefetchScalarGridSpec(
+            num_scalar_prefetch=1,
+            grid=(front // step,),
+            in_specs=[spec] * len(fields),
+            out_specs=spec,
+            scratch_shapes=[pltpu.VMEM((count, 3 * len(places) * count), jnp.bfloat16)],
+        ),
+        out_shape=jax.ShapeDtypeStruct((planes, holders, front), jnp.float32),
+        name="gather",
+        compiler_params=ROOM,
+        cost_estimate=pl.CostEstimate(
+            flops=10**9, bytes_accessed=20 * planes * holders * front, transcendentals=0
+        ),
+    )(spot, *fields)
 
 
 def columns_of(planes, p, low, side):
@@ -268,7 +321,7 @@
     )(modes, weights, columns)
 
 
-def faces_kernel(table, s_ref, o_ref, count):
+def faces_kernel(table, place_ref, s_ref, o_ref, count):
     doms, tiles, spare, wide = o_ref.shape
     slots = (tiles - 1) // 3
     place = iota((spare, wide), 1) % (wide // 2)
@@ -281,7 +334,7 @@
         length = table[r, 3]
         part = jnp.minimum(table[r, 0], s_ref.shape[0] - 1)
         facing = jnp.minimum(table[r, 1], 3)
-        to = jnp.minimum(table[r, 4], doms - 1)
+        to = jnp.minimum(table[r, 4], doms - 1) ^ place_ref[0]
         seen = count[to]
         count[to] = seen + jnp.minimum(length, 1)
         slot = jnp.minimum(seen, slots - 1)
@@ -296,14 +349,14 @@
     lax.fori_loop(0, table.shape[0], body, 0, unroll=4)
 
 
-def find_faces(sides, table, doms):
+def find_faces(sides, table, here, doms):
     _, _, spare, wide = sides.shape
     slots = max(2, table.shape[0] // doms)
     shape = (doms, 3 * slots + 1, spare, wide)
     return pl.pallas_call(
         faces_kernel,
         grid_spec=pltpu.PrefetchScalarGridSpec(
-            num_scalar_prefetch=1,
+            num_scalar_prefetch=2,
             grid=(1,),
             in_specs=[whole(sides.shape)],
             out_specs=whole(shape),
@@ -313,15 +366,17 @@
         name="faces",
         compiler_params=ROOM,
         cost_estimate=pl.CostEstimate(flops=10**8, bytes_accessed=10**6, transcendentals=0),
-    )(table, sides)
+    )(table, here, sides)
 
 
 def force_kernel(
-    total, pairs, labels, spot, box_ref, r_ref, s_ref, ct_ref, rt_ref, sr_ref, sc_ref, now_ref,
-    prev_ref, o_ref, f_ref, m_ref, b_ref,
+    total, pairs, doms, *refs
 ):
+    labels, spot, refs = refs[:doms], refs[doms], refs[doms + 1 :]
+    box_ref, s_ref, ct_ref, rt_ref, sr_ref, sc_ref, now_ref, prev_ref, *r_refs = refs
+    *r_refs, o_ref, f_ref, m_ref, b_ref = r_refs
     group, holders, cells = now_ref.shape
-    doms, tiles, spare, wide = r_ref.shape
+    tiles, spare, wide = r_refs[0].shape
     side = wide // 2
     half = side // 2
     slots = (tiles - 1) // 3
@@ -332,25 +387,18 @@
         f_ref[...] = jnp.zeros_like(f_ref)
         place = iota((spare, wide), 1) % side
 
-        def gather(n, carry):
-            d, i = n // slots, n % slots
-            part = labels[n, 0]
-            facing = labels[n, 1]
-            start = labels[n, 2]
-            mask = (place >= start) & (place < start + labels[n, 3])
-            jumps = [
-                jnp.where(
-                    mask,
-                    pltpu.roll(r_ref[d, i * 3 + j], start, 1) - s_ref[part, facing * 3 + j],
-                    0.0,
-                )
-                for j in range(3)
-            ]
-            for i in range(3):
-                f_ref[part, facing * 3 + i] += sum(STENCIL[i + j] * jumps[j] for j in range(3 - i))
-            return carry
-
-        lax.fori_loop(0, doms * slots, gather, 0, unroll=4)
+        for d in range(doms):
+            for n in range(slots):
+                label = labels[d]
+                part, facing, start = label[n, 0], label[n, 1], label[n, 2]
+                mask = (place >= start) & (place < start + label[n, 3])
+                jumps = []
+                for j in range(3):
+                    moved = pltpu.roll(r_refs[d][n * 3 + j], start, 1)
+                    jumps.append(jnp.where(mask, moved - s_ref[part, facing * 3 + j], 0.0))
+                for i in range(3):
+                    push = sum(STENCIL[i + j] * jumps[j] for j in range(3 - i))
+                    f_ref[part, facing * 3 + i] += push
         shape = (6 * spare, wide)
         pair = iota(shape, 0) % spare
         left = iota(shape, 1) < side
@@ -419,18 +467,20 @@
 
 def advance(spot, boxes, received, sides, tables, modes_now, modes_prev, shares):
     planes, holders, cells = modes_now.shape
-    doms, tiles, spare, wide = received.shape
+    tiles, spare, wide = received[0].shape
     slots = (tiles - 1) // 3
-    labels = received[:, tiles - 1, :slots, :4].astype(jnp.int32).reshape(doms * slots, 4)
+    labels = [r[tiles - 1, :slots, :4].astype(jnp.int32) for r in received]
     pairs = planes // 2
-    operands = (boxes, received, sides, *tables)
+    operands = (boxes, sides, *tables)
     block = pl.BlockSpec((GROUP, holders, cells), lambda i, *_: (i, 0, 0))
     return pl.pallas_call(
-        functools.partial(force_kernel, float(shares * planes), pairs),
+        functools.partial(force_kernel, float(shares * planes), pairs, len(received)),
         grid_spec=pltpu.PrefetchScalarGridSpec(
-            num_scalar_prefetch=2,
+            num_scalar_prefetch=len(received) + 1,
             grid=(planes // GROUP,),
-            in_specs=[whole(o.shape) for o in operands] + [block, block],
+            in_specs=[whole(o.shape) for o in operands]
+            + [block, block]
+            + [whole(r.shape) for r in received],
             out_specs=block,
             scratch_shapes=[
                 pltpu.VMEM((holders, SIDES, spare, wide), jnp.float32),
@@ -444,7 +494,7 @@
         cost_estimate=pl.CostEstimate(
             flops=8 * 10**9, bytes_accessed=12 * planes * holders * cells, transcendentals=0
         ),
-    )(labels, spot, *operands, modes_now, modes_prev)
+    )(*labels, spot, *operands, modes_now, modes_prev, *received)
 
 
 def cells_kernel(w_ref, c_ref, *refs):
@@ -454,7 +504,11 @@
     half = side // 2
     wide = 2 * side
     low = iota((half, wide), 1) < side
-    planes = [sum(ref[z] for ref in part_refs).reshape(holders, half, wide) for z in range(group)]
+    first_ref, *part_refs = part_refs
+    planes = []
+    for z in range(group):
+        rest = sum(ref[z] for ref in part_refs)
+        planes.append(jnp.concatenate([first_ref[z], rest], 1).reshape(holders, half, wide))
     outs = [[] for _ in range(group)]
     for p in range(holders):
         v = dot(w_ref[p], columns_of(planes, p, low, side))
@@ -474,10 +528,14 @@
     cells_kernel(*refs)
 
 
-def to_cells(parts, weights, columns, chunk, planes, buffer):
-    group, holders, cells = parts[0].shape
-    operands = [weights, columns, *parts]
-    specs = [whole(o.shape) for o in operands]
+def to_cells(first, parts, weights, columns, chunk, buffer):
+    planes, holders, front = first.shape
+    size, _, rest = parts[0].shape
+    cells = rest + front
+    operands = [weights, columns, first, *parts]
+    specs = [whole(weights.shape), whole(columns.shape)]
+    specs.append(pl.BlockSpec((GROUP, holders, front), lambda i: (i + chunk, 0, 0)))
+    specs += [pl.BlockSpec((GROUP, holders, rest), lambda i: (i, 0, 0))] * len(parts)
     kernel, aliases = cells_kernel, {}
     if buffer is not None:
         operands = [buffer] + operands
@@ -485,15 +543,15 @@
         kernel, aliases = resumed_kernel, {0: 0}
     return pl.pallas_call(
         kernel,
-        grid=(1,),
+        grid=(size // GROUP,),
         in_specs=specs,
-        out_specs=pl.BlockSpec((group, holders, cells), lambda i: (chunk, 0, 0)),
+        out_specs=pl.BlockSpec((GROUP, holders, cells), lambda i: (i + chunk, 0, 0)),
         out_shape=jax.ShapeDtypeStruct((planes, holders, cells), jnp.float32),
         input_output_aliases=aliases,
         name="cells",
         compiler_params=ROOM,
         cost_estimate=pl.CostEstimate(
-            flops=2 * 10**9, bytes_accessed=12 * group * holders * cells, transcendentals=0
+            flops=10**8 * size * 5, bytes_accessed=12 * size * holders * cells, transcendentals=0
         ),
     )(*operands)
 
@@ -505,26 +563,38 @@
     doms = lax.axis_size("dom")
     spare = -(-planes // 16) * 8
     spot = lax.axis_index("height").astype(jnp.int32).reshape(1)
-    masks = [m for m in range(shares) if m & 1 == m // (shares // 2)]
-    swap = lambda mask: [(h, h ^ mask) for h in range(shares)]
-    other = lax.ppermute(modes_now, "height", swap(1))
-    w, c, ws, cs, *tables = make_tables(partition_boxes, side, spare)
-    parts = mix(spot, modes_now, other, shares)
-    sent = []
-    for m, part in zip(masks[1:], parts[1:]):
-        sent.append([lax.ppermute(x, "height", swap(m)) for x in part])
-    later, _ = lax.optimization_barrier((modes_now, parts[0][0]))
-    sides = find_sides(later, ws, cs, spare)
-    outgoing = find_faces(sides, face_table, doms)
-    received = lax.all_to_all(outgoing, "dom", split_axis=0, concat_axis=0, tiled=True)
+    here = lax.axis_index("dom").astype(jnp.int32).reshape(1)
+    swap = lambda size, mask: [(h, h ^ mask) for h in range(size)]
+    front = cells // 4
+    raw, whole_modes = lax.optimization_barrier((modes_now[:, :, :front], modes_now))
+    far = list(range(2, shares, 2))
+    arrived = [lax.ppermute(raw, "height", swap(shares, mask)) for mask in far]
+    other = lax.ppermute(whole_modes, "height", swap(shares, 1))
+    w, c, ws, cs, *tables = make_tables(partition_boxes, face_table, here, spot, side, spare)
+    parts = mix(spot, modes_now, other, shares, front)
+    kept, sent = parts[0], [[], []]
+    for k in range(2):
+        for m, part in enumerate(parts[1:], 1):
+            goal = near_masks(shares)[m // 2] ^ (shares - 1) * (m % 2)
+            sent[k].append(lax.ppermute(part[k], "height", swap(shares, goal)))
+    sides = find_sides(modes_now, ws, cs, spare)
+    *arrived, sides = lax.optimization_barrier((*arrived, sides))
+    passed = [lax.ppermute(x, "height", swap(shares, 1)) for x in arrived]
+    outgoing = find_faces(sides, face_table, here, doms)
+    received = [outgoing[0]]
+    for mask in range(1, doms):
+        received.append(lax.ppermute(outgoing[mask], "dom", swap(doms, mask)))
+    fields = [modes_now, other, *arrived, *passed]
+    places = [0, 1, *far, *(mask ^ 1 for mask in far)]
+    first = gather_mix(spot, fields, places, front)
     new_modes = advance(
         spot, partition_boxes, received, sides, tables, modes_now, modes_prev, shares
     )
     pressure = None
-    parts[0][0], new_modes = lax.optimization_barrier((parts[0][0], new_modes))
-    for k in range(planes // GROUP):
-        pieces = [parts[0][k]] + [group[k] for group in sent]
-        pressure = to_cells(pieces, w, c, k, planes, pressure)
+    kept[0], new_modes = lax.optimization_barrier((kept[0], new_modes))
+    for k in range(2):
+        chunk = k * (planes // GROUP - 1)
+        pressure = to_cells(first, [kept[k]] + sent[k], w, c, chunk, pressure)
     return (new_modes, pressure)
 
 

time: 85.8 us -> 74.8 us (0.87)
  local copies, waits for them, and re-layouts: 12 us -> 2.64 us
  Pallas kernels: 42.9 us -> 33.9 us
  starting transfers between devices: 11 us -> 16.9 us
  waiting for transfers between devices: 18.6 us -> 20.3 us
    ppermute x5 -> x12, starting transfers between devices: 4.05 us -> 16.9 us  [the longest x7 12.1 us: on_device(): received.append(lax.ppermute(outgoing[mask], 'dom', swap(doms, mask)))]
    ppermute x5 -> x12, waiting for transfers between devices: 9.15 us -> 20.3 us  [the longest x2 17.4 us: on_device(): sent[k].append(lax.ppermute(part[k], 'height', swap(shares, goal)))]
    unnamed x52 -> x6, local copies, waits for them, and re-layouts: 12 us -> 1.53 us
    all_to_all x1 -> x0, waiting for transfers between devices: 9.41 us -> none  [on_device(): lax.all_to_all(outgoing, 'dom', split_axis=0, concat_axis=0, tiled=True)]
    all_to_all x1 -> x0, starting transfers between devices: 6.9 us -> none  [on_device(): lax.all_to_all(outgoing, 'dom', split_axis=0, concat_axis=0, tiled=True)]
    pallas_call x5 -> x4, Pallas kernels: 20.6 us -> 13.9 us  [the longest x2 8.2 us: to_cells(): pl.pallas_call(kernel, grid=(size // GROUP,), in_specs=specs, out_specs=p...]
    slice x0 -> x1, local copies, waits for them, and re-layouts: none -> 1.08 us  [on_device(): modes_now[:, :, :front]]
    pallas_call x1, Pallas kernels: 4.67 us -> 3.71 us  [make_tables(): pl.pallas_call(tables_kernel, grid_spec=pltpu.PrefetchScalarGridSpec(num_...]
  transfers between devices with their start and end apart: 6 -> 12, of which waited for: 3 -> 5; matrix products, arithmetic and copies ran while one was open for 2% -> 2% of each run, Pallas kernels for 29% -> 42%
where the time goes in v3:
time: 74.8 us; the launch traced here: 74.5 us
  Pallas kernels  33.9 us (45%)
  waiting for transfers between devices  20.3 us (27%)
  starting transfers between devices  16.9 us (23%)
  local copies, waits for them, and re-layouts  2.64 us (4%)
  between operations  0.76 us (1%)
    ppermute x2, waiting for transfers between devices, on_device(): sent[k].append(lax.ppermute(part[k], 'height', swap(shares, goal)))  17.4 us
    ppermute x7, starting transfers between devices, on_device(): received.append(lax.ppermute(outgoing[mask], 'dom', swap(doms, mask)))  12.1 us
    pallas_call x1, Pallas kernels, advance(): pl.pallas_call(functools.partial(force_kernel, float(shares * planes), pa...  8.95 us
    pallas_call x2, Pallas kernels, to_cells(): pl.pallas_call(kernel, grid=(size // GROUP,), in_specs=specs, out_specs=p...  8.2 us
    pallas_call x1, Pallas kernels, find_sides(): pl.pallas_call(sides_kernel, grid=(planes // GROUP,), in_specs=[pl.BlockS...  5.69 us
    pallas_call x1, Pallas kernels, make_tables(): pl.pallas_call(tables_kernel, grid_spec=pltpu.PrefetchScalarGridSpec(num_...  3.71 us
    pallas_call x1, Pallas kernels, mix(): pl.pallas_call(functools.partial(mix_kernel, shares * planes), grid_spec=...  3.57 us
    ppermute x1, starting transfers between devices, on_device(): arrived = [lax.ppermute(raw, 'height', swap(shares, mask)) for mask in far]  3.03 us
  transfers between devices with their start and end apart: 12, of which 5 were waited for; matrix products, arithmetic and copies ran while one was open for 2% of the time, Pallas kernels for 42%

profile of v3, /device:TPU:0, one launch (start us, length us, event | category | flops | bytes accessed | tf_op | source)
XLA Modules:
  0.0 74.5 jit_solution(9084361179225424135)
XLA Ops:
  0.6 1.1 %slice.51 = f32[16,8,1024]{2,1,0:T(8,128)S(1)} slice(f32[16,8,4096]{2,1,0:T(8,128)} %refs_0_.1), slice={[0:16], [0:8], [0:1024]} | slice | bytes 1048576 | tf_op jit(solution)/shard_map/slice | solution.py:569
  1.7 3.0 %collective-permute-start.1 = (f32[16,8,1024]{2,1,0:T(8,128)S(1)}, f32[16,8,1024]{2,1,0:T(8,128)S(1)}, u32[]{:S(2)}, u32[]{:S(2)}) collective-permute-start(f32[16,8,1024]{2,1,0:T(8,128)S(1)} %slice.51), channel_id=1, source_target_pairs={{0,16},{8,24},{16,0},{24,8},{1,17},{9,25},{17,1},{25,9},{2,18},{10... | collective-permute-start | bytes 1572872 | tf_op jit(solution)/shard_map/ppermute | solution.py:571
  4.8 0.8 %copy.9.faces.table = s32[32,8]{1,0:T(8,128)S(1)} copy(s32[32,8]{0,1:T(8,128)} %param.7) | data formatting | bytes 2048 | tf_op args[3]
  5.5 0.8 %copy.7.boxes.refs_9_ = s32[8,2]{1,0:T(8,128)S(1)} copy(s32[8,2]{0,1:T(2,128)} %param.6) | data formatting | bytes 128 | tf_op args[2]
  6.3 3.7 %tables.1 = (bf16[8,64,192]{2,1,0:T(8,128)(2,1)S(1)}, bf16[8,384,128]{2,1,0:T(8,128)(2,1)S(1)}, bf16[8,80,192]{2,1,0:T(8,128)(2,1)S(1)}, bf16[8,384,256]{2,1,0:T...) custom-call(s32[8,2]{1,0:T(8,128)S(1)} %copy.7.boxes.refs_9_, ...), custom_call_target="tpu_custom_call" | custom-call | flops 1000000000 | bytes 5000000 | tf_op jit(solution)/shard_map/tables/pallas_call | solution.py:125
  10.0 5.7 %sides.1.s_ref.refs_10_ = f32[8,12,8,128]{3,2,1,0:T(8,128)S(1)} custom-call(f32[16,8,4096]{2,1,0:T(8,128)S(1)} %copy-done, bf16[8,80,192]{2,1,0:T(8,128)(2,1)S(1)} %get-tuple-element.23.w_ref, bf16[8,384,256]{2,1,0:T(8,128)(2,1)S(1)} %get-tuple-element.24.c_ref), custom_call_target="tpu_custom_call" | custom-call | flops 6000000000 | bytes 2097152 | tf_op jit(solution)/shard_map/sides/pallas_call | solution.py:306
  15.7 1.0 %collective-permute-done.1.refs_2_ = f32[16,8,1024]{2,1,0:T(8,128)S(1)} collective-permute-done((f32[16,8,1024]{2,1,0:T(8,128)S(1)}, f32[16,8,1024]{2,1,0:T(8,128)S(1)}, u32[]{:S(2)}, u32[]{:S(2)}) %collective-permute-start.1) | collective-permute-done | bytes 524320 | tf_op jit(solution)/shard_map/ppermute | solution.py:571
  16.7 1.6 %faces.2 = f32[8,13,8,128]{3,2,1,0:T(8,128)S(1)} custom-call(s32[32,8]{1,0:T(8,128)S(1)} %copy.9.faces.table, s32[1]{0:T(128)} %bitcast.1.here.place_ref, f32[8,12,8,128]{3,2,1,0:T(8,128)S(1)} %sides.1.s_ref.refs_10_), custom_call_target="tpu_custom_call" | custom-call | flops 100000000 | bytes 1000000 | tf_op jit(solution)/shard_map/faces/pallas_call | solution.py:356
  18.4 4.9 %collective-permute-start.8 = (f32[13,8,128]{2,1,0:T(8,128)S(1)}, f32[13,8,128]{2,1,0:T(8,128)S(1)}, u32[]{:S(2)}, u32[]{:S(2)}) collective-permute-start(f32[13,8,128]{2,1,0:T(8,128)S(1)} %get-tuple-element.38), channel_id=1, source_target_pairs={{0,7},{1,6},{2,5},{3,4},{4,3},{5,2},{6,1},{7,0},{8,15},{9,14},{10,... | collective-permute-start | bytes 159752 | tf_op jit(solution)/shard_map/ppermute | solution.py:586
  23.5 0.7 collective-permute-start.6
  24.2 2.0 %collective-permute-start.5 = (f32[13,8,128]{2,1,0:T(8,128)S(1)}, f32[13,8,128]{2,1,0:T(8,128)S(1)}, u32[]{:S(2)}, u32[]{:S(2)}) collective-permute-start(f32[13,8,128]{2,1,0:T(8,128)S(1)} %get-tuple-element.41), channel_id=1, source_target_pairs={{0,4},{1,5},{2,6},{3,7},{4,0},{5,1},{6,2},{7,3},{8,12},{9,13},{10,... | collective-permute-start | bytes 159752 | tf_op jit(solution)/shard_map/ppermute | solution.py:586
  26.2 2.4 %collective-permute-start.4 = (f32[13,8,128]{2,1,0:T(8,128)S(1)}, f32[13,8,128]{2,1,0:T(8,128)S(1)}, u32[]{:S(2)}, u32[]{:S(2)}) collective-permute-start(f32[13,8,128]{2,1,0:T(8,128)S(1)} %get-tuple-element.42), channel_id=1, source_target_pairs={{0,3},{1,2},{2,1},{3,0},{4,7},{5,6},{6,5},{7,4},{8,11},{9,10},{10,... | collective-permute-start | bytes 159752 | tf_op jit(solution)/shard_map/ppermute | solution.py:586
  28.6 0.9 %collective-permute-done.7.refs_23_ = f32[13,8,128]{2,1,0:T(8,128)S(1)} collective-permute-done((f32[13,8,128]{2,1,0:T(8,128)S(1)}, f32[13,8,128]{2,1,0:T(8,128)S(1)}, u32[]{:S(2)}, u32[]{:S(2)}) %collective-permute-start.7) | collective-permute-done | bytes 53280 | tf_op jit(solution)/shard_map/ppermute | solution.py:586
  29.5 0.7 %collective-permute-start.3 = (f32[13,8,128]{2,1,0:T(8,128)S(1)}, f32[13,8,128]{2,1,0:T(8,128)S(1)}, u32[]{:S(2)}, u32[]{:S(2)}) collective-permute-start(f32[13,8,128]{2,1,0:T(8,128)S(1)} %get-tuple-element.43), channel_id=1, source_target_pairs={{0,2},{1,3},{2,0},{3,1},{4,6},{5,7},{6,4},{7,5},{8,10},{9,11},{10,... | collective-permute-start | bytes 159752 | tf_op jit(solution)/shard_map/ppermute | solution.py:586
  30.2 1.0 %collective-permute-done.6.refs_22_ = f32[13,8,128]{2,1,0:T(8,128)S(1)} collective-permute-done((f32[13,8,128]{2,1,0:T(8,128)S(1)}, f32[13,8,128]{2,1,0:T(8,128)S(1)}, u32[]{:S(2)}, u32[]{:S(2)}) %collective-permute-start.6) | collective-permute-done | bytes 53280 | tf_op jit(solution)/shard_map/ppermute | solution.py:586
  31.3 1.1 %collective-permute-start.2 = (f32[13,8,128]{2,1,0:T(8,128)S(1)}, f32[13,8,128]{2,1,0:T(8,128)S(1)}, u32[]{:S(2)}, u32[]{:S(2)}) collective-permute-start(f32[13,8,128]{2,1,0:T(8,128)S(1)} %get-tuple-element.44), channel_id=1, source_target_pairs={{0,1},{1,0},{2,3},{3,2},{4,5},{5,4},{6,7},{7,6},{8,9},{9,8},{10,11... | collective-permute-start | bytes 159752 | tf_op jit(solution)/shard_map/ppermute | solution.py:586
  32.4 3.6 %mix.1 = (f32[12,8,3072]{2,1,0:T(8,128)S(1)}, f32[4,8,3072]{2,1,0:T(8,128)S(1)}, f32[12,8,3072]{2,1,0:T(8,128)S(1)}, f32[4,8,3072]{2,1,0:T(8,128)S(1)}) custom-call(s32[1]{0:T(128)} %bitcast.spot.refs_8_, f32[16,8,4096]{2,1,0:T(8,128)S(1)} %copy-done, f32[16,8,4096]{2,1,0:T(8,128)} %collective-permute-done.other_ref.refs_1_), custom_call_target="tpu_custom_call" | custom-call | flops 3000000000 | bytes 6291456 | tf_op jit(solution)/shard_map/mix/pallas_call | solution.py:191
  36.0 1.3 %collective-permute-start.10 = (f32[12,8,3072]{2,1,0:T(8,128)S(1)}, f32[12,8,3072]{2,1,0:T(8,128)S(1)}, u32[]{:S(2)}, u32[]{:S(2)}) collective-permute-start(f32[12,8,3072]{2,1,0:T(8,128)S(1)} %get-tuple-element.35), channel_id=1, source_target_pairs={{0,24},{8,16},{16,8},{24,0},{1,25},{9,17},{17,9},{25,1},{2,26},{10... | collective-permute-start | bytes 3538952 | tf_op jit(solution)/shard_map/ppermute | solution.py:579
  37.3 9.0 %force.1 = f32[16,8,4096]{2,1,0:T(8,128)} custom-call(s32[4,4]{1,0:T(4,128)S(1)} %fusion.7.refs_0_, s32[4,4]{1,0:T(4,128)S(1)} %fusion.6.refs_1_, s32[4,4]{1,0:T(4,128)S(1)} %fusion.5.refs_2_, s32[4,4]{1,0:T(4,128)S(1)} %fusion.4.refs_3_, s32[4,4]{1,0:T(4,128)S(1)} %fusion.3.refs_4_, s32[4,4]{1,0:T(4,128)S(1)} %fusion.2.refs_5_, s32[4,4]{1,0:T(4,128)S(1)} %fusion.1.refs_6_, ...), custom_call_target="tpu_custom_call" | custom-call | flops 8000000000 | bytes 6291456 | tf_op jit(solution)/shard_map/force/pallas_call | solution.py:476
  46.8 2.1 %gather.1.refs_0_.refs_2_ = f32[16,8,1024]{2,1,0:T(8,128)S(1)} custom-call(s32[1]{0:T(128)} %bitcast.spot.refs_8_, f32[16,8,4096]{2,1,0:T(8,128)S(1)} %copy-done, f32[16,8,4096]{2,1,0:T(8,128)} %collective-permute-done.other_ref.refs_1_, f32[16,8,1024]{2,1,0:T(8,128)S(1)} %collective-permute-done.1.refs_2_, f32[16,8,1024]{2,1,0:T(8,128)S(1)} %collective-permute-done.9.refs_3_), custom_call_target="tpu_custom_call" | custom-call | flops 1000000000 | bytes 2621440 | tf_op jit(solution)/shard_map/gather/pallas_call | solution.py:241
  48.9 14.7 %collective-permute-done.10.refs_2_ = f32[12,8,3072]{2,1,0:T(8,128)S(1)} collective-permute-done((f32[12,8,3072]{2,1,0:T(8,128)S(1)}, f32[12,8,3072]{2,1,0:T(8,128)S(1)}, u32[]{:S(2)}, u32[]{:S(2)}) %collective-permute-start.10) | collective-permute-done | bytes 1179680 | tf_op jit(solution)/shard_map/ppermute | solution.py:579
  63.7 5.8 %cells.2.buffer_ref = f32[16,8,4096]{2,1,0:T(8,128)} custom-call(bf16[8,64,192]{2,1,0:T(8,128)(2,1)S(1)} %get-tuple-element.31.w_ref.refs_0_, bf16[8,384,128]{2,1,0:T(8,128)(2,1)S(1)} %get-tuple-element.32.c_ref.refs_1_, f32[16,8,1024]{2,1,0:T(8,128)S(1)} %gather.1.refs_0_.refs_2_, f32[12,8,3072]{2,1,0:T(8,128)S(1)} %get-tuple-element.34.refs_1_, ...), custom_call_target="tpu_custom_call" | custom-call | flops 6000000000 | bytes 4718592 | tf_op jit(solution)/shard_map/cells/pallas_call | solution.py:544
  69.4 2.7 %collective-permute-done.11.refs_4_ = f32[4,8,3072]{2,1,0:T(8,128)S(1)} collective-permute-done((f32[4,8,3072]{2,1,0:T(8,128)S(1)}, f32[4,8,3072]{2,1,0:T(8,128)S(1)}, u32[]{:S(2)}, u32[]{:S(2)}) %collective-permute-start.11) | collective-permute-done | bytes 393248 | tf_op jit(solution)/shard_map/ppermute | solution.py:579
  72.1 2.4 %cells.3 = f32[16,8,4096]{2,1,0:T(8,128)} custom-call(f32[16,8,4096]{2,1,0:T(8,128)} %cells.2.buffer_ref, bf16[8,64,192]{2,1,0:T(8,128)(2,1)S(1)} %get-tuple-element.31.w_ref.refs_0_, bf16[8,384,128]{2,1,0:T(8,128)(2,1)S(1)} %get-tuple-element.32.c_ref.refs_1_, f32[16,8,1024]{2,1,0:T(8,128)S(1)} %gather.1.refs_0_.refs_2_, ...), custom_call_target="tpu_custom_call", output_to_operand_aliasing={{}: (0, {})} | custom-call | flops 2000000000 | bytes 1572864 | tf_op jit(solution)/shard_map/cells/pallas_call | solution.py:544
  (24 shorter events, 0.9 us)
Async XLA Ops:
  1.7 8.3 %copy-start = (f32[16,8,4096]{2,1,0:T(8,128)S(1)}, f32[16,8,4096]{2,1,0:T(8,128)}, u32[]{:S(2)}) copy-start(f32[16,8,4096]{2,1,0:T(8,128)} %refs_0_.1) | copy-start | bytes 6291460
  1.7 15.0 %collective-permute-start.1 = (f32[16,8,1024]{2,1,0:T(8,128)S(1)}, f32[16,8,1024]{2,1,0:T(8,128)S(1)}, u32[]{:S(2)}, u32[]{:S(2)}) collective-permute-start(f32[16,8,1024]{2,1,0:T(8,128)S(1)} %slice.51), channel_id=1, source_target_pairs={{0,16},{8,24},{16,0},{24,8},{1,17},{9,25},{17,1},{25,9},{2,18},{10... | collective-permute-start | bytes 1572872 | tf_op jit(solution)/shard_map/ppermute | solution.py:571
  4.8 27.7 %collective-permute-start = (f32[16,8,4096]{2,1,0:T(8,128)}, f32[16,8,4096]{2,1,0:T(8,128)}, u32[]{:S(2)}, u32[]{:S(2)}) collective-permute-start(f32[16,8,4096]{2,1,0:T(8,128)} %refs_0_.1), channel_id=1, source_target_pairs={{0,8},{8,0},{16,24},{24,16},{1,9},{9,1},{17,25},{25,17},{2,10},{10... | collective-permute-start | bytes 6291464 | tf_op jit(solution)/shard_map/ppermute | solution.py:572
  18.4 7.9 %collective-permute-start.8 = (f32[13,8,128]{2,1,0:T(8,128)S(1)}, f32[13,8,128]{2,1,0:T(8,128)S(1)}, u32[]{:S(2)}, u32[]{:S(2)}) collective-permute-start(f32[13,8,128]{2,1,0:T(8,128)S(1)} %get-tuple-element.38), channel_id=1, source_target_pairs={{0,7},{1,6},{2,5},{3,4},{4,3},{5,2},{6,1},{7,0},{8,15},{9,14},{10,... | collective-permute-start | bytes 159752 | tf_op jit(solution)/shard_map/ppermute | solution.py:586
  23.2 6.2 %collective-permute-start.7 = (f32[13,8,128]{2,1,0:T(8,128)S(1)}, f32[13,8,128]{2,1,0:T(8,128)S(1)}, u32[]{:S(2)}, u32[]{:S(2)}) collective-permute-start(f32[13,8,128]{2,1,0:T(8,128)S(1)} %get-tuple-element.39), channel_id=1, source_target_pairs={{0,6},{1,7},{2,4},{3,5},{4,2},{5,3},{6,0},{7,1},{8,14},{9,15},{10,... | collective-permute-start | bytes 159752 | tf_op jit(solution)/shard_map/ppermute | solution.py:586
  23.5 7.8 %collective-permute-start.6 = (f32[13,8,128]{2,1,0:T(8,128)S(1)}, f32[13,8,128]{2,1,0:T(8,128)S(1)}, u32[]{:S(2)}, u32[]{:S(2)}) collective-permute-start(f32[13,8,128]{2,1,0:T(8,128)S(1)} %get-tuple-element.40), channel_id=1, source_target_pairs={{0,5},{1,4},{2,7},{3,6},{4,1},{5,0},{6,3},{7,2},{8,13},{9,12},{10,... | collective-permute-start | bytes 159752 | tf_op jit(solution)/shard_map/ppermute | solution.py:586
  24.2 8.2 %collective-permute-start.5 = (f32[13,8,128]{2,1,0:T(8,128)S(1)}, f32[13,8,128]{2,1,0:T(8,128)S(1)}, u32[]{:S(2)}, u32[]{:S(2)}) collective-permute-start(f32[13,8,128]{2,1,0:T(8,128)S(1)} %get-tuple-element.41), channel_id=1, source_target_pairs={{0,4},{1,5},{2,6},{3,7},{4,0},{5,1},{6,2},{7,3},{8,12},{9,13},{10,... | collective-permute-start | bytes 159752 | tf_op jit(solution)/shard_map/ppermute | solution.py:586
  26.2 6.1 %collective-permute-start.4 = (f32[13,8,128]{2,1,0:T(8,128)S(1)}, f32[13,8,128]{2,1,0:T(8,128)S(1)}, u32[]{:S(2)}, u32[]{:S(2)}) collective-permute-start(f32[13,8,128]{2,1,0:T(8,128)S(1)} %get-tuple-element.42), channel_id=1, source_target_pairs={{0,3},{1,2},{2,1},{3,0},{4,7},{5,6},{6,5},{7,4},{8,11},{9,10},{10,... | collective-permute-start | bytes 159752 | tf_op jit(solution)/shard_map/ppermute | solution.py:586
  29.5 7.8 %collective-permute-start.3 = (f32[13,8,128]{2,1,0:T(8,128)S(1)}, f32[13,8,128]{2,1,0:T(8,128)S(1)}, u32[]{:S(2)}, u32[]{:S(2)}) collective-permute-start(f32[13,8,128]{2,1,0:T(8,128)S(1)} %get-tuple-element.43), channel_id=1, source_target_pairs={{0,2},{1,3},{2,0},{3,1},{4,6},{5,7},{6,4},{7,5},{8,10},{9,11},{10,... | collective-permute-start | bytes 159752 | tf_op jit(solution)/shard_map/ppermute | solution.py:586
  31.3 6.0 %collective-permute-start.2 = (f32[13,8,128]{2,1,0:T(8,128)S(1)}, f32[13,8,128]{2,1,0:T(8,128)S(1)}, u32[]{:S(2)}, u32[]{:S(2)}) collective-permute-start(f32[13,8,128]{2,1,0:T(8,128)S(1)} %get-tuple-element.44), channel_id=1, source_target_pairs={{0,1},{1,0},{2,3},{3,2},{4,5},{5,4},{6,7},{7,6},{8,9},{9,8},{10,11... | collective-permute-start | bytes 159752 | tf_op jit(solution)/shard_map/ppermute | solution.py:586
  32.4 14.4 %collective-permute-start.9 = (f32[16,8,1024]{2,1,0:T(8,128)S(1)}, f32[16,8,1024]{2,1,0:T(8,128)S(1)}, u32[]{:S(2)}, u32[]{:S(2)}) collective-permute-start(f32[16,8,1024]{2,1,0:T(8,128)S(1)} %collective-permute-done.1.refs_2_), channel_id=1, source_target_pairs={{0,8},{8,0},{16,24},{24,16},{1,9},{9,1},{17,25},{25,17},{2,10},{10... | collective-permute-start | bytes 1572872 | tf_op jit(solution)/shard_map/ppermute | solution.py:582
  32.4 4.9 %copy-start.1 = (f32[16,8,4096]{2,1,0:T(8,128)S(1)}, f32[16,8,4096]{2,1,0:T(8,128)}, u32[]{:S(2)}) copy-start(f32[16,8,4096]{2,1,0:T(8,128)} %refs_16_.1) | copy-start | bytes 6291460
  36.0 27.7 %collective-permute-start.10 = (f32[12,8,3072]{2,1,0:T(8,128)S(1)}, f32[12,8,3072]{2,1,0:T(8,128)S(1)}, u32[]{:S(2)}, u32[]{:S(2)}) collective-permute-start(f32[12,8,3072]{2,1,0:T(8,128)S(1)} %get-tuple-element.35), channel_id=1, source_target_pairs={{0,24},{8,16},{16,8},{24,0},{1,25},{9,17},{17,9},{25,1},{2,26},{10... | collective-permute-start | bytes 3538952 | tf_op jit(solution)/shard_map/ppermute | solution.py:579
  46.3 25.8 %collective-permute-start.11 = (f32[4,8,3072]{2,1,0:T(8,128)S(1)}, f32[4,8,3072]{2,1,0:T(8,128)S(1)}, u32[]{:S(2)}, u32[]{:S(2)}) collective-permute-start(f32[4,8,3072]{2,1,0:T(8,128)S(1)} %get-tuple-element.37), channel_id=1, source_target_pairs={{0,24},{8,16},{16,8},{24,0},{1,25},{9,17},{17,9},{25,1},{2,26},{10... | collective-permute-start | bytes 1179656 | tf_op jit(solution)/shard_map/ppermute | solution.py:579

commit v4 on v3

--- a/solution.py
+++ b/solution.py
@@ -12,7 +12,7 @@
 COUPLING = 32.0
 STENCIL = (COUPLING * 270.0 / 180.0, COUPLING * -27.0 / 180.0, COUPLING * 2.0 / 180.0)
 TIME_STEP = 0.4
-SERIES = (1.0, -1.0 / 6, 1.0 / 120, -1.0 / 5040, 1.0 / 362880, -1.0 / 39916800, 1.0 / 6227020800)
+SERIES = (1.0, -1.0 / 6, 1.0 / 120, -1.0 / 5040, 1.0 / 362880, -1.0 / 39916800)
 GROUP = 4
 SIDES = 12
 ROOM = pltpu.CompilerParams(vmem_limit_bytes=24 * 2**20)
@@ -209,51 +209,113 @@
     return [list(outs[2 * k : 2 * k + 2]) for k in range(2 * count)]
 
 
-def gather_kernel(places, spot, *refs):
-    *in_refs, o_ref, t_ref = refs
-    planes, holders, step = o_ref.shape
+def exchange_kernel(total, places, box_ref, out_ref, now_ref, prev_ref, *refs):
+    field_refs = refs[: len(places)]
+    r_ref, first_ref, kept_ref, gain_ref, land_ref, t_ref, send_sem, recv_sem = refs[len(places) :]
+    doms = out_ref.shape[0]
+    planes, holders, cells = now_ref.shape
+    front = first_ref.shape[2]
+    here = lax.axis_index("dom")
+    me = lax.axis_index("height")
     count = planes * holders
-    total = planes * len(places)
-    me = spot[0]
-
-    @pl.when(pl.program_id(0) == 0)
-    def _():
-        for k, mask in enumerate(places):
-            shape = (count, count)
-            row, col = iota(shape, 0), iota(shape, 1)
-            values = cosines((me ^ mask) * planes + col // holders, me * planes + row // holders, total)
-            high, low = split(jnp.where(row % holders == col % holders, values, 0.0))
-            for n, part in enumerate((high, low, high)):
-                at = n * len(places) + k
-                t_ref[:, at * count : (at + 1) * count] = part
-
-    x = jnp.concatenate([ref[...].reshape(count, step) for ref in in_refs], 0)
-    high, low = split(x)
-    out = dot(t_ref[...], jnp.concatenate([high, high, low], 0))
-    o_ref[...] = out.reshape(planes, holders, step)
-
-
-def gather_mix(spot, fields, places, front):
-    planes, holders, _ = fields[0].shape
-    step = front // 2
-    spec = pl.BlockSpec((planes, holders, step), lambda i, s: (0, 0, i))
+
+    barrier = pltpu.get_barrier_semaphore()
+    for m in range(1, doms):
+        goal = {"dom": lax.rem(here + m, doms)}
+        pl.semaphore_signal(barrier, inc=1, device_id=goal, device_id_type=pl.DeviceIdType.MESH)
+    for k, mask in enumerate(places):
+        shape = (count, count)
+        row, col = iota(shape, 0), iota(shape, 1)
+        values = cosines((me ^ mask) * planes + col // holders, me * planes + row // holders, total)
+        high, low = split(jnp.where(row % holders == col % holders, values, 0.0))
+        for n, part in enumerate((high, low, high)):
+            at = n * len(places) + k
+            t_ref[:, at * count : (at + 1) * count] = part
+    pl.semaphore_wait(barrier, doms - 1)
+    copies = []
+    for m in range(1, doms):
+        copy = pltpu.make_async_remote_copy(
+            src_ref=out_ref.at[m],
+            dst_ref=land_ref.at[m],
+            send_sem=send_sem.at[m],
+            recv_sem=recv_sem.at[m],
+            device_id={"dom": lax.rem(here + m, doms)},
+            device_id_type=pl.DeviceIdType.MESH,
+        )
+        copy.start()
+        copies.append(copy)
+    r_ref[0] = out_ref[0]
+
+    step = front // 4
+    for n in range(4):
+        at = slice(n * step, (n + 1) * step)
+        x = jnp.concatenate([ref[:, :, at].reshape(count, step) for ref in field_refs], 0)
+        high, low = split(x)
+        mixed = dot(t_ref[...], jnp.concatenate([high, high, low], 0))
+        first_ref[:, :, at] = mixed.reshape(planes, holders, step)
+
+    scale = (math.pi * TIME_STEP / 2) ** 2
+    side = math.isqrt(cells)
+    cell = iota((holders, cells), 1)
+    wave_row, wave_col = cell // side, cell % side
+    extent_row, extent_col = box_ref[:, 0:1], box_ref[:, 1:2]
+    ratio_row = wave_row.astype(jnp.float32) / extent_row.astype(jnp.float32)
+    ratio_col = wave_col.astype(jnp.float32) / extent_col.astype(jnp.float32)
+    inside = (wave_row < extent_row) & (wave_col < extent_col)
+    base = scale * (ratio_row * ratio_row + ratio_col * ratio_col)
+    gain_ref[0] = jnp.where(inside, base, -1.0)
+    kept_ref[0] = jnp.where(inside, base, -1.0)
+
+    def pace(n, carry):
+        z = planes - 1 - n
+        base = gain_ref[0]
+        depth = (me * planes + z).astype(jnp.float32) / total
+        quarter = base + scale * (depth * depth)
+        ratio = jnp.float32(SERIES[-1])
+        for coefficient in SERIES[-2::-1]:
+            ratio = ratio * quarter + coefficient
+        ratio = ratio * ratio
+        kept = (2.0 - 4.0 * quarter * ratio) * now_ref[z] - prev_ref[z]
+        kept_ref[z] = jnp.where(base >= 0.0, kept, 0.0)
+        gain_ref[z] = jnp.where(base >= 0.0, (TIME_STEP * TIME_STEP) * ratio, 0.0)
+        return carry
+
+    lax.fori_loop(0, planes, pace, 0)
+    for copy in copies:
+        copy.wait_recv()
+    for m in range(1, doms):
+        r_ref[m] = land_ref[m]
+    for copy in copies:
+        copy.wait_send()
+
+
+def exchange(boxes, outgoing, now, prev, fields, places, front, shares):
+    planes, holders, _ = now.shape
     count = planes * holders
+    doms = outgoing.shape[0]
+    field = pl.BlockSpec((planes, holders, front), lambda i: (0, 0, 0))
+    like = lambda shape: jax.ShapeDtypeStruct(shape, jnp.float32)
+    outs = [outgoing.shape, (planes, holders, front), now.shape, now.shape]
     return pl.pallas_call(
-        functools.partial(gather_kernel, places),
-        grid_spec=pltpu.PrefetchScalarGridSpec(
-            num_scalar_prefetch=1,
-            grid=(front // step,),
-            in_specs=[spec] * len(fields),
-            out_specs=spec,
-            scratch_shapes=[pltpu.VMEM((count, 3 * len(places) * count), jnp.bfloat16)],
-        ),
-        out_shape=jax.ShapeDtypeStruct((planes, holders, front), jnp.float32),
-        name="gather",
-        compiler_params=ROOM,
+        functools.partial(exchange_kernel, shares * planes, places),
+        grid=(1,),
+        in_specs=[whole(o.shape) for o in (boxes, outgoing, now, prev)] + [field] * len(fields),
+        out_specs=[whole(shape) for shape in outs],
+        out_shape=[like(shape) for shape in outs],
+        scratch_shapes=[
+            pltpu.VMEM(outgoing.shape, jnp.float32),
+            pltpu.VMEM((count, 3 * len(places) * count), jnp.bfloat16),
+            pltpu.SemaphoreType.DMA((doms,)),
+            pltpu.SemaphoreType.DMA((doms,)),
+        ],
+        name="exchange",
+        compiler_params=pltpu.CompilerParams(
+            vmem_limit_bytes=24 * 2**20, collective_id=0, has_side_effects=True
+        ),
         cost_estimate=pl.CostEstimate(
-            flops=10**9, bytes_accessed=20 * planes * holders * front, transcendentals=0
-        ),
-    )(spot, *fields)
+            flops=10**10, bytes_accessed=20 * planes * holders * front, transcendentals=0
+        ),
+    )(boxes, outgoing, now, prev, *fields)
 
 
 def columns_of(planes, p, low, side):
@@ -334,7 +396,8 @@
         length = table[r, 3]
         part = jnp.minimum(table[r, 0], s_ref.shape[0] - 1)
         facing = jnp.minimum(table[r, 1], 3)
-        to = jnp.minimum(table[r, 4], doms - 1) ^ place_ref[0]
+        to = jnp.minimum(table[r, 4], doms - 1) - place_ref[0]
+        to = jnp.where(to < 0, to + doms, to)
         seen = count[to]
         count[to] = seen + jnp.minimum(length, 1)
         slot = jnp.minimum(seen, slots - 1)
@@ -370,17 +433,14 @@
 
 
 def force_kernel(
-    total, pairs, doms, *refs
+    pairs, labels, r_ref, s_ref, ct_ref, rt_ref, sr_ref, sc_ref, kept_ref, gain_ref, o_ref, f_ref,
+    m_ref,
 ):
-    labels, spot, refs = refs[:doms], refs[doms], refs[doms + 1 :]
-    box_ref, s_ref, ct_ref, rt_ref, sr_ref, sc_ref, now_ref, prev_ref, *r_refs = refs
-    *r_refs, o_ref, f_ref, m_ref, b_ref = r_refs
-    group, holders, cells = now_ref.shape
-    tiles, spare, wide = r_refs[0].shape
+    group, holders, cells = kept_ref.shape
+    doms, tiles, spare, wide = r_ref.shape
     side = wide // 2
     half = side // 2
     slots = (tiles - 1) // 3
-    scale = (math.pi * TIME_STEP / 2) ** 2
 
     @pl.when(pl.program_id(0) == 0)
     def _():
@@ -389,12 +449,12 @@
 
         for d in range(doms):
             for n in range(slots):
-                label = labels[d]
-                part, facing, start = label[n, 0], label[n, 1], label[n, 2]
-                mask = (place >= start) & (place < start + label[n, 3])
+                at = d * slots + n
+                part, facing, start = labels[at, 0], labels[at, 1], labels[at, 2]
+                mask = (place >= start) & (place < start + labels[at, 3])
                 jumps = []
                 for j in range(3):
-                    moved = pltpu.roll(r_refs[d][n * 3 + j], start, 1)
+                    moved = pltpu.roll(r_ref[d, n * 3 + j], start, 1)
                     jumps.append(jnp.where(mask, moved - s_ref[part, facing * 3 + j], 0.0))
                 for i in range(3):
                     push = sum(STENCIL[i + j] * jumps[j] for j in range(3 - i))
@@ -412,15 +472,15 @@
             sc = sc_ref[p]
             sc_left = jnp.where(left, sc, 0.0)
             sc_right = jnp.where(left, 0.0, sc)
-            far = jnp.concatenate(
-                [
-                    jnp.concatenate([jnp.where(pair == k, t, 0.0) for t in (fc, sc_left, sc_right)], 0)
-                    for k in range(pairs)
-                ],
-                1,
+            highs, lows = zip(*(split(t) for t in (fc, sc_left, sc_right)))
+            masks = [jnp.where(pair == k, 1.0, 0.0).astype(jnp.bfloat16) for k in range(pairs)]
+            far_high, far_low = (
+                jnp.concatenate(
+                    [jnp.concatenate([t * mask for t in parts], 0) for mask in masks], 1
+                )
+                for parts in (highs, lows)
             )
             near_high, near_low = split(near)
-            far_high, far_low = split(far)
             out = lax.dot_general(
                 jnp.concatenate([near_high, near_low, near_high], 0),
                 jnp.concatenate([far_high, far_high, far_low], 0),
@@ -432,13 +492,6 @@
             return carry
 
         lax.fori_loop(0, holders, spread, 0)
-        cell = iota((holders, cells), 1)
-        wave_row, wave_col = cell // side, cell % side
-        extent_row, extent_col = box_ref[:, 0:1], box_ref[:, 1:2]
-        ratio_row = wave_row.astype(jnp.float32) / extent_row.astype(jnp.float32)
-        ratio_col = wave_col.astype(jnp.float32) / extent_col.astype(jnp.float32)
-        inside = (wave_row < extent_row) & (wave_col < extent_col)
-        b_ref[...] = jnp.where(inside, scale * (ratio_row * ratio_row + ratio_col * ratio_col), -1.0)
 
     low = iota((half, wide), 1) < side
     for k in range(group // 2):
@@ -449,52 +502,36 @@
         for c in range(2):
             z = 2 * k + c
             force = jnp.stack([out[c] for out in outs], 0).reshape(holders, cells)
-            depth = (spot[0] * 2 * pairs + pl.program_id(0) * group + z).astype(jnp.float32)
-            depth = depth / total
-            base = b_ref[...]
-            quarter = base + scale * (depth * depth)
-            ratio = jnp.float32(SERIES[-1])
-            for coefficient in SERIES[-2::-1]:
-                ratio = ratio * quarter + coefficient
-            ratio = ratio * ratio
-            updated = (
-                (2.0 - 4.0 * quarter * ratio) * now_ref[z]
-                - prev_ref[z]
-                + (TIME_STEP * TIME_STEP) * ratio * force
-            )
-            o_ref[z] = jnp.where(base >= 0.0, updated, 0.0)
-
-
-def advance(spot, boxes, received, sides, tables, modes_now, modes_prev, shares):
-    planes, holders, cells = modes_now.shape
-    tiles, spare, wide = received[0].shape
+            o_ref[z] = kept_ref[z] + gain_ref[z] * force
+
+
+def advance(received, sides, tables, kept, gain):
+    planes, holders, cells = kept.shape
+    doms, tiles, spare, wide = received.shape
     slots = (tiles - 1) // 3
-    labels = [r[tiles - 1, :slots, :4].astype(jnp.int32) for r in received]
+    labels = received[:, tiles - 1, :slots, :4].astype(jnp.int32).reshape(doms * slots, 4)
     pairs = planes // 2
-    operands = (boxes, sides, *tables)
+    operands = (received, sides, *tables)
     block = pl.BlockSpec((GROUP, holders, cells), lambda i, *_: (i, 0, 0))
     return pl.pallas_call(
-        functools.partial(force_kernel, float(shares * planes), pairs, len(received)),
+        functools.partial(force_kernel, pairs),
         grid_spec=pltpu.PrefetchScalarGridSpec(
-            num_scalar_prefetch=len(received) + 1,
+            num_scalar_prefetch=1,
             grid=(planes // GROUP,),
-            in_specs=[whole(o.shape) for o in operands]
-            + [block, block]
-            + [whole(r.shape) for r in received],
+            in_specs=[whole(o.shape) for o in operands] + [block, block],
             out_specs=block,
             scratch_shapes=[
                 pltpu.VMEM((holders, SIDES, spare, wide), jnp.float32),
                 pltpu.VMEM((pairs, holders, wide // 2, wide), jnp.float32),
-                pltpu.VMEM((holders, cells), jnp.float32),
             ],
         ),
-        out_shape=jax.ShapeDtypeStruct(modes_now.shape, jnp.float32),
+        out_shape=jax.ShapeDtypeStruct(kept.shape, jnp.float32),
         name="force",
         compiler_params=ROOM,
         cost_estimate=pl.CostEstimate(
             flops=8 * 10**9, bytes_accessed=12 * planes * holders * cells, transcendentals=0
         ),
-    )(*labels, spot, *operands, modes_now, modes_prev, *received)
+    )(labels, *operands, kept, gain)
 
 
 def cells_kernel(w_ref, c_ref, *refs):
@@ -581,15 +618,12 @@
     *arrived, sides = lax.optimization_barrier((*arrived, sides))
     passed = [lax.ppermute(x, "height", swap(shares, 1)) for x in arrived]
     outgoing = find_faces(sides, face_table, here, doms)
-    received = [outgoing[0]]
-    for mask in range(1, doms):
-        received.append(lax.ppermute(outgoing[mask], "dom", swap(doms, mask)))
     fields = [modes_now, other, *arrived, *passed]
     places = [0, 1, *far, *(mask ^ 1 for mask in far)]
-    first = gather_mix(spot, fields, places, front)
-    new_modes = advance(
-        spot, partition_boxes, received, sides, tables, modes_now, modes_prev, shares
+    received, first, steady, gain = exchange(
+        partition_boxes, outgoing, modes_now, modes_prev, fields, places, front, shares
     )
+    new_modes = advance(received, sides, tables, steady, gain)
     pressure = None
     kept[0], new_modes = lax.optimization_barrier((kept[0], new_modes))
     for k in range(2):

time: 74.8 us -> 61.7 us (0.82)
  starting transfers between devices: 16.9 us -> 5.05 us
  waiting for transfers between devices: 20.3 us -> 9.6 us
  Pallas kernels: 33.9 us -> 43.4 us
    ppermute x7 -> x0, starting transfers between devices: 12.1 us -> none  [on_device(): received.append(lax.ppermute(outgoing[mask], 'dom', swap(doms, mask)))]
    pallas_call x2, Pallas kernels: 11.1 us -> 20.6 us  [the longest x1 12.8 us: exchange(): pl.pallas_call(functools.partial(exchange_kernel, shares * planes, places...]
    ppermute x2, waiting for transfers between devices: 17.4 us -> 8.01 us  [on_device(): sent[k].append(lax.ppermute(part[k], 'height', swap(shares, goal)))]
    ppermute x7 -> x0, waiting for transfers between devices: 1.93 us -> none  [on_device(): received.append(lax.ppermute(outgoing[mask], 'dom', swap(doms, mask)))]
  transfers between devices with their start and end apart: 12 -> 5, of which waited for: 5 -> 3; matrix products, arithmetic and copies ran while one was open for 2% -> 2% of each run, Pallas kernels for 42% -> 67%
where the time goes in v4:
time: 61.7 us; the launch traced here: 61.4 us
  Pallas kernels  43.4 us (70%)
  waiting for transfers between devices  9.6 us (16%)
  starting transfers between devices  5.05 us (8%)
  local copies, waits for them, and re-layouts  2.61 us (4%)
  between operations  0.71 us (1%)
    pallas_call x1, Pallas kernels, exchange(): pl.pallas_call(functools.partial(exchange_kernel, shares * planes, places...  12.8 us
    pallas_call x2, Pallas kernels, to_cells(): pl.pallas_call(kernel, grid=(size // GROUP,), in_specs=specs, out_specs=p...  8.17 us
    ppermute x2, waiting for transfers between devices, on_device(): sent[k].append(lax.ppermute(part[k], 'height', swap(shares, goal)))  8.01 us
    pallas_call x1, Pallas kernels, advance(): pl.pallas_call(functools.partial(force_kernel, pairs), grid_spec=pltpu.Pr...  7.79 us
    pallas_call x1, Pallas kernels, find_sides(): pl.pallas_call(sides_kernel, grid=(planes // GROUP,), in_specs=[pl.BlockS...  5.69 us
    pallas_call x1, Pallas kernels, make_tables(): pl.pallas_call(tables_kernel, grid_spec=pltpu.PrefetchScalarGridSpec(num_...  3.71 us
    pallas_call x1, Pallas kernels, mix(): pl.pallas_call(functools.partial(mix_kernel, shares * planes), grid_spec=...  3.57 us
    ppermute x1, starting transfers between devices, on_device(): arrived = [lax.ppermute(raw, 'height', swap(shares, mask)) for mask in far]  2.55 us
  transfers between devices with their start and end apart: 5, of which 3 were waited for; matrix products, arithmetic and copies ran while one was open for 2% of the time, Pallas kernels for 67%

profile of v4, /device:TPU:0, one launch (start us, length us, event | category | flops | bytes accessed | tf_op | source)
XLA Modules:
  0.0 61.4 jit_solution(2816118651562765153)
XLA Ops:
  0.6 1.1 %slice.6 = f32[16,8,1024]{2,1,0:T(8,128)S(1)} slice(f32[16,8,4096]{2,1,0:T(8,128)} %refs_0_.1), slice={[0:16], [0:8], [0:1024]} | slice | bytes 1048576 | tf_op jit(solution)/shard_map/slice | solution.py:606
  1.7 0.0 copy-start
  1.7 0.6 collective-permute-start
  2.3 2.6 %collective-permute-start.1 = (f32[16,8,1024]{2,1,0:T(8,128)S(1)}, f32[16,8,1024]{2,1,0:T(8,128)S(1)}, u32[]{:S(2)}, u32[]{:S(2)}) collective-permute-start(f32[16,8,1024]{2,1,0:T(8,128)S(1)} %slice.6), channel_id=1, source_target_pairs={{0,16},{8,24},{16,0},{24,8},{1,17},{9,25},{17,1},{25,9},{2,18},{10... | collective-permute-start | bytes 1572872 | tf_op jit(solution)/shard_map/ppermute | solution.py:608
  4.8 0.8 %copy.21.faces.table = s32[32,8]{1,0:T(8,128)S(1)} copy(s32[32,8]{0,1:T(8,128)} %param.7) | data formatting | bytes 2048 | tf_op args[3]
  5.6 0.8 %copy.22.boxes.box_ref = s32[8,2]{1,0:T(8,128)S(1)} copy(s32[8,2]{0,1:T(2,128)} %param.6) | data formatting | bytes 128 | tf_op args[2]
  6.4 3.7 %tables.1 = (bf16[8,64,192]{2,1,0:T(8,128)(2,1)S(1)}, bf16[8,384,128]{2,1,0:T(8,128)(2,1)S(1)}, bf16[8,80,192]{2,1,0:T(8,128)(2,1)S(1)}, bf16[8,384,256]{2,1,0:T...) custom-call(s32[8,2]{1,0:T(8,128)S(1)} %copy.22.boxes.box_ref, ...), custom_call_target="tpu_custom_call" | custom-call | flops 1000000000 | bytes 5000000 | tf_op jit(solution)/shard_map/tables/pallas_call | solution.py:125
  10.1 5.7 %sides.1.s_ref = f32[8,12,8,128]{3,2,1,0:T(8,128)S(1)} custom-call(f32[16,8,4096]{2,1,0:T(8,128)S(1)} %copy-done, bf16[8,80,192]{2,1,0:T(8,128)(2,1)S(1)} %get-tuple-element.27.w_ref, bf16[8,384,256]{2,1,0:T(8,128)(2,1)S(1)} %get-tuple-element.28.c_ref), custom_call_target="tpu_custom_call" | custom-call | flops 6000000000 | bytes 2097152 | tf_op jit(solution)/shard_map/sides/pallas_call | solution.py:368
  15.8 1.6 %collective-permute-done.1.refs_2_ = f32[16,8,1024]{2,1,0:T(8,128)S(1)} collective-permute-done((f32[16,8,1024]{2,1,0:T(8,128)S(1)}, f32[16,8,1024]{2,1,0:T(8,128)S(1)}, u32[]{:S(2)}, u32[]{:S(2)}) %collective-permute-start.1) | collective-permute-done | bytes 524320 | tf_op jit(solution)/shard_map/ppermute | solution.py:608
  17.4 0.0 collective-permute-start.2
  17.4 1.6 %faces.2.out_ref = f32[8,13,8,128]{3,2,1,0:T(8,128)S(1)} custom-call(s32[32,8]{1,0:T(8,128)S(1)} %copy.21.faces.table, s32[1]{0:T(128)} %bitcast.1.here.place_ref, f32[8,12,8,128]{3,2,1,0:T(8,128)S(1)} %sides.1.s_ref), custom_call_target="tpu_custom_call" | custom-call | flops 100000000 | bytes 1000000 | tf_op jit(solution)/shard_map/faces/pallas_call | solution.py:419
  19.0 0.0 copy-start.1
  19.0 0.0 collective-permute-done.other_ref.refs_1_
  19.0 3.6 %mix.1 = (f32[12,8,3072]{2,1,0:T(8,128)S(1)}, f32[4,8,3072]{2,1,0:T(8,128)S(1)}, f32[12,8,3072]{2,1,0:T(8,128)S(1)}, f32[4,8,3072]{2,1,0:T(8,128)S(1)}) custom-call(s32[1]{0:T(128)} %bitcast.spot, f32[16,8,4096]{2,1,0:T(8,128)S(1)} %copy-done, f32[16,8,4096]{2,1,0:T(8,128)} %collective-permute-done.other_ref.refs_1_), custom_call_target="tpu_custom_call" | custom-call | flops 3000000000 | bytes 6291456 | tf_op jit(solution)/shard_map/mix/pallas_call | solution.py:191
  22.6 1.9 %collective-permute-start.3 = (f32[12,8,3072]{2,1,0:T(8,128)S(1)}, f32[12,8,3072]{2,1,0:T(8,128)S(1)}, u32[]{:S(2)}, u32[]{:S(2)}) collective-permute-start(f32[12,8,3072]{2,1,0:T(8,128)S(1)} %get-tuple-element.43), channel_id=1, source_target_pairs={{0,24},{8,16},{16,8},{24,0},{1,25},{9,17},{17,9},{25,1},{2,26},{10... | collective-permute-start | bytes 3538952 | tf_op jit(solution)/shard_map/ppermute | solution.py:616
  24.5 0.0 collective-permute-done.2.refs_3_
  24.5 0.0 copy-done.1
  24.5 12.8 %exchange.1 = (f32[8,13,8,128]{3,2,1,0:T(8,128)S(1)}, f32[16,8,1024]{2,1,0:T(8,128)S(1)}, f32[16,8,4096]{2,1,0:T(8,128)S(1)}, f32[16,8,4096]{2,1,0:T(8,128)S(1)}) custom-call(s32[8,2]{1,0:T(8,128)S(1)} %copy.22.boxes.box_ref, f32[8,13,8,128]{3,2,1,0:T(8,128)S(1)} %faces.2.out_ref, f32[16,8,4096]{2,1,0:T(8,128)S(1)} %copy-done, f32[16,8,4096]{2,1,0:T(8,128)S(1)} %copy-done.1, ...), custom_call_target="tpu_custom_call" | custom-call | flops 10000000000 | bytes 2621440 | tf_op jit(solution)/shard_map/exchange/pallas_call | solution.py:299
  37.4 7.8 %force.1 = f32[16,8,4096]{2,1,0:T(8,128)} custom-call(s32[32,4]{1,0:T(8,128)S(1)} %bitcast.3, f32[8,13,8,128]{3,2,1,0:T(8,128)S(1)} %get-tuple-element.31.r_ref, f32[8,12,8,128]{3,2,1,0:T(8,128)S(1)} %sides.1.s_ref, bf16[8,384,128]{2,1,0:T(8,128)(2,1)S(1)} %get-tuple-element.32.ct_ref, bf16[8,384,128]{2,1,0:T(8,128)(2,1)S(1)} %get-tuple-element.33.rt_ref, ...), custom_call_target="tpu_custom_call" | custom-call | flops 8000000000 | bytes 6291456 | tf_op jit(solution)/shard_map/force/pallas_call | solution.py:516
  45.2 0.0 collective-permute-start.4
  45.2 5.7 %collective-permute-done.3.refs_2_ = f32[12,8,3072]{2,1,0:T(8,128)S(1)} collective-permute-done((f32[12,8,3072]{2,1,0:T(8,128)S(1)}, f32[12,8,3072]{2,1,0:T(8,128)S(1)}, u32[]{:S(2)}, u32[]{:S(2)}) %collective-permute-start.3) | collective-permute-done | bytes 1179680 | tf_op jit(solution)/shard_map/ppermute | solution.py:616
  50.9 5.7 %cells.2.buffer_ref = f32[16,8,4096]{2,1,0:T(8,128)} custom-call(bf16[8,64,192]{2,1,0:T(8,128)(2,1)S(1)} %get-tuple-element.39.w_ref.refs_0_, bf16[8,384,128]{2,1,0:T(8,128)(2,1)S(1)} %get-tuple-element.40.c_ref.refs_1_, f32[16,8,1024]{2,1,0:T(8,128)S(1)} %get-tuple-element.41.refs_0_.refs_2_, f32[12,8,3072]{2,1,0:T(8,128)S(1)} %get-tuple-element.42.refs_1_, ...), custom_call_target="tpu_custom_call" | custom-call | flops 6000000000 | bytes 4718592 | tf_op jit(solution)/shard_map/cells/pallas_call | solution.py:581
  56.6 2.3 %collective-permute-done.4.refs_4_ = f32[4,8,3072]{2,1,0:T(8,128)S(1)} collective-permute-done((f32[4,8,3072]{2,1,0:T(8,128)S(1)}, f32[4,8,3072]{2,1,0:T(8,128)S(1)}, u32[]{:S(2)}, u32[]{:S(2)}) %collective-permute-start.4) | collective-permute-done | bytes 393248 | tf_op jit(solution)/shard_map/ppermute | solution.py:616
  58.9 2.4 %cells.3 = f32[16,8,4096]{2,1,0:T(8,128)} custom-call(f32[16,8,4096]{2,1,0:T(8,128)} %cells.2.buffer_ref, bf16[8,64,192]{2,1,0:T(8,128)(2,1)S(1)} %get-tuple-element.39.w_ref.refs_0_, bf16[8,384,128]{2,1,0:T(8,128)(2,1)S(1)} %get-tuple-element.40.c_ref.refs_1_, f32[16,8,1024]{2,1,0:T(8,128)S(1)} %get-tuple-element.41.refs_0_.refs_2_, ...), custom_call_target="tpu_custom_call", output_to_operand_aliasing={{}: (0, {})} | custom-call | flops 2000000000 | bytes 1572864 | tf_op jit(solution)/shard_map/cells/pallas_call | solution.py:581
  (2 shorter events, 0.0 us)
Async XLA Ops:
  1.7 8.4 %copy-start = (f32[16,8,4096]{2,1,0:T(8,128)S(1)}, f32[16,8,4096]{2,1,0:T(8,128)}, u32[]{:S(2)}) copy-start(f32[16,8,4096]{2,1,0:T(8,128)} %refs_0_.1) | copy-start | bytes 6291460
  1.7 17.3 %collective-permute-start = (f32[16,8,4096]{2,1,0:T(8,128)}, f32[16,8,4096]{2,1,0:T(8,128)}, u32[]{:S(2)}, u32[]{:S(2)}) collective-permute-start(f32[16,8,4096]{2,1,0:T(8,128)} %refs_0_.1), channel_id=1, source_target_pairs={{0,8},{8,0},{16,24},{24,16},{1,9},{9,1},{17,25},{25,17},{2,10},{10... | collective-permute-start | bytes 6291464 | tf_op jit(solution)/shard_map/ppermute | solution.py:609
  2.3 15.1 %collective-permute-start.1 = (f32[16,8,1024]{2,1,0:T(8,128)S(1)}, f32[16,8,1024]{2,1,0:T(8,128)S(1)}, u32[]{:S(2)}, u32[]{:S(2)}) collective-permute-start(f32[16,8,1024]{2,1,0:T(8,128)S(1)} %slice.6), channel_id=1, source_target_pairs={{0,16},{8,24},{16,0},{24,8},{1,17},{9,25},{17,1},{25,9},{2,18},{10... | collective-permute-start | bytes 1572872 | tf_op jit(solution)/shard_map/ppermute | solution.py:608
  17.4 7.2 %collective-permute-start.2 = (f32[16,8,1024]{2,1,0:T(8,128)S(1)}, f32[16,8,1024]{2,1,0:T(8,128)S(1)}, u32[]{:S(2)}, u32[]{:S(2)}) collective-permute-start(f32[16,8,1024]{2,1,0:T(8,128)S(1)} %collective-permute-done.1.refs_2_), channel_id=1, source_target_pairs={{0,8},{8,0},{16,24},{24,16},{1,9},{9,1},{17,25},{25,17},{2,10},{10... | collective-permute-start | bytes 1572872 | tf_op jit(solution)/shard_map/ppermute | solution.py:619
  19.0 5.5 %copy-start.1 = (f32[16,8,4096]{2,1,0:T(8,128)S(1)}, f32[16,8,4096]{2,1,0:T(8,128)}, u32[]{:S(2)}) copy-start(f32[16,8,4096]{2,1,0:T(8,128)} %prev_ref.1) | copy-start | bytes 6291460
  22.6 28.3 %collective-permute-start.3 = (f32[12,8,3072]{2,1,0:T(8,128)S(1)}, f32[12,8,3072]{2,1,0:T(8,128)S(1)}, u32[]{:S(2)}, u32[]{:S(2)}) collective-permute-start(f32[12,8,3072]{2,1,0:T(8,128)S(1)} %get-tuple-element.43), channel_id=1, source_target_pairs={{0,24},{8,16},{16,8},{24,0},{1,25},{9,17},{17,9},{25,1},{2,26},{10... | collective-permute-start | bytes 3538952 | tf_op jit(solution)/shard_map/ppermute | solution.py:616
  45.2 13.8 %collective-permute-start.4 = (f32[4,8,3072]{2,1,0:T(8,128)S(1)}, f32[4,8,3072]{2,1,0:T(8,128)S(1)}, u32[]{:S(2)}, u32[]{:S(2)}) collective-permute-start(f32[4,8,3072]{2,1,0:T(8,128)S(1)} %get-tuple-element.45), channel_id=1, source_target_pairs={{0,24},{8,16},{16,8},{24,0},{1,25},{9,17},{17,9},{25,1},{2,26},{10... | collective-permute-start | bytes 1179656 | tf_op jit(solution)/shard_map/ppermute | solution.py:616

commit v5 on v4

--- a/solution.py
+++ b/solution.py
@@ -65,19 +65,36 @@
     return jnp.where(row < 3, row, jnp.where(row < 6, extent + 2 - row, extent))
 
 
-def tables_kernel(boxes, faces, here, spot, w_ref, c_ref, ws_ref, cs_ref, ct_ref, rt_ref, sr_ref, sc_ref):
+def paired(values, left):
+    high, low = split(values)
+    return [
+        jnp.concatenate([jnp.where(left, part, 0), jnp.where(left, 0, part)], 0)
+        for part in (high, high, low)
+    ]
+
+
+def force_tables(p, boxes, ct_ref, rt_ref, sr_ref, sc_ref):
+    rows, cols = boxes[0, p], boxes[1, p]
+    side = sr_ref.shape[2]
+    spare = sr_ref.shape[1] // 6
+    shape = (side, 2 * side)
+    row, wide = iota(shape, 0), iota(shape, 1)
+    left, col = wide < side, wide % side
+    ct_ref[p] = jnp.concatenate(paired(cosines(col, row, cols), left), 0)
+    rt_ref[p] = jnp.concatenate(paired(cosines(shuffle(col, side), row, rows), left), 0)
+    shape = (6 * spare, side)
+    row, col = iota(shape, 0) // spare, iota(shape, 1)
+    sr_ref[p] = cosines(shuffle(col, side), layer_place(row, rows), rows)
+    shape = (6 * spare, 2 * side)
+    row, col = iota(shape, 0) // spare, iota(shape, 1)
+    sc_ref[p] = cosines(col % side, layer_place(row, cols), cols)
+
+
+def tables_kernel(boxes, faces, here, spot, w_ref, c_ref, ws_ref, cs_ref):
     side = w_ref.shape[1]
-    spare = sr_ref.shape[1] // 6
-
-    def paired(values, left):
-        high, low = split(values)
-        return [
-            jnp.concatenate([jnp.where(left, part, 0), jnp.where(left, 0, part)], 0)
-            for part in (high, high, low)
-        ]
 
     def body(p, carry):
-        rows, cols = boxes[p, 0], boxes[p, 1]
+        rows, cols = boxes[0, p], boxes[1, p]
         shape = (side, side)
         row, col = iota(shape, 0), shuffle(iota(shape, 1), side)
         high, low = split(cosines(col, shuffle(row, side), rows))
@@ -97,30 +114,18 @@
         values = cosines(row, layer_place(wide % 8, cols), cols)
         values = jnp.where((wide < 16) & (wide % 8 < 6), values, 0.0)
         cs_ref[p, :, 2 * side :] = jnp.concatenate(paired(values, wide < 8), 0)
-        ct_ref[p] = jnp.concatenate(paired(cosines(col, row, cols), left), 0)
-        rt_ref[p] = jnp.concatenate(paired(cosines(shuffle(col, side), row, rows), left), 0)
-        shape = (6 * spare, side)
-        row, col = iota(shape, 0) // spare, iota(shape, 1)
-        sr_ref[p] = cosines(shuffle(col, side), layer_place(row, rows), rows)
-        shape = (6 * spare, 2 * side)
-        row, col = iota(shape, 0) // spare, iota(shape, 1)
-        sc_ref[p] = cosines(col % side, layer_place(row, cols), cols)
         return carry
 
     lax.fori_loop(0, w_ref.shape[0], body, 0)
 
 
-def make_tables(boxes, faces, here, spot, side, spare):
-    holders = boxes.shape[0]
+def make_tables(boxes, faces, here, spot, side):
+    holders = boxes.shape[1]
     shapes = [
         ((holders, side, 3 * side), jnp.bfloat16),
         ((holders, 6 * side, 2 * side), jnp.bfloat16),
         ((holders, side + 16, 3 * side), jnp.bfloat16),
         ((holders, 6 * side, 4 * side), jnp.bfloat16),
-        ((holders, 6 * side, 2 * side), jnp.bfloat16),
-        ((holders, 6 * side, 2 * side), jnp.bfloat16),
-        ((holders, 6 * spare, side), jnp.float32),
-        ((holders, 6 * spare, 2 * side), jnp.float32),
     ]
     return pl.pallas_call(
         tables_kernel,
@@ -209,9 +214,10 @@
     return [list(outs[2 * k : 2 * k + 2]) for k in range(2 * count)]
 
 
-def exchange_kernel(total, places, box_ref, out_ref, now_ref, prev_ref, *refs):
+def exchange_kernel(total, places, boxes, out_ref, now_ref, prev_ref, *refs):
     field_refs = refs[: len(places)]
-    r_ref, first_ref, kept_ref, gain_ref, land_ref, t_ref, send_sem, recv_sem = refs[len(places) :]
+    r_ref, first_ref, kept_ref, gain_ref, *table_refs = refs[len(places) :]
+    *table_refs, land_ref, t_ref, send_sem, recv_sem = table_refs
     doms = out_ref.shape[0]
     planes, holders, cells = now_ref.shape
     front = first_ref.shape[2]
@@ -258,7 +264,12 @@
     side = math.isqrt(cells)
     cell = iota((holders, cells), 1)
     wave_row, wave_col = cell // side, cell % side
-    extent_row, extent_col = box_ref[:, 0:1], box_ref[:, 1:2]
+    holder = iota((holders, 1), 0)
+    extent_row = jnp.zeros((holders, 1), jnp.int32)
+    extent_col = jnp.zeros((holders, 1), jnp.int32)
+    for p in range(holders):
+        extent_row = jnp.where(holder == p, boxes[0, p], extent_row)
+        extent_col = jnp.where(holder == p, boxes[1, p], extent_col)
     ratio_row = wave_row.astype(jnp.float32) / extent_row.astype(jnp.float32)
     ratio_col = wave_col.astype(jnp.float32) / extent_col.astype(jnp.float32)
     inside = (wave_row < extent_row) & (wave_col < extent_col)
@@ -281,6 +292,12 @@
         return carry
 
     lax.fori_loop(0, planes, pace, 0)
+
+    def table(p, carry):
+        force_tables(p, boxes, *table_refs)
+        return carry
+
+    lax.fori_loop(0, holders, table, 0)
     for copy in copies:
         copy.wait_recv()
     for m in range(1, doms):
@@ -294,14 +311,19 @@
     count = planes * holders
     doms = outgoing.shape[0]
     field = pl.BlockSpec((planes, holders, front), lambda i: (0, 0, 0))
-    like = lambda shape: jax.ShapeDtypeStruct(shape, jnp.float32)
+    side, spare = outgoing.shape[3] // 2, outgoing.shape[2]
     outs = [outgoing.shape, (planes, holders, front), now.shape, now.shape]
+    outs = [(shape, jnp.float32) for shape in outs]
+    outs += [((holders, 6 * side, 2 * side), jnp.bfloat16)] * 2
+    outs += [((holders, 6 * spare, n * side), jnp.float32) for n in (1, 2)]
     return pl.pallas_call(
         functools.partial(exchange_kernel, shares * planes, places),
         grid=(1,),
-        in_specs=[whole(o.shape) for o in (boxes, outgoing, now, prev)] + [field] * len(fields),
-        out_specs=[whole(shape) for shape in outs],
-        out_shape=[like(shape) for shape in outs],
+        in_specs=[pl.BlockSpec(memory_space=pltpu.SMEM)]
+        + [whole(o.shape) for o in (outgoing, now, prev)]
+        + [field] * len(fields),
+        out_specs=[whole(shape) for shape, _ in outs],
+        out_shape=[jax.ShapeDtypeStruct(*out) for out in outs],
         scratch_shapes=[
             pltpu.VMEM(outgoing.shape, jnp.float32),
             pltpu.VMEM((count, 3 * len(places) * count), jnp.bfloat16),
@@ -393,28 +415,28 @@
         count[d] = 0
 
     def body(r, carry):
-        length = table[r, 3]
-        part = jnp.minimum(table[r, 0], s_ref.shape[0] - 1)
-        facing = jnp.minimum(table[r, 1], 3)
-        to = jnp.minimum(table[r, 4], doms - 1) - place_ref[0]
+        length = table[3, r]
+        part = jnp.minimum(table[0, r], s_ref.shape[0] - 1)
+        facing = jnp.minimum(table[1, r], 3)
+        to = jnp.minimum(table[4, r], doms - 1) - place_ref[0]
         to = jnp.where(to < 0, to + doms, to)
         seen = count[to]
         count[to] = seen + jnp.minimum(length, 1)
         slot = jnp.minimum(seen, slots - 1)
         for j in range(3):
-            moved = pltpu.roll(s_ref[part, facing * 3 + j], wide - table[r, 2], 1)
+            moved = pltpu.roll(s_ref[part, facing * 3 + j], wide - table[2, r], 1)
             o_ref[to, slot * 3 + j] += jnp.where(place < length, moved, 0.0)
-        label = jnp.where(lane == 0, table[r, 5], jnp.where(lane == 1, table[r, 6], table[r, 7]))
+        label = jnp.where(lane == 0, table[5, r], jnp.where(lane == 1, table[6, r], table[7, r]))
         label = jnp.where(lane == 3, length, label) * jnp.minimum(length, 1)
         o_ref[to, tiles - 1, pl.ds(slot, 1), :] += label.astype(jnp.float32)
         return carry
 
-    lax.fori_loop(0, table.shape[0], body, 0, unroll=4)
+    lax.fori_loop(0, table.shape[1], body, 0, unroll=4)
 
 
 def find_faces(sides, table, here, doms):
     _, _, spare, wide = sides.shape
-    slots = max(2, table.shape[0] // doms)
+    slots = max(2, table.shape[1] // doms)
     shape = (doms, 3 * slots + 1, spare, wide)
     return pl.pallas_call(
         faces_kernel,
@@ -601,13 +623,14 @@
     spare = -(-planes // 16) * 8
     spot = lax.axis_index("height").astype(jnp.int32).reshape(1)
     here = lax.axis_index("dom").astype(jnp.int32).reshape(1)
+    boxes, listed = partition_boxes.T, face_table.T
     swap = lambda size, mask: [(h, h ^ mask) for h in range(size)]
     front = cells // 4
     raw, whole_modes = lax.optimization_barrier((modes_now[:, :, :front], modes_now))
     far = list(range(2, shares, 2))
     arrived = [lax.ppermute(raw, "height", swap(shares, mask)) for mask in far]
     other = lax.ppermute(whole_modes, "height", swap(shares, 1))
-    w, c, ws, cs, *tables = make_tables(partition_boxes, face_table, here, spot, side, spare)
+    w, c, ws, cs = make_tables(boxes, listed, here, spot, side)
     parts = mix(spot, modes_now, other, shares, front)
     kept, sent = parts[0], [[], []]
     for k in range(2):
@@ -617,11 +640,11 @@
     sides = find_sides(modes_now, ws, cs, spare)
     *arrived, sides = lax.optimization_barrier((*arrived, sides))
     passed = [lax.ppermute(x, "height", swap(shares, 1)) for x in arrived]
-    outgoing = find_faces(sides, face_table, here, doms)
+    outgoing = find_faces(sides, listed, here, doms)
     fields = [modes_now, other, *arrived, *passed]
     places = [0, 1, *far, *(mask ^ 1 for mask in far)]
-    received, first, steady, gain = exchange(
-        partition_boxes, outgoing, modes_now, modes_prev, fields, places, front, shares
+    received, first, steady, gain, *tables = exchange(
+        boxes, outgoing, modes_now, modes_prev, fields, places, front, shares
     )
     new_modes = advance(received, sides, tables, steady, gain)
     pressure = None

time: 61.7 us -> 61.5 us (level)
  waiting for transfers between devices: 9.6 us -> 11 us
  Pallas kernels: 43.4 us -> 42 us
    ppermute x1, waiting for transfers between devices: 1.58 us -> 3.13 us  [on_device(): arrived = [lax.ppermute(raw, 'height', swap(shares, mask)) for mask in far]]
    pallas_call x1, Pallas kernels: 3.71 us -> 2.3 us  [make_tables(): pl.pallas_call(tables_kernel, grid_spec=pltpu.PrefetchScalarGridSpec(num_...]
    unnamed x6 -> x12, local copies, waits for them, and re-layouts: 1.53 us -> 1.39 us
  transfers between devices with their start and end apart: 5 -> 5, of which waited for: 3 -> 3; matrix products, arithmetic and copies ran while one was open for 2% -> 0% of each run, Pallas kernels for 67% -> 65%
where the time goes in v5:
time: 61.5 us; the launch traced here: 61.2 us
  Pallas kernels  42 us (68%)
  waiting for transfers between devices  11 us (18%)
  starting transfers between devices  5.04 us (8%)
  local copies, waits for them, and re-layouts  2.47 us (4%)
  between operations  0.72 us (1%)
    pallas_call x1, Pallas kernels, exchange(): pl.pallas_call(functools.partial(exchange_kernel, shares * planes, places...  13 us
    pallas_call x2, Pallas kernels, to_cells(): pl.pallas_call(kernel, grid=(size // GROUP,), in_specs=specs, out_specs=p...  8.17 us
    ppermute x2, waiting for transfers between devices, on_device(): sent[k].append(lax.ppermute(part[k], 'height', swap(shares, goal)))  7.85 us
    pallas_call x1, Pallas kernels, advance(): pl.pallas_call(functools.partial(force_kernel, pairs), grid_spec=pltpu.Pr...  7.79 us
    pallas_call x1, Pallas kernels, find_sides(): pl.pallas_call(sides_kernel, grid=(planes // GROUP,), in_specs=[pl.BlockS...  5.69 us
    pallas_call x1, Pallas kernels, mix(): pl.pallas_call(functools.partial(mix_kernel, shares * planes), grid_spec=...  3.57 us
    ppermute x1, waiting for transfers between devices, on_device(): arrived = [lax.ppermute(raw, 'height', swap(shares, mask)) for mask in far]  3.13 us
    ppermute x1, starting transfers between devices, on_device(): arrived = [lax.ppermute(raw, 'height', swap(shares, mask)) for mask in far]  2.55 us
  transfers between devices with their start and end apart: 5, of which 3 were waited for; matrix products, arithmetic and copies ran while one was open for 0% of the time, Pallas kernels for 65%

profile of v5, /device:TPU:0, one launch (start us, length us, event | category | flops | bytes accessed | tf_op | source)
XLA Modules:
  0.0 61.2 jit_solution(3983320976848529972)
XLA Ops:
  0.6 1.1 %slice.6 = f32[16,8,1024]{2,1,0:T(8,128)S(1)} slice(f32[16,8,4096]{2,1,0:T(8,128)} %refs_0_.1), slice={[0:16], [0:8], [0:1024]} | slice | bytes 1048576 | tf_op jit(solution)/shard_map/slice | solution.py:629
  1.7 0.0 copy-start
  1.7 0.6 collective-permute-start
  2.3 2.6 %collective-permute-start.1 = (f32[16,8,1024]{2,1,0:T(8,128)S(1)}, f32[16,8,1024]{2,1,0:T(8,128)S(1)}, u32[]{:S(2)}, u32[]{:S(2)}) collective-permute-start(f32[16,8,1024]{2,1,0:T(8,128)S(1)} %slice.6), channel_id=1, source_target_pairs={{0,16},{8,24},{16,0},{24,8},{1,17},{9,25},{17,1},{25,9},{2,18},{10... | collective-permute-start | bytes 1572872 | tf_op jit(solution)/shard_map/ppermute | solution.py:631
  4.8 0.7 %copy-done.1 = s32[32,8]{0,1:T(8,128)S(1)} copy-done((s32[32,8]{0,1:T(8,128)S(1)}, s32[32,8]{0,1:T(8,128)}, u32[]{:S(2)}) %copy-start.1) | copy-done | bytes 1048
  5.5 0.7 %copy-done.4 = s32[8,2]{0,1:T(2,128)S(1)} copy-done((s32[8,2]{0,1:T(2,128)S(1)}, s32[8,2]{0,1:T(2,128)}, u32[]{:S(2)}) %copy-start.4) | copy-done | bytes 88
  6.2 2.3 %tables.1 = (bf16[8,64,192]{2,1,0:T(8,128)(2,1)S(1)}, bf16[8,384,128]{2,1,0:T(8,128)(2,1)S(1)}, bf16[8,80,192]{2,1,0:T(8,128)(2,1)S(1)}, bf16[8,384,256]{2,1,0:T(8,128)(2,1)S(1)}) custom-call(s32[2,8]{1,0:T(2,128)S(1)} %bitcast.8, s32[8,32]{1,0:T(8,128)S(1)} %bitcast.6, s32[1]{0:T(128)} %bitcast.3.here.place_ref, s32[1]{0:T(128)} %bitcast.spot), custom_call_target="tpu_custom_call" | custom-call | flops 1000000000 | bytes 5000000 | tf_op jit(solution)/shard_map/tables/pallas_call | solution.py:130
  8.5 0.0 copy-start.2
  8.5 5.7 %sides.1.s_ref = f32[8,12,8,128]{3,2,1,0:T(8,128)S(1)} custom-call(f32[16,8,4096]{2,1,0:T(8,128)S(1)} %copy-done, bf16[8,80,192]{2,1,0:T(8,128)(2,1)S(1)} %get-tuple-element.27.w_ref, bf16[8,384,256]{2,1,0:T(8,128)(2,1)S(1)} %get-tuple-element.28.c_ref), custom_call_target="tpu_custom_call" | custom-call | flops 6000000000 | bytes 2097152 | tf_op jit(solution)/shard_map/sides/pallas_call | solution.py:390
  14.2 3.1 %collective-permute-done.1.refs_2_ = f32[16,8,1024]{2,1,0:T(8,128)S(1)} collective-permute-done((f32[16,8,1024]{2,1,0:T(8,128)S(1)}, f32[16,8,1024]{2,1,0:T(8,128)S(1)}, u32[]{:S(2)}, u32[]{:S(2)}) %collective-permute-start.1) | collective-permute-done | bytes 524320 | tf_op jit(solution)/shard_map/ppermute | solution.py:631
  17.4 0.0 collective-permute-start.2
  17.4 1.5 %faces.1.out_ref = f32[8,13,8,128]{3,2,1,0:T(8,128)S(1)} custom-call(s32[8,32]{1,0:T(8,128)S(1)} %bitcast.7, s32[1]{0:T(128)} %bitcast.3.here.place_ref, f32[8,12,8,128]{3,2,1,0:T(8,128)S(1)} %sides.1.s_ref), custom_call_target="tpu_custom_call" | custom-call | flops 100000000 | bytes 1000000 | tf_op jit(solution)/shard_map/faces/pallas_call | solution.py:441
  18.8 0.0 copy-start.3
  18.8 0.0 copy-start.5
  18.9 0.0 collective-permute-done.other_ref.refs_1_
  18.9 3.6 %mix.1 = (f32[12,8,3072]{2,1,0:T(8,128)S(1)}, f32[4,8,3072]{2,1,0:T(8,128)S(1)}, f32[12,8,3072]{2,1,0:T(8,128)S(1)}, f32[4,8,3072]{2,1,0:T(8,128)S(1)}) custom-call(s32[1]{0:T(128)} %bitcast.spot, f32[16,8,4096]{2,1,0:T(8,128)S(1)} %copy-done, f32[16,8,4096]{2,1,0:T(8,128)} %collective-permute-done.other_ref.refs_1_), custom_call_target="tpu_custom_call" | custom-call | flops 3000000000 | bytes 6291456 | tf_op jit(solution)/shard_map/mix/pallas_call | solution.py:196
  22.4 1.9 %collective-permute-start.3 = (f32[12,8,3072]{2,1,0:T(8,128)S(1)}, f32[12,8,3072]{2,1,0:T(8,128)S(1)}, u32[]{:S(2)}, u32[]{:S(2)}) collective-permute-start(f32[12,8,3072]{2,1,0:T(8,128)S(1)} %get-tuple-element.43), channel_id=1, source_target_pairs={{0,24},{8,16},{16,8},{24,0},{1,25},{9,17},{17,9},{25,1},{2,26},{10... | collective-permute-start | bytes 3538952 | tf_op jit(solution)/shard_map/ppermute | solution.py:639
  24.4 13.0 %exchange.1 = (f32[8,13,8,128]{3,2,1,0:T(8,128)S(1)}, f32[16,8,1024]{2,1,0:T(8,128)S(1)}, f32[16,8,4096]{2,1,0:T(8,128)S(1)}, f32[16,8,4096]{2,1,0:T(8,128)S(1)}...) custom-call(s32[2,8]{1,0:T(2,128)S(1)} %bitcast.9, ...), custom_call_target="tpu_custom_call" | custom-call | flops 10000000000 | bytes 2621440 | tf_op jit(solution)/shard_map/exchange/pallas_call | solution.py:319
  37.4 7.8 %force.1 = f32[16,8,4096]{2,1,0:T(8,128)} custom-call(s32[32,4]{1,0:T(8,128)S(1)} %bitcast.5, f32[8,13,8,128]{3,2,1,0:T(8,128)S(1)} %get-tuple-element.31.r_ref, f32[8,12,8,128]{3,2,1,0:T(8,128)S(1)} %sides.1.s_ref, bf16[8,384,128]{2,1,0:T(8,128)(2,1)S(1)} %get-tuple-element.32.ct_ref, bf16[8,384,128]{2,1,0:T(8,128)(2,1)S(1)} %get-tuple-element.33.rt_ref, ...), custom_call_target="tpu_custom_call" | custom-call | flops 8000000000 | bytes 6291456 | tf_op jit(solution)/shard_map/force/pallas_call | solution.py:538
  45.2 0.0 collective-permute-start.4
  45.2 5.6 %collective-permute-done.3.refs_2_ = f32[12,8,3072]{2,1,0:T(8,128)S(1)} collective-permute-done((f32[12,8,3072]{2,1,0:T(8,128)S(1)}, f32[12,8,3072]{2,1,0:T(8,128)S(1)}, u32[]{:S(2)}, u32[]{:S(2)}) %collective-permute-start.3) | collective-permute-done | bytes 1179680 | tf_op jit(solution)/shard_map/ppermute | solution.py:639
  50.7 5.7 %cells.2.buffer_ref = f32[16,8,4096]{2,1,0:T(8,128)} custom-call(bf16[8,64,192]{2,1,0:T(8,128)(2,1)S(1)} %get-tuple-element.39.w_ref.refs_0_, bf16[8,384,128]{2,1,0:T(8,128)(2,1)S(1)} %get-tuple-element.40.c_ref.refs_1_, f32[16,8,1024]{2,1,0:T(8,128)S(1)} %get-tuple-element.41.refs_0_.refs_2_, f32[12,8,3072]{2,1,0:T(8,128)S(1)} %get-tuple-element.42.refs_1_, ...), custom_call_target="tpu_custom_call" | custom-call | flops 6000000000 | bytes 4718592 | tf_op jit(solution)/shard_map/cells/pallas_call | solution.py:603
  56.5 2.3 %collective-permute-done.4.refs_4_ = f32[4,8,3072]{2,1,0:T(8,128)S(1)} collective-permute-done((f32[4,8,3072]{2,1,0:T(8,128)S(1)}, f32[4,8,3072]{2,1,0:T(8,128)S(1)}, u32[]{:S(2)}, u32[]{:S(2)}) %collective-permute-start.4) | collective-permute-done | bytes 393248 | tf_op jit(solution)/shard_map/ppermute | solution.py:639
  58.8 2.4 %cells.3 = f32[16,8,4096]{2,1,0:T(8,128)} custom-call(f32[16,8,4096]{2,1,0:T(8,128)} %cells.2.buffer_ref, bf16[8,64,192]{2,1,0:T(8,128)(2,1)S(1)} %get-tuple-element.39.w_ref.refs_0_, bf16[8,384,128]{2,1,0:T(8,128)(2,1)S(1)} %get-tuple-element.40.c_ref.refs_1_, f32[16,8,1024]{2,1,0:T(8,128)S(1)} %get-tuple-element.41.refs_0_.refs_2_, ...), custom_call_target="tpu_custom_call", output_to_operand_aliasing={{}: (0, {})} | custom-call | flops 2000000000 | bytes 1572864 | tf_op jit(solution)/shard_map/cells/pallas_call | solution.py:603
  (8 shorter events, 0.0 us)
Async XLA Ops:
  1.7 6.8 %copy-start = (f32[16,8,4096]{2,1,0:T(8,128)S(1)}, f32[16,8,4096]{2,1,0:T(8,128)}, u32[]{:S(2)}) copy-start(f32[16,8,4096]{2,1,0:T(8,128)} %refs_0_.1) | copy-start | bytes 6291460
  1.7 17.1 %collective-permute-start = (f32[16,8,4096]{2,1,0:T(8,128)}, f32[16,8,4096]{2,1,0:T(8,128)}, u32[]{:S(2)}, u32[]{:S(2)}) collective-permute-start(f32[16,8,4096]{2,1,0:T(8,128)} %refs_0_.1), channel_id=1, source_target_pairs={{0,8},{8,0},{16,24},{24,16},{1,9},{9,1},{17,25},{25,17},{2,10},{10... | collective-permute-start | bytes 6291464 | tf_op jit(solution)/shard_map/ppermute | solution.py:632
  2.3 15.1 %collective-permute-start.1 = (f32[16,8,1024]{2,1,0:T(8,128)S(1)}, f32[16,8,1024]{2,1,0:T(8,128)S(1)}, u32[]{:S(2)}, u32[]{:S(2)}) collective-permute-start(f32[16,8,1024]{2,1,0:T(8,128)S(1)} %slice.6), channel_id=1, source_target_pairs={{0,16},{8,24},{16,0},{24,8},{1,17},{9,25},{17,1},{25,9},{2,18},{10... | collective-permute-start | bytes 1572872 | tf_op jit(solution)/shard_map/ppermute | solution.py:631
  4.8 0.7 %copy-start.1 = (s32[32,8]{0,1:T(8,128)S(1)}, s32[32,8]{0,1:T(8,128)}, u32[]{:S(2)}) copy-start(s32[32,8]{0,1:T(8,128)} %param.7) | copy-start | bytes 3076
  5.5 0.7 %copy-start.4 = (s32[8,2]{0,1:T(2,128)S(1)}, s32[8,2]{0,1:T(2,128)}, u32[]{:S(2)}) copy-start(s32[8,2]{0,1:T(2,128)} %param.6) | copy-start | bytes 196
  8.5 8.8 %copy-start.2 = (s32[32,8]{0,1:T(8,128)S(1)}, s32[32,8]{0,1:T(8,128)}, u32[]{:S(2)}) copy-start(s32[32,8]{0,1:T(8,128)} %param.7) | copy-start | bytes 3076
  17.4 7.0 %collective-permute-start.2 = (f32[16,8,1024]{2,1,0:T(8,128)S(1)}, f32[16,8,1024]{2,1,0:T(8,128)S(1)}, u32[]{:S(2)}, u32[]{:S(2)}) collective-permute-start(f32[16,8,1024]{2,1,0:T(8,128)S(1)} %collective-permute-done.1.refs_2_), channel_id=1, source_target_pairs={{0,8},{8,0},{16,24},{24,16},{1,9},{9,1},{17,25},{25,17},{2,10},{10... | collective-permute-start | bytes 1572872 | tf_op jit(solution)/shard_map/ppermute | solution.py:642
  18.8 5.5 %copy-start.3 = (f32[16,8,4096]{2,1,0:T(8,128)S(1)}, f32[16,8,4096]{2,1,0:T(8,128)}, u32[]{:S(2)}) copy-start(f32[16,8,4096]{2,1,0:T(8,128)} %prev_ref.1) | copy-start | bytes 6291460
  18.8 5.5 %copy-start.5 = (s32[8,2]{0,1:T(2,128)S(1)}, s32[8,2]{0,1:T(2,128)}, u32[]{:S(2)}) copy-start(s32[8,2]{0,1:T(2,128)} %param.6) | copy-start | bytes 196
  22.4 28.3 %collective-permute-start.3 = (f32[12,8,3072]{2,1,0:T(8,128)S(1)}, f32[12,8,3072]{2,1,0:T(8,128)S(1)}, u32[]{:S(2)}, u32[]{:S(2)}) collective-permute-start(f32[12,8,3072]{2,1,0:T(8,128)S(1)} %get-tuple-element.43), channel_id=1, source_target_pairs={{0,24},{8,16},{16,8},{24,0},{1,25},{9,17},{17,9},{25,1},{2,26},{10... | collective-permute-start | bytes 3538952 | tf_op jit(solution)/shard_map/ppermute | solution.py:639
  45.2 13.6 %collective-permute-start.4 = (f32[4,8,3072]{2,1,0:T(8,128)S(1)}, f32[4,8,3072]{2,1,0:T(8,128)S(1)}, u32[]{:S(2)}, u32[]{:S(2)}) collective-permute-start(f32[4,8,3072]{2,1,0:T(8,128)S(1)} %get-tuple-element.45), channel_id=1, source_target_pairs={{0,24},{8,16},{16,8},{24,0},{1,25},{9,17},{17,9},{25,1},{2,26},{10... | collective-permute-start | bytes 1179656 | tf_op jit(solution)/shard_map/ppermute | solution.py:639
